TPU v7x, 32 devices: a whole 2x2x4 slice. The times are simulated.
32 devices in a mesh: gx: 8 (over z, y), gy: 4 (over x, core).
Axes of the slice: x: 2, y: 2, z: 4, core: 2. Of those that a mesh axis runs over, the one named last changes fastest.
Arguments:
- velocity: float32 [3, 96, 256, 256], P(None, 'gx', 'gy'), may hold values from -6 to 6
- target: float32 [3, 16384], P(None, ('gx', 'gy')), may hold values from -6 to 6
- weights: float32 [3, 6, 16384], P(None, None, ('gx', 'gy')), may hold values from 0.02 to 0.34
- corners: int32 [3, 16384], P(None, ('gx', 'gy')), may hold values from 0 to 250, as said below
- dest: int32 [16384, 1], P(('gx', 'gy')), may hold values from 0 to 7; in each aligned block of 512 rows (0 to 511, 512 to 1023, ...) at most 128 rows name the same one
Outputs:
- velocity_next: float32 [3, 96, 256, 256], P(None, 'gx', 'gy')
- marker_force: float32 [3, 16384], P(None, ('gx', 'gy'))
Inputs may be any that keep to these rules, and one draw needn't show every extreme that they name: Each corner keeps its 6-cell box inside one device's block: corners[0] is at most 6, corners[1] at most 58, corners[2] at most 250. `dest`: among the markers of one device, at most 128 name the same streamwise index.
All inputs are finite; a program needn't handle non-finite values.
Results may differ from a plain program's by a relative error of at most 0.000071.
Values sent between devices are 32-bit elements; how exact they have to be, the bound alone decides.
No kernel may reach another device: no remote copies, remote signals or barrier semaphores. Data moves between devices by JAX's collectives and lax.ppermute only.
A program may use at most 128 MiB of HBM per device.

v0:
```python
import jax
import jax.numpy as jnp
from jax import lax
from jax.sharding import PartitionSpec as P

MARK_DEV = 512
SLOT_MIN = 12


diffusion = 0.4


def extended(cells, sides, width):
    for axis, dim in sides:
        count = lax.axis_size(axis)
        head = lax.slice_in_dim(cells, 0, width, axis=dim)
        tail = lax.slice_in_dim(cells, cells.shape[dim] - width, cells.shape[dim], axis=dim)
        cells = jnp.concatenate(
            [
                lax.ppermute(tail, axis, [(i, (i + 1) % count) for i in range(count)]),
                cells,
                lax.ppermute(head, axis, [((i + 1) % count, i) for i in range(count)]),
            ],
            axis=dim,
        )
    return cells


def window(delta, corner, length):
    cells = jnp.arange(length, dtype=jnp.int32)[:, None] - corner[None, :]
    offsets = jnp.arange(6, dtype=jnp.int32)[:, None, None]
    return jnp.sum(delta[:, None, :] * (cells[None, :, :] == offsets).astype(jnp.float32), axis=0)


def walls(padded):
    lower = jnp.where(lax.axis_index("gy") == 0, 0.0, 1.0).astype(jnp.float32)
    upper = jnp.where(lax.axis_index("gy") == lax.axis_size("gy") - 1, 0.0, 1.0).astype(jnp.float32)
    padded = padded.at[:, :, 0, :].multiply(lower)
    return padded.at[:, :, -1, :].multiply(upper)


def per_device(velocity, target, weights, corners, dest):
    n_stream = lax.axis_size("gx")
    owned = target.shape[1]
    capacity = max(SLOT_MIN, 2 * MARK_DEV // n_stream)
    total_slots = n_stream * capacity
    _, cells_x, cells_y, cells_z = velocity.shape
    picks = (dest == jnp.arange(n_stream, dtype=jnp.int32)[None, :]).astype(jnp.int32)
    ranking = jnp.sum(jnp.cumsum(picks, axis=0) * picks, axis=1) - 1
    position = dest[:, 0] * capacity + ranking
    payload = jnp.concatenate([target, weights.reshape(18, owned)], axis=0)
    outgoing = jnp.zeros((21, total_slots), jnp.float32).at[:, position].set(payload)
    outgoing_corner = jnp.zeros((3, total_slots), jnp.int32).at[:, position].set(corners)
    arrived, arrived_corner = (
        lax.all_to_all(outgoing, "gx", split_axis=1, concat_axis=1, tiled=True),
        lax.all_to_all(outgoing_corner, "gx", split_axis=1, concat_axis=1, tiled=True),
    )
    weight_x = window(arrived[3:9], arrived_corner[0], cells_x)
    weight_y = window(arrived[9:15], arrived_corner[1], cells_y)
    weight_z = window(arrived[15:21], arrived_corner[2], cells_z)
    flat = velocity.reshape(3 * cells_x * cells_y, cells_z)
    partial_z = jnp.dot(flat, weight_z, precision=lax.Precision.HIGHEST).reshape(
        3, cells_x, cells_y, total_slots
    )
    sampled = jnp.einsum(
        "cxys,xs,ys->cs", partial_z, weight_x, weight_y, precision=lax.Precision.HIGHEST
    )
    slot_force = arrived[0:3] - sampled
    boxes = slot_force[:, None, None, :] * weight_x[None, :, None, :] * weight_y[None, None, :, :]
    spread = jnp.dot(
        boxes.reshape(3 * cells_x * cells_y, total_slots),
        weight_z.T,
        precision=lax.Precision.HIGHEST,
    )
    spread = spread.reshape(velocity.shape)
    returned = lax.all_to_all(slot_force, "gx", split_axis=1, concat_axis=1, tiled=True)
    marker_force = returned[:, position]
    rhs = velocity + spread
    padded = extended(rhs, (("gx", 1), ("gy", 2)), 1)
    padded = walls(padded)
    neighbours = (
        padded[:, 2:, 1:-1] + padded[:, :-2, 1:-1] + padded[:, 1:-1, 2:] + padded[:, 1:-1, :-2]
    )
    neighbours = neighbours + jnp.roll(rhs, 1, 3) + jnp.roll(rhs, -1, 3)
    velocity_next = (rhs + diffusion * neighbours) / (1.0 + 6.0 * diffusion)
    return (velocity_next, marker_force)


def solution(mesh):
    in_specs = (
        P(None, "gx", "gy", None),
        P(None, ("gx", "gy")),
        P(None, None, ("gx", "gy")),
        P(None, ("gx", "gy")),
        P(("gx", "gy"), None),
    )
    out_specs = (P(None, "gx", "gy", None), P(None, ("gx", "gy")))
    return jax.shard_map(
        per_device, mesh=mesh, in_specs=in_specs, out_specs=out_specs, check_vma=False
    )
```

profile of v0, /device:TPU:0, one launch (start us, length us, event | category | flops | bytes accessed | tf_op | source)
XLA Modules:
  0.0 118.4 jit_solution(16771207240958988617)
XLA Ops:
  0.6 0.7 fusion.19
  1.3 1.1 reduce-window.6
  2.4 0.2 slice_reduce_fusion
  2.7 0.8 fusion.18
  3.5 0.7 compare_select_fusion
  4.2 0.8 copy.37
  5.0 1.8 %scatter_custom_fusion.1 = s32[3,1024]{0,1:T(8,128)S(1)} fusion(s32[512]{0:T(512)S(1)} %bitcast.71, s32[512,3]{1,0:T(8,128)S(1)} %copy.37, s32[]{:T(128)} %constant.79.clone.1), kind=kCustom, calls=%fused_computation.28 | custom fusion | bytes 12292 | tf_op jit(solution)/shard_map/scatter | solution.py:53
  6.9 0.8 copy.38
  7.6 7.3 %all-to-all-start.1 = ((s32[3,8,128]{2,0,1:T(4,128)}), s32[3,8,128]{2,0,1:T(4,128)S(1)}, u32[]{:S(2)}, u32[]{:S(2)}) async-start(s32[3,8,128]{2,0,1:T(4,128)} %copy.38), calls=%async_computation.1 | async-start | bytes 32768 | tf_op jit(solution)/shard_map/all_to_all | solution.py:56
  15.0 0.8 reshape.206
  15.8 0.7 maximum_bitcast_fusion
  16.5 0.6 pad_clamp_fusion
  17.1 0.1 copy.35
  17.2 1.8 %scatter_custom_fusion = f32[21,1024]{0,1:T(8,128)S(1)} fusion(s32[512]{0:T(512)S(1)} %bitcast.73, f32[512,21]{1,0:T(8,128)S(1)} %copy.35, f32[]{:T(128)} %constant.77.clone.1), kind=kCustom, calls=%fused_computation.30 | custom fusion | bytes 86020 | tf_op jit(solution)/shard_map/scatter | solution.py:52
  19.1 0.8 copy.36
  19.9 1.6 %all-to-all-done.1 = s32[3,8,128]{2,0,1:T(4,128)S(1)} async-done(((s32[3,8,128]{2,0,1:T(4,128)}), s32[3,8,128]{2,0,1:T(4,128)S(1)}, u32[]{:S(2)}, u32[]{:S(2)}) %all-to-all-start.1) | async-done | bytes 12320 | tf_op jit(solution)/shard_map/all_to_all | solution.py:56
  21.5 4.4 %all-to-all-start = ((f32[21,8,128]{2,0,1:T(8,128)}), f32[21,8,128]{2,0,1:T(8,128)S(1)}, u32[]{:S(2)}, u32[]{:S(2)}) async-start(f32[21,8,128]{2,0,1:T(8,128)} %copy.36), calls=%async_computation | async-start | bytes 196608 | tf_op jit(solution)/shard_map/all_to_all | solution.py:55
  25.9 0.1 iota_subtract_fusion
  26.1 6.9 %all-to-all-done = f32[21,8,128]{2,0,1:T(8,128)S(1)} async-done(((f32[21,8,128]{2,0,1:T(8,128)}), f32[21,8,128]{2,0,1:T(8,128)S(1)}, u32[]{:S(2)}, u32[]{:S(2)}) %all-to-all-start) | async-done | bytes 86048 | tf_op jit(solution)/shard_map/all_to_all | solution.py:55
  33.0 0.6 select_reduce_fusion
  33.7 19.0 %convolution_bitcast_fusion = f32[2304,1024]{0,1:T(8,128)} fusion(f32[256,1024]{1,0:T(8,128)S(1)} %select_reduce_fusion, f32[2304,256]{1,0:T(8,128)} %bitcast.58), kind=kOutput, calls=%fused_computation.6 | convolution fusion | flops 7247757312 | bytes 12845056 | tf_op jit(solution)/shard_map/dot_general | solution.py:62
  52.7 9.6 %copy.58 = f32[2304,1024]{1,0:T(8,128)} copy(f32[2304,1024]{0,1:T(8,128)} %convolution_bitcast_fusion) | data formatting | bytes 18874368
  62.3 0.2 select_reduce_fusion.1
  62.5 0.0 copy-start
  62.5 5.3 %multiply_reduce_fusion = f32[1024,3,12]{0,2,1:T(8,128)S(1)} fusion(f32[1024,64,3,12]{0,1,3,2:T(8,128)} %bitcast.57, f32[1024,64]{0,1:T(8,128)S(1)} %bitcast.61), kind=kLoop, calls=%fused_computation.3 | loop fusion | flops 4681728 | bytes 9846784 | tf_op jit(solution)/shard_map/cxys,xs,ys->cs/dot_general | solution.py:65
  67.8 0.6 fusion.17
  68.5 0.7 broadcast_multiply_fusion
  69.2 8.1 %fusion.9 = f32[3,12,64,256]{3,2,1,0:T(8,128)S(1)} fusion(f32[3,12,64,256]{3,2,1,0:T(8,128)S(1)} %copy-done, f32[64,1024]{1,0:T(8,128)S(1)} %select_reduce_fusion.1, f32[3,12,1024]{2,1,0:T(8,128)S(1)} %broadcast_multiply_fusion, f32[256,1024]{1,0:T(8,128)S(1)} %select_reduce_fusion), kind=kOutput, calls=%fused_computation.22 | convolution fusion | flops 7250706432 | bytes 6176768 | tf_op jit(solution)/shard_map/dot_general | solution.py:70
  77.3 0.4 collective-permute-start
  77.7 4.4 %collective-permute-start.1 = (f32[3,1,64,256]{3,2,1,0:T(8,128)S(1)}, f32[3,1,64,256]{3,2,1,0:T(8,128)S(1)}, u32[]{:S(2)}, u32[]{:S(2)}) collective-permute-start(f32[3,1,64,256]{3,2,1,0:T(8,128)S(1)} %get-tuple-element.41), channel_id=1, source_target_pairs={{4,0},{8,4},{12,8},{16,12},{20,16},{24,20},{28,24},{0,28},{5,1},{9... | collective-permute-start | bytes 589832 | tf_op jit(solution)/shard_map/ppermute | solution.py:22
  82.1 3.0 %fusion.20 = (f32[3,12,64,255]{3,2,1,0:T(8,128)}, f32[3,12,64,255]{3,2,1,0:T(8,128)}) fusion(f32[3,12,64,256]{3,2,1,0:T(8,128)S(1)} %fusion.9), kind=kLoop, calls=%fused_computation.55 | loop fusion | bytes 9400320 | tf_op jit(solution)/shard_map/jit(_roll_static)/slice | solution.py:84
  85.1 3.3 %all-to-all-start.2 = ((f32[3,8,128]{2,0,1:T(4,128)}), f32[3,8,128]{2,0,1:T(4,128)S(1)}, u32[]{:S(2)}, u32[]{:S(2)}) async-start(f32[3,8,128]{2,0,1:T(4,128)} %bitcast.29), calls=%async_computation.2 | async-start | bytes 32768 | tf_op jit(solution)/shard_map/all_to_all | solution.py:76
  88.5 0.0 collective-permute-done.1
  88.5 0.8 pad_maximum_fusion.3
  89.3 1.7 %collective-permute-start.3 = (f32[3,14,1,256]{3,2,1,0:T(1,128)}, f32[3,14,1,256]{3,2,1,0:T(1,128)}, u32[]{:S(2)}, u32[]{:S(2)}) collective-permute-start(f32[3,14,1,256]{3,2,1,0:T(1,128)} %get-tuple-element.35), channel_id=1, source_target_pairs={{1,0},{2,1},{3,2},{0,3},{5,4},{6,5},{7,6},{4,7},{9,8},{10,9},{11,1... | collective-permute-start | bytes 129032 | tf_op jit(solution)/shard_map/ppermute | solution.py:22
  91.1 1.6 %fusion.21 = (f32[3,12,64,1]{3,2,1,0:T(8,128)S(1)}, f32[3,12,64,1]{3,2,1,0:T(8,128)}) fusion(f32[3,12,64,256]{3,2,1,0:T(8,128)S(1)} %fusion.9), kind=kLoop, calls=%fused_computation.56 | loop fusion | bytes 36864 | tf_op jit(solution)/shard_map/jit(_roll_static)/slice | solution.py:84
  92.6 2.4 %all-to-all-done.2 = f32[3,8,128]{2,0,1:T(4,128)S(1)} async-done(((f32[3,8,128]{2,0,1:T(4,128)}), f32[3,8,128]{2,0,1:T(4,128)S(1)}, u32[]{:S(2)}, u32[]{:S(2)}) %all-to-all-start.2) | async-done | bytes 12320 | tf_op jit(solution)/shard_map/all_to_all | solution.py:76
  95.0 1.0 copy.43
  96.0 2.8 %gather_fusion = f32[512,3]{1,0:T(8,128)} fusion(f32[3,1024]{0,1:T(8,128)} %bitcast.62, s32[1024]{0:T(1024)} %pad_clamp_fusion), kind=kCustom, calls=%fused_computation | custom fusion | bytes 14336 | tf_op jit(solution)/shard_map/gather | solution.py:77
  98.8 1.7 %copy.44 = f32[3,512]{1,0:T(4,128)} copy(f32[3,512]{0,1:T(8,128)} %bitcast.64) | data formatting | bytes 12288
  100.5 0.0 collective-permute-done.2
  100.5 0.0 collective-permute-done.3
  100.5 3.1 %pad_maximum_fusion = f32[3,14,66,256]{3,2,1,0:T(8,128)} fusion(f32[3,14,1,256]{3,2,1,0:T(1,128)} %collective-permute-done.3, f32[3,1,64,256]{3,2,1,0:T(8,128)} %copy-done.2, f32[3,12,64,256]{3,2,1,0:T(8,128)S(1)} %fusion.9, f32[3,1,64,256]{3,2,1,0:T(8,128)} %copy-done.1, f32[3,14,1,256]{3,2,1,0:T(1,128)} %collective-permute-done.2), kind=kLoop, calls=%fused_computation.11 | loop fusion | flops 2838528 | bytes 5677056 | tf_op jit(solution)/shard_map/concatenate | solution.py:18
  103.5 1.4 %broadcast_multiply_fusion.1 = f32[3,14,1,256]{3,2,1,0:T(1,128)} fusion(f32[3,14,1,256]{3,2,1,0:T(1,128)} %collective-permute-done.2, f32[]{:T(128)S(6)} %select_n.14), kind=kLoop, calls=%fused_computation.43 | loop fusion | flops 10752 | bytes 86020 | tf_op jit(solution)/shard_map/mul | solution.py:38
  105.0 1.9 %scatter-mul.6 = f32[3,14,66,256]{3,2,1,0:T(8,128)} dynamic-update-slice(f32[3,14,66,256]{3,2,1,0:T(8,128)} %pad_maximum_fusion, f32[3,14,1,256]{3,2,1,0:T(1,128)} %broadcast_multiply_fusion.1, s32[]{:T(128)} %constant.79.clone.1, s32[]{:T(128)} %constant.79.clone.1, s32[]{:T(128)} %constant.79.clone.1, s32[]{:T(128)} %constant.79.clone.1) | dynamic-update-slice | bytes 86020 | tf_op jit(solution)/shard_map/scatter-mul | solution.py:38
  106.9 1.6 %slice_multiply_fusion = f32[3,14,1,256]{3,2,1,0:T(1,128)} fusion(f32[3,14,66,256]{3,2,1,0:T(8,128)} %scatter-mul.6, f32[]{:T(128)S(6)} %select_n.15), kind=kLoop, calls=%fused_computation.36 | loop fusion | flops 10752 | bytes 86020 | tf_op jit(solution)/shard_map/mul | solution.py:39
  108.5 1.9 %scatter-mul.9 = f32[3,14,66,256]{3,2,1,0:T(8,128)} dynamic-update-slice(f32[3,14,66,256]{3,2,1,0:T(8,128)} %scatter-mul.6, f32[3,14,1,256]{3,2,1,0:T(1,128)} %slice_multiply_fusion, s32[]{:T(128)} %constant.79.clone.1, s32[]{:T(128)} %constant.79.clone.1, s32[]{:T(128)} %constant.85.clone.1, s32[]{:T(128)} %constant.79.clone.1) | dynamic-update-slice | bytes 86020 | tf_op jit(solution)/shard_map/scatter-mul | solution.py:39
  110.3 8.1 %fusion.8 = f32[3,12,64,256]{3,2,1,0:T(8,128)} fusion(f32[3,12,64,256]{3,2,1,0:T(8,128)S(1)} %fusion.9, f32[3,14,66,256]{3,2,1,0:T(8,128)} %scatter-mul.9, f32[3,12,64,255]{3,2,1,0:T(8,128)} %get-tuple-element.37, f32[3,12,64,1]{3,2,1,0:T(8,128)} %get-tuple-element.39, f32[3,12,64,1]{3,2,1,0:T(8,128)S(1)} %get-tuple-element.38, ...), kind=kLoop, calls=%fused_computation.17 | loop fusion | flops 5898240 | bytes 18874368 | tf_op jit(solution)/shard_map/div | solution.py:85
  (17 shorter events, 0.2 us)
Async XLA Ops:
  7.6 13.9 %all-to-all-start.1 = ((s32[3,8,128]{2,0,1:T(4,128)}), s32[3,8,128]{2,0,1:T(4,128)S(1)}, u32[]{:S(2)}, u32[]{:S(2)}) async-start(s32[3,8,128]{2,0,1:T(4,128)} %copy.38), calls=%async_computation.1 | async-start | bytes 32768 | tf_op jit(solution)/shard_map/all_to_all | solution.py:56
  21.5 11.5 %all-to-all-start = ((f32[21,8,128]{2,0,1:T(8,128)}), f32[21,8,128]{2,0,1:T(8,128)S(1)}, u32[]{:S(2)}, u32[]{:S(2)}) async-start(f32[21,8,128]{2,0,1:T(8,128)} %copy.36), calls=%async_computation | async-start | bytes 196608 | tf_op jit(solution)/shard_map/all_to_all | solution.py:55
  62.5 6.7 %copy-start = (f32[3,12,64,256]{3,2,1,0:T(8,128)S(1)}, f32[3,12,64,256]{3,2,1,0:T(8,128)}, u32[]{:S(2)}) copy-start(f32[3,12,64,256]{3,2,1,0:T(8,128)} %param.9) | copy-start | bytes 7077892
  77.3 11.2 %collective-permute-start = (f32[3,1,64,256]{3,2,1,0:T(8,128)S(1)}, f32[3,1,64,256]{3,2,1,0:T(8,128)S(1)}, u32[]{:S(2)}, u32[]{:S(2)}) collective-permute-start(f32[3,1,64,256]{3,2,1,0:T(8,128)S(1)} %get-tuple-element.40), channel_id=1, source_target_pairs={{0,4},{4,8},{8,12},{12,16},{16,20},{20,24},{24,28},{28,0},{1,5},{5... | collective-permute-start | bytes 589832 | tf_op jit(solution)/shard_map/ppermute | solution.py:20
  77.7 10.8 %collective-permute-start.1 = (f32[3,1,64,256]{3,2,1,0:T(8,128)S(1)}, f32[3,1,64,256]{3,2,1,0:T(8,128)S(1)}, u32[]{:S(2)}, u32[]{:S(2)}) collective-permute-start(f32[3,1,64,256]{3,2,1,0:T(8,128)S(1)} %get-tuple-element.41), channel_id=1, source_target_pairs={{4,0},{8,4},{12,8},{16,12},{20,16},{24,20},{28,24},{0,28},{5,1},{9... | collective-permute-start | bytes 589832 | tf_op jit(solution)/shard_map/ppermute | solution.py:22
  85.1 9.9 %all-to-all-start.2 = ((f32[3,8,128]{2,0,1:T(4,128)}), f32[3,8,128]{2,0,1:T(4,128)S(1)}, u32[]{:S(2)}, u32[]{:S(2)}) async-start(f32[3,8,128]{2,0,1:T(4,128)} %bitcast.29), calls=%async_computation.2 | async-start | bytes 32768 | tf_op jit(solution)/shard_map/all_to_all | solution.py:76
  88.5 0.8 copy-start.1
  88.5 0.8 copy-start.2
  89.3 11.2 %collective-permute-start.2 = (f32[3,14,1,256]{3,2,1,0:T(1,128)}, f32[3,14,1,256]{3,2,1,0:T(1,128)}, u32[]{:S(2)}, u32[]{:S(2)}) collective-permute-start(f32[3,14,1,256]{3,2,1,0:T(1,128)} %get-tuple-element.34), channel_id=1, source_target_pairs={{0,1},{1,2},{2,3},{3,0},{4,5},{5,6},{6,7},{7,4},{8,9},{9,10},{10,1... | collective-permute-start | bytes 129032 | tf_op jit(solution)/shard_map/ppermute | solution.py:20
  89.3 11.2 %collective-permute-start.3 = (f32[3,14,1,256]{3,2,1,0:T(1,128)}, f32[3,14,1,256]{3,2,1,0:T(1,128)}, u32[]{:S(2)}, u32[]{:S(2)}) collective-permute-start(f32[3,14,1,256]{3,2,1,0:T(1,128)} %get-tuple-element.35), channel_id=1, source_target_pairs={{1,0},{2,1},{3,2},{0,3},{5,4},{6,5},{7,6},{4,7},{9,8},{10,9},{11,1... | collective-permute-start | bytes 129032 | tf_op jit(solution)/shard_map/ppermute | solution.py:22
where the time goes:
time: 119 us; the launch traced here: 118 us
  local copies, waits for them, and re-layouts  30.8 us (26%)
  other arithmetic  27.3 us (23%)
  matrix products  27.1 us (23%)
  starting transfers between devices  21.5 us (18%)
  waiting for transfers between devices  11 us (9%)
    dot_general x1, matrix products, per_device(): jnp.dot(flat, weight_z, precision=lax.Precision.HIGHEST)  19 us
    unnamed x9, local copies, waits for them, and re-layouts  12.1 us
    div x1, other arithmetic, per_device(): velocity_next = (rhs + diffusion * neighbours) / (1.0 + 6.0 * diffusion)  8.07 us
    dot_general x1, matrix products, per_device(): jnp.dot(boxes.reshape(3 * cells_x * cells_y, total_slots), weight_z.T, pr...  8.05 us
    all_to_all x1, starting transfers between devices, per_device(): lax.all_to_all(outgoing_corner, 'gx', split_axis=1, concat_axis=1, tiled=...  7.31 us
    all_to_all x1, waiting for transfers between devices, per_device(): lax.all_to_all(outgoing, 'gx', split_axis=1, concat_axis=1, tiled=True)  6.94 us
    ppermute x2, starting transfers between devices, extended(): lax.ppermute(head, axis, [((i + 1) % count, i) for i in range(count)])  6.16 us
    dot_general x2, other arithmetic, per_device(): jnp.einsum('cxys,xs,ys->cs', partial_z, weight_x, weight_y, precision=lax...  5.31 us
  transfers between devices with their start and end apart: 7, of which 3 were waited for; matrix products, arithmetic and copies ran while one was open for 13% of the time, Pallas kernels for 0%

commit v1 on v0

v1 whole, which is shorter than its diff:
```python
import functools

import jax
import jax.numpy as jnp
from jax import lax
from jax.experimental import pallas as pl
from jax.experimental.pallas import tpu as pltpu
from jax.sharding import PartitionSpec as P

SLOT_MIN = 12
SPAN = 6
ROWS = 24

diffusion = 0.4

f32 = jnp.float32
bf16 = jnp.bfloat16
i32 = jnp.int32
VMEM = pl.BlockSpec(memory_space=pltpu.VMEM)
NN = (((1,), (0,)), ((), ()))
NT = (((1,), (1,)), ((), ()))


def dot(a, b, dims=NN):
    return lax.dot_general(a, b, dims, preferred_element_type=f32)


def halves(x):
    high = x.astype(bf16)
    return high, (x - high.astype(f32)).astype(bf16)


def dot3(ah, al, bh, bl, dims=NN):
    return dot(ah, bh, dims) + dot(ah, bl, dims) + dot(al, bh, dims)


def thirds(x):
    high = x.astype(bf16).astype(f32)
    rest = x - high
    mid = rest.astype(bf16).astype(f32)
    return jnp.concatenate([high, mid, rest - mid], axis=0).astype(bf16)


def one_hot(position, slots):
    rows = lax.broadcasted_iota(i32, (slots, position.shape[1]), 0)
    return jnp.where(rows == position, 1.0, 0.0).astype(bf16)


def pack_kernel(capacity, chunked, span_y, dest_ref, target_ref, weights_ref, corners_ref, out_ref, pos_ref, rows_ref):
    owned = target_ref.shape[1]
    dest = dest_ref[...]
    lane = lax.broadcasted_iota(i32, (1, owned), 1)
    first = dest * (span_y * owned)
    key = first + corners_ref[1:2, :] * owned + lane
    column = jnp.transpose(jnp.broadcast_to(key, (8, owned)))[:, 0:1]
    ahead = jnp.where((column < key) & (column >= first), 1.0, 0.0)
    position = dest * capacity + jnp.sum(ahead, axis=0, keepdims=True).astype(i32)
    pos_ref[...] = position
    rows_ref[0:3, :] = target_ref[...]
    for dim in range(3):
        rows_ref[3 + 6 * dim : 9 + 6 * dim, :] = weights_ref[dim]
    rows_ref[21:24, :] = corners_ref[...].astype(f32)
    slots = out_ref.size // ROWS
    moved = dot(thirds(rows_ref[...]), one_hot(position, slots), NT)
    moved = moved[0:ROWS] + moved[ROWS : 2 * ROWS] + moved[2 * ROWS :]
    if chunked:
        for chunk in range(slots // capacity):
            out_ref[chunk] = moved[:, chunk * capacity : (chunk + 1) * capacity]
    else:
        out_ref[...] = moved


def split_kernel(velocity_ref, high_ref, low_ref):
    rows, cells_z = high_ref.shape[1:]
    for c in range(3):
        high, low = halves(velocity_ref[c].reshape(rows, cells_z))
        high_ref[c] = high
        low_ref[c] = low


def window(weights, corner, length):
    offset = lax.broadcasted_iota(i32, (length, weights.shape[1]), 0) - corner
    out = jnp.zeros(offset.shape, f32)
    for k in range(SPAN):
        out = jnp.where(offset == k, weights[k : k + 1, :], out)
    return out


def sample_kernel(
    chunked, tile, arrived_ref, high_ref, low_ref, velocity_ref,
    force_ref, wzh_ref, wzl_ref, wy_ref, fx_ref, x0_ref, x1_ref, y0_ref, y1_ref, boxh_ref, boxl_ref,
):
    _, cells_x, cells_y, cells_z = velocity_ref.shape
    slots = wy_ref.shape[1]
    capacity = arrived_ref.shape[2] if chunked else 0
    for t in range(slots // tile):
        at = slice(t * tile, (t + 1) * tile)
        if chunked:
            per = tile // capacity
            data = jnp.concatenate([arrived_ref[t * per + k] for k in range(per)], axis=1)
        else:
            data = arrived_ref[:, at]
        corner = data[21:24, :].astype(i32)
        wx = window(data[3:9], corner[0:1], cells_x)
        wy = window(data[9:15], corner[1:2], cells_y)
        wzh, wzl = halves(window(data[15:21], corner[2:3], cells_z))
        wzh_ref[:, at] = wzh
        wzl_ref[:, at] = wzl
        wy_ref[:, at] = wy
        forces = []
        for c in range(3):
            along = dot3(high_ref[c], low_ref[c], wzh, wzl)
            along = along.reshape(cells_x, cells_y, tile) * wy[None]
            sampled = jnp.sum(jnp.sum(along, axis=1) * wx, axis=0, keepdims=True)
            force = data[c : c + 1] - sampled
            fx_ref[c, :, at] = force * wx
            forces.append(force)
        forces = jnp.concatenate(forces + [jnp.zeros((5, tile), f32)], axis=0)
        if chunked:
            for k in range(per):
                force_ref[t * per + k] = forces[:, k * capacity : (k + 1) * capacity]
        else:
            force_ref[:, at] = forces
    wy = wy_ref[...]
    base = 0
    for x in (0, cells_x - 1):
        for c in range(3):
            high, low = halves(fx_ref[c, x : x + 1, :] * wy)
            boxh_ref[base : base + cells_y] = high
            boxl_ref[base : base + cells_y] = low
            base += cells_y
    pad = -(-cells_x // 16) * 16
    for y in (0, cells_y - 1):
        for c in range(3):
            rows = fx_ref[c] * wy[y : y + 1, :]
            rows = jnp.concatenate([rows, jnp.zeros((pad - cells_x, slots), f32)], axis=0)
            high, low = halves(rows)
            boxh_ref[base : base + pad] = high
            boxl_ref[base : base + pad] = low
            base += pad
    spread = dot3(boxh_ref[...], boxl_ref[...], wzh_ref[...], wzl_ref[...], NT)
    base = 0
    for x, ref in ((0, x0_ref), (cells_x - 1, x1_ref)):
        for c in range(3):
            ref[c] = velocity_ref[c, x] + spread[base : base + cells_y]
            base += cells_y
    for y, ref in ((0, y0_ref), (cells_y - 1, y1_ref)):
        for c in range(3):
            ref[c] = velocity_ref[c, :, y, :] + spread[base : base + cells_x]
            base += pad


def spread_kernel(velocity_ref, wzh_ref, wzl_ref, wy_ref, fx_ref, rhs_ref, boxh_ref, boxl_ref):
    _, cells_x, cells_y, cells_z = velocity_ref.shape
    wy = wy_ref[...]
    for c in range(3):
        for x in range(cells_x):
            high, low = halves(fx_ref[c, x : x + 1, :] * wy)
            boxh_ref[x * cells_y : (x + 1) * cells_y] = high
            boxl_ref[x * cells_y : (x + 1) * cells_y] = low
        spread = dot3(boxh_ref[...], boxl_ref[...], wzh_ref[...], wzl_ref[...], NT)
        rhs_ref[c] = velocity_ref[c] + spread.reshape(cells_x, cells_y, cells_z)


def finish_kernel(
    chunked, rhs_ref, x0_ref, x1_ref, y0_ref, y1_ref, returned_ref, pos_ref, next_hbm, force_ref, next_ref, sem,
):
    _, cells_x, cells_y, cells_z = rhs_ref.shape
    row = lax.broadcasted_iota(i32, (cells_y, cells_z), 0)
    scale = 1.0 / (1.0 + 6.0 * diffusion)
    copies = []
    for c in range(3):
        for x in range(cells_x):
            cell = rhs_ref[c, x]
            back = rhs_ref[c, x - 1] if x else x0_ref[c]
            ahead = rhs_ref[c, x + 1] if x < cells_x - 1 else x1_ref[c]
            below = jnp.where(row == 0, y0_ref[c, x : x + 1, :], pltpu.roll(cell, 1, 0))
            above = jnp.where(row == cells_y - 1, y1_ref[c, x : x + 1, :], pltpu.roll(cell, cells_y - 1, 0))
            side = pltpu.roll(cell, 1, 1) + pltpu.roll(cell, cells_z - 1, 1)
            near = (ahead + back) + (above + below) + side
            next_ref[c, x] = (cell + diffusion * near) * scale
        copy = pltpu.make_async_copy(next_ref.at[c], next_hbm.at[c], sem.at[c])
        copy.start()
        copies.append(copy)
    if chunked:
        held = jnp.concatenate([returned_ref[k] for k in range(returned_ref.shape[0])], axis=1)
    else:
        held = returned_ref[...]
    moved = dot(thirds(held), one_hot(pos_ref[...], held.shape[1]))
    moved = moved[0:8] + moved[8:16] + moved[16:24]
    force_ref[...] = moved[0:3]
    for copy in copies:
        copy.wait()


def per_device(velocity, target, weights, corners, dest):
    n_stream = lax.axis_size("gx")
    n_wall = lax.axis_size("gy")
    owned = target.shape[1]
    capacity = max(SLOT_MIN, 2 * owned // n_stream)
    slots = n_stream * capacity
    _, cells_x, cells_y, cells_z = velocity.shape
    chunked = capacity % 128 == 0
    tile = 256 if slots % 256 == 0 else 128
    shape = jax.ShapeDtypeStruct

    def exchange(packed):
        rows = packed.shape[1] if chunked else packed.shape[0]
        if chunked:
            return lax.all_to_all(packed, "gx", split_axis=0, concat_axis=0, tiled=True)
        packed = packed.reshape(rows, n_stream, capacity)
        packed = lax.all_to_all(packed, "gx", split_axis=1, concat_axis=1, tiled=True)
        return packed.reshape(rows, slots)

    def packed_shape(rows):
        return shape((n_stream, rows, capacity) if chunked else (rows, slots), f32)

    outgoing, position = pl.pallas_call(
        functools.partial(pack_kernel, capacity, chunked, cells_y),
        out_shape=(packed_shape(ROWS), shape((1, owned), i32)),
        in_specs=[VMEM] * 4,
        out_specs=(VMEM, VMEM),
        scratch_shapes=[pltpu.VMEM((ROWS, owned), f32)],
        name="pack",
    )(dest.reshape(1, owned), target, weights, corners)
    arrived = exchange(outgoing)

    block = cells_x * cells_y
    high, low = pl.pallas_call(
        split_kernel,
        out_shape=(shape((3, block, cells_z), bf16),) * 2,
        in_specs=[VMEM],
        out_specs=(VMEM, VMEM),
        name="split",
    )(velocity)

    pad = -(-cells_x // 16) * 16
    edge_rows = 6 * cells_y + 6 * pad
    face_x = shape((3, cells_y, cells_z), f32)
    face_y = shape((3, cells_x, cells_z), f32)
    force, wzh, wzl, wy, fx, x0, x1, y0, y1 = pl.pallas_call(
        functools.partial(sample_kernel, chunked, tile),
        out_shape=(
            packed_shape(8),
            shape((cells_z, slots), bf16),
            shape((cells_z, slots), bf16),
            shape((cells_y, slots), f32),
            shape((3, cells_x, slots), f32),
            face_x, face_x, face_y, face_y,
        ),
        in_specs=[VMEM] * 4,
        out_specs=(VMEM,) * 9,
        scratch_shapes=[pltpu.VMEM((edge_rows, slots), bf16)] * 2,
        name="sample",
    )(arrived, high, low, velocity)

    up_x = [(i, (i + 1) % n_stream) for i in range(n_stream)]
    down_x = [(j, i) for i, j in up_x]
    up_y = [(i, i + 1) for i in range(n_wall - 1)]
    down_y = [(j, i) for i, j in up_y]
    from_x0 = lax.ppermute(x1, "gx", up_x)
    from_x1 = lax.ppermute(x0, "gx", down_x)
    from_y0 = lax.ppermute(y1, "gy", up_y)
    from_y1 = lax.ppermute(y0, "gy", down_y)
    returned = exchange(force)

    rhs = pl.pallas_call(
        spread_kernel,
        out_shape=shape(velocity.shape, f32),
        in_specs=[VMEM] * 5,
        out_specs=VMEM,
        scratch_shapes=[pltpu.VMEM((block, slots), bf16)] * 2,
        cost_estimate=pl.CostEstimate(flops=18 * block * slots * cells_z, bytes_accessed=8 * 3 * block * cells_z, transcendentals=0),
        name="spread",
    )(velocity, wzh, wzl, wy, fx)

    return pl.pallas_call(
        functools.partial(finish_kernel, chunked),
        out_shape=(shape(velocity.shape, f32), shape((3, owned), f32)),
        in_specs=[VMEM] * 7,
        out_specs=(pl.BlockSpec(memory_space=pl.ANY), VMEM),
        scratch_shapes=[pltpu.VMEM(velocity.shape, f32), pltpu.SemaphoreType.DMA((3,))],
        name="finish",
    )(rhs, from_x0, from_x1, from_y0, from_y1, returned, position)


def solution(mesh):
    in_specs = (
        P(None, "gx", "gy", None),
        P(None, ("gx", "gy")),
        P(None, None, ("gx", "gy")),
        P(None, ("gx", "gy")),
        P(("gx", "gy"), None),
    )
    out_specs = (P(None, "gx", "gy", None), P(None, ("gx", "gy")))
    return jax.shard_map(
        per_device, mesh=mesh, in_specs=in_specs, out_specs=out_specs, check_vma=False
    )
```

time: 119 us -> 54.2 us (0.46)
  the two profiles are of different devices: /device:TPU:0 before, /device:TPU:1 now
where the time goes in v1:
time: 54.2 us; the launch traced here: 53.8 us
  Pallas kernels  27.8 us (51%)
  starting transfers between devices  21.1 us (39%)
  waiting for transfers between devices  2.72 us (5%)
  local copies, waits for them, and re-layouts  1.38 us (3%)
  between operations  0.72 us (1%)
    pallas_call x1, Pallas kernels, per_device(): pl.pallas_call(functools.partial(sample_kernel, chunked, tile), out_shape...  9.76 us
    all_to_all x2, starting transfers between devices, exchange(): return lax.all_to_all(packed, 'gx', split_axis=0, concat_axis=0, tiled=True)  9.7 us
    pallas_call x1, Pallas kernels, per_device(): pl.pallas_call(spread_kernel, out_shape=shape(velocity.shape, f32), in_sp...  7.36 us
    ppermute x1, starting transfers between devices, per_device(): from_y0 = lax.ppermute(y1, 'gy', up_y)  5.01 us
    pallas_call x1, Pallas kernels, per_device(): pl.pallas_call(functools.partial(finish_kernel, chunked), out_shape=(shap...  4.95 us
    pallas_call x1, Pallas kernels, per_device(): pl.pallas_call(split_kernel, out_shape=(shape((3, block, cells_z), bf16),...  3.37 us
    ppermute x1, starting transfers between devices, per_device(): from_x1 = lax.ppermute(x0, 'gx', down_x)  2.8 us
    all_to_all x2, waiting for transfers between devices, exchange(): return lax.all_to_all(packed, 'gx', split_axis=0, concat_axis=0, tiled=True)  2.71 us
  transfers between devices with their start and end apart: 6, of which 1 were waited for; matrix products, arithmetic and copies ran while one was open for 0% of the time, Pallas kernels for 20%

profile of v1, /device:TPU:1, one launch (start us, length us, event | category | flops | bytes accessed | tf_op | source)
XLA Modules:
  0.0 53.8 jit_solution(1533963050707474940)
XLA Ops:
  0.6 2.4 %pack.1 = (f32[8,24,128]{2,1,0:T(8,128)}, s32[1,512]{1,0:T(1,128)}) custom-call(s32[1,512]{1,0:T(1,128)} %bitcast.1, f32[3,512]{1,0:T(4,128)} %target_ref.1, f32[3,6,512]{2,1,0:T(8,128)} %weights_ref.1, s32[3,512]{1,0:T(4,128)} %corners_ref.1), custom_call_target="tpu_custom_call" | custom-call | tf_op jit(solution)/shard_map/pack/pallas_call | solution.py:218
  3.0 6.4 %all-to-all-start = ((f32[8,24,128]{2,1,0:T(8,128)}), f32[8,24,128]{2,1,0:T(8,128)S(1)}, u32[]{:S(2)}, u32[]{:S(2)}) async-start(f32[8,24,128]{2,1,0:T(8,128)} %get-tuple-element.15), calls=%async_computation | async-start | bytes 196608 | tf_op jit(solution)/shard_map/all_to_all | solution.py:210
  9.4 3.4 %split.1 = (bf16[3,768,256]{2,1,0:T(8,128)(2,1)}, bf16[3,768,256]{2,1,0:T(8,128)(2,1)}) custom-call(f32[3,12,64,256]{3,2,1,0:T(8,128)} %velocity_ref.5), custom_call_target="tpu_custom_call" | custom-call | tf_op jit(solution)/shard_map/split/pallas_call | solution.py:229
  12.8 2.7 %all-to-all-done.arrived_ref = f32[8,24,128]{2,1,0:T(8,128)S(1)} async-done(((f32[8,24,128]{2,1,0:T(8,128)}), f32[8,24,128]{2,1,0:T(8,128)S(1)}, u32[]{:S(2)}, u32[]{:S(2)}) %all-to-all-start) | async-done | bytes 98336 | tf_op jit(solution)/shard_map/all_to_all | solution.py:210
  15.5 0.0 copy-start
  15.5 0.6 %copy-done = f32[8,24,128]{2,1,0:T(8,128)} copy-done((f32[8,24,128]{2,1,0:T(8,128)}, f32[8,24,128]{2,1,0:T(8,128)S(1)}, u32[]{:S(2)}) %copy-start) | copy-done | bytes 98328
  16.1 9.8 %sample.1 = (f32[8,8,128]{2,1,0:T(8,128)}, bf16[256,1024]{1,0:T(8,128)(2,1)}, bf16[256,1024]{1,0:T(8,128)(2,1)}, f32[64,1024]{1,0:T(8,128)}, f32[3,12,1024]{2,1,...) custom-call(f32[8,24,128]{2,1,0:T(8,128)} %copy-done, ...), custom_call_target="tpu_custom_call" | custom-call | tf_op jit(solution)/shard_map/sample/pallas_call | solution.py:241
  25.9 3.3 %all-to-all-start.1 = ((f32[8,8,128]{2,1,0:T(8,128)}), f32[8,8,128]{2,1,0:T(8,128)S(1)}, u32[]{:S(2)}, u32[]{:S(2)}) async-start(f32[8,8,128]{2,1,0:T(8,128)} %get-tuple-element.26), calls=%async_computation.1 | async-start | bytes 65536 | tf_op jit(solution)/shard_map/all_to_all | solution.py:210
  29.2 5.0 %collective-permute-start.2 = (f32[3,12,256]{2,1,0:T(8,128)}, f32[3,12,256]{2,1,0:T(8,128)S(1)}, u32[]{:S(2)}, u32[]{:S(2)}) collective-permute-start(f32[3,12,256]{2,1,0:T(8,128)} %get-tuple-element.24), channel_id=1, source_target_pairs={{0,1},{1,2},{2,3},{4,5},{5,6},{6,7},{8,9},{9,10},{10,11},{12,13},{... | collective-permute-start | bytes 110600 | tf_op jit(solution)/shard_map/ppermute | solution.py:263
  34.2 1.9 %collective-permute-start.3 = (f32[3,12,256]{2,1,0:T(8,128)}, f32[3,12,256]{2,1,0:T(8,128)S(1)}, u32[]{:S(2)}, u32[]{:S(2)}) collective-permute-start(f32[3,12,256]{2,1,0:T(8,128)} %get-tuple-element.25), channel_id=1, source_target_pairs={{1,0},{2,1},{3,2},{5,4},{6,5},{7,6},{9,8},{10,9},{11,10},{13,12},{... | collective-permute-start | bytes 110600 | tf_op jit(solution)/shard_map/ppermute | solution.py:264
  36.2 1.7 %collective-permute-start = (f32[3,64,256]{2,1,0:T(8,128)}, f32[3,64,256]{2,1,0:T(8,128)S(1)}, u32[]{:S(2)}, u32[]{:S(2)}) collective-permute-start(f32[3,64,256]{2,1,0:T(8,128)} %get-tuple-element.22), channel_id=1, source_target_pairs={{0,4},{4,8},{8,12},{12,16},{16,20},{20,24},{24,28},{28,0},{1,5},{5... | collective-permute-start | bytes 589832 | tf_op jit(solution)/shard_map/ppermute | solution.py:261
  37.8 2.8 %collective-permute-start.1 = (f32[3,64,256]{2,1,0:T(8,128)}, f32[3,64,256]{2,1,0:T(8,128)S(1)}, u32[]{:S(2)}, u32[]{:S(2)}) collective-permute-start(f32[3,64,256]{2,1,0:T(8,128)} %get-tuple-element.23), channel_id=1, source_target_pairs={{4,0},{8,4},{12,8},{16,12},{20,16},{24,20},{28,24},{0,28},{5,1},{9... | collective-permute-start | bytes 589832 | tf_op jit(solution)/shard_map/ppermute | solution.py:262
  40.6 7.4 %spread.1.rhs_ref = f32[3,12,64,256]{3,2,1,0:T(8,128)} custom-call(f32[3,12,64,256]{3,2,1,0:T(8,128)} %velocity_ref.5, bf16[256,1024]{1,0:T(8,128)(2,1)} %get-tuple-element.18.wzh_ref, bf16[256,1024]{1,0:T(8,128)(2,1)} %get-tuple-element.19.wzl_ref, f32[64,1024]{1,0:T(8,128)} %get-tuple-element.20.wy_ref, f32[3,12,1024]{2,1,0:T(8,128)} %get-tuple-element.21.fx_ref), custom_call_target="tpu_custom_call" | custom-call | flops 3623878656 | bytes 4718592 | tf_op jit(solution)/shard_map/spread/pallas_call | solution.py:267
  48.0 0.0 collective-permute-done.2.y0_ref
  48.0 0.0 copy-start.4
  48.0 0.0 collective-permute-done.3.y1_ref
  48.0 0.0 copy-start.5
  48.0 0.0 all-to-all-done.1.returned_ref
  48.0 0.0 copy-start.3
  48.1 0.0 collective-permute-done.x0_ref
  48.1 0.0 copy-start.1
  48.1 0.0 collective-permute-done.1.x1_ref
  48.1 0.0 copy-start.2
  48.1 0.5 copy-done.4
  48.6 0.0 copy-done.5
  48.7 0.0 copy-done.3
  48.7 0.1 copy-done.1
  48.7 0.1 copy-done.2
  48.8 5.0 %finish.1 = (f32[3,12,64,256]{3,2,1,0:T(8,128)}, f32[3,512]{1,0:T(4,128)}) custom-call(f32[3,12,64,256]{3,2,1,0:T(8,128)} %spread.1.rhs_ref, f32[3,64,256]{2,1,0:T(8,128)} %copy-done.1, f32[3,64,256]{2,1,0:T(8,128)} %copy-done.2, f32[3,12,256]{2,1,0:T(8,128)} %copy-done.4, f32[3,12,256]{2,1,0:T(8,128)} %copy-done.5, f32[8,8,128]{2,1,0:T(8,128)} %copy-done.3, ...), custom_call_target="tpu_custom_call" | custom-call | tf_op jit(solution)/shard_map/finish/pallas_call | solution.py:277
Async XLA Ops:
  3.0 12.4 %all-to-all-start = ((f32[8,24,128]{2,1,0:T(8,128)}), f32[8,24,128]{2,1,0:T(8,128)S(1)}, u32[]{:S(2)}, u32[]{:S(2)}) async-start(f32[8,24,128]{2,1,0:T(8,128)} %get-tuple-element.15), calls=%async_computation | async-start | bytes 196608 | tf_op jit(solution)/shard_map/all_to_all | solution.py:210
  15.5 0.6 %copy-start = (f32[8,24,128]{2,1,0:T(8,128)}, f32[8,24,128]{2,1,0:T(8,128)S(1)}, u32[]{:S(2)}) copy-start(f32[8,24,128]{2,1,0:T(8,128)S(1)} %all-to-all-done.arrived_ref) | copy-start | bytes 294916
  25.9 22.1 %all-to-all-start.1 = ((f32[8,8,128]{2,1,0:T(8,128)}), f32[8,8,128]{2,1,0:T(8,128)S(1)}, u32[]{:S(2)}, u32[]{:S(2)}) async-start(f32[8,8,128]{2,1,0:T(8,128)} %get-tuple-element.26), calls=%async_computation.1 | async-start | bytes 65536 | tf_op jit(solution)/shard_map/all_to_all | solution.py:210
  29.2 18.8 %collective-permute-start.2 = (f32[3,12,256]{2,1,0:T(8,128)}, f32[3,12,256]{2,1,0:T(8,128)S(1)}, u32[]{:S(2)}, u32[]{:S(2)}) collective-permute-start(f32[3,12,256]{2,1,0:T(8,128)} %get-tuple-element.24), channel_id=1, source_target_pairs={{0,1},{1,2},{2,3},{4,5},{5,6},{6,7},{8,9},{9,10},{10,11},{12,13},{... | collective-permute-start | bytes 110600 | tf_op jit(solution)/shard_map/ppermute | solution.py:263
  34.2 13.8 %collective-permute-start.3 = (f32[3,12,256]{2,1,0:T(8,128)}, f32[3,12,256]{2,1,0:T(8,128)S(1)}, u32[]{:S(2)}, u32[]{:S(2)}) collective-permute-start(f32[3,12,256]{2,1,0:T(8,128)} %get-tuple-element.25), channel_id=1, source_target_pairs={{1,0},{2,1},{3,2},{5,4},{6,5},{7,6},{9,8},{10,9},{11,10},{13,12},{... | collective-permute-start | bytes 110600 | tf_op jit(solution)/shard_map/ppermute | solution.py:264
  36.2 11.9 %collective-permute-start = (f32[3,64,256]{2,1,0:T(8,128)}, f32[3,64,256]{2,1,0:T(8,128)S(1)}, u32[]{:S(2)}, u32[]{:S(2)}) collective-permute-start(f32[3,64,256]{2,1,0:T(8,128)} %get-tuple-element.22), channel_id=1, source_target_pairs={{0,4},{4,8},{8,12},{12,16},{16,20},{20,24},{24,28},{28,0},{1,5},{5... | collective-permute-start | bytes 589832 | tf_op jit(solution)/shard_map/ppermute | solution.py:261
  37.8 10.2 %collective-permute-start.1 = (f32[3,64,256]{2,1,0:T(8,128)}, f32[3,64,256]{2,1,0:T(8,128)S(1)}, u32[]{:S(2)}, u32[]{:S(2)}) collective-permute-start(f32[3,64,256]{2,1,0:T(8,128)} %get-tuple-element.23), channel_id=1, source_target_pairs={{4,0},{8,4},{12,8},{16,12},{20,16},{24,20},{28,24},{0,28},{5,1},{9... | collective-permute-start | bytes 589832 | tf_op jit(solution)/shard_map/ppermute | solution.py:262
  48.0 0.6 %copy-start.4 = (f32[3,12,256]{2,1,0:T(8,128)}, f32[3,12,256]{2,1,0:T(8,128)S(1)}, u32[]{:S(2)}) copy-start(f32[3,12,256]{2,1,0:T(8,128)S(1)} %collective-permute-done.2.y0_ref) | copy-start | bytes 110596
  48.0 0.6 %copy-start.5 = (f32[3,12,256]{2,1,0:T(8,128)}, f32[3,12,256]{2,1,0:T(8,128)S(1)}, u32[]{:S(2)}) copy-start(f32[3,12,256]{2,1,0:T(8,128)S(1)} %collective-permute-done.3.y1_ref) | copy-start | bytes 110596
  48.0 0.6 %copy-start.3 = (f32[8,8,128]{2,1,0:T(8,128)}, f32[8,8,128]{2,1,0:T(8,128)S(1)}, u32[]{:S(2)}) copy-start(f32[8,8,128]{2,1,0:T(8,128)S(1)} %all-to-all-done.1.returned_ref) | copy-start | bytes 98308
  48.1 0.7 %copy-start.1 = (f32[3,64,256]{2,1,0:T(8,128)}, f32[3,64,256]{2,1,0:T(8,128)S(1)}, u32[]{:S(2)}) copy-start(f32[3,64,256]{2,1,0:T(8,128)S(1)} %collective-permute-done.x0_ref) | copy-start | bytes 589828
  48.1 0.7 %copy-start.2 = (f32[3,64,256]{2,1,0:T(8,128)}, f32[3,64,256]{2,1,0:T(8,128)S(1)}, u32[]{:S(2)}) copy-start(f32[3,64,256]{2,1,0:T(8,128)S(1)} %collective-permute-done.1.x1_ref) | copy-start | bytes 589828

commit v2 on v1

v2 whole, which is shorter than its diff:
```python
import functools

import jax
import jax.numpy as jnp
from jax import lax
from jax.experimental import pallas as pl
from jax.experimental.pallas import tpu as pltpu
from jax.sharding import PartitionSpec as P


SLOT_MIN = 12
SPAN = 6
ROWS = 24

diffusion = 0.4


f32 = jnp.float32
bf16 = jnp.bfloat16
i32 = jnp.int32
VMEM = pl.BlockSpec(memory_space=pltpu.VMEM)
HBM = pl.BlockSpec(memory_space=pltpu.HBM)
NN = (((1,), (0,)), ((), ()))
NT = (((1,), (1,)), ((), ()))


def dot(a, b, dims=NN):
    return lax.dot_general(a, b, dims, preferred_element_type=f32)


def halves(x):
    high = x.astype(bf16)
    return high, (x - high.astype(f32)).astype(bf16)


def dot3(ah, al, bh, bl, dims=NN):
    return dot(ah, bh, dims) + dot(ah, bl, dims) + dot(al, bh, dims)


def thirds(x):
    high = x.astype(bf16).astype(f32)
    rest = x - high
    mid = rest.astype(bf16).astype(f32)
    return jnp.concatenate([high, mid, rest - mid], axis=0).astype(bf16)


def one_hot(position, slots):
    rows = lax.broadcasted_iota(i32, (slots, position.shape[1]), 0)
    return jnp.where(rows == position, 1.0, 0.0).astype(bf16)


def pack_kernel(capacity, chunked, span_y, dest_ref, target_ref, weights_ref, corners_ref, out_ref, pos_ref, rows_ref):
    owned = target_ref.shape[1]
    dest = dest_ref[...]
    lane = lax.broadcasted_iota(i32, (1, owned), 1)
    first = dest * (span_y * owned)
    key = first + corners_ref[1:2, :] * owned + lane
    column = jnp.transpose(jnp.broadcast_to(key, (8, owned)))[:, 0:1]
    ahead = jnp.where((column < key) & (column >= first), 1.0, 0.0)
    position = dest * capacity + jnp.sum(ahead, axis=0, keepdims=True).astype(i32)
    pos_ref[...] = position
    rows_ref[0:3, :] = target_ref[...]
    for dim in range(3):
        rows_ref[3 + 6 * dim : 9 + 6 * dim, :] = weights_ref[dim]
    rows_ref[21:24, :] = corners_ref[...].astype(f32)
    slots = out_ref.size // ROWS
    moved = dot(thirds(rows_ref[...]), one_hot(position, slots), NT)
    moved = moved[0:ROWS] + moved[ROWS : 2 * ROWS] + moved[2 * ROWS :]
    if chunked:
        for chunk in range(slots // capacity):
            out_ref[chunk] = moved[:, chunk * capacity : (chunk + 1) * capacity]
    else:
        out_ref[...] = moved


def split_kernel(velocity_ref, high_ref, low_ref, x0_ref, x1_ref):
    _, cells_x, cells_y, cells_z = velocity_ref.shape
    high, low = halves(velocity_ref[0].reshape(cells_x * cells_y, cells_z))
    high_ref[0] = high
    low_ref[0] = low
    x0_ref[0] = velocity_ref[0, 0]
    x1_ref[0] = velocity_ref[0, cells_x - 1]


def window(weights, corner, length):
    offset = lax.broadcasted_iota(i32, (length, weights.shape[1]), 0) - corner
    out = jnp.zeros(offset.shape, f32)
    for k in range(SPAN):
        out = jnp.where(offset == k, weights[k : k + 1, :], out)
    return out


def tiles_of(arrived_ref, tile, slots):
    for t in range(slots // tile):
        at = slice(t * tile, (t + 1) * tile)
        if len(arrived_ref.shape) == 3:
            per = tile // arrived_ref.shape[2]
            yield at, jnp.concatenate([arrived_ref[t * per + k] for k in range(per)], axis=1)
        else:
            yield at, arrived_ref[:, at]


def sample_kernel(
    tile, arrived_ref, high_hbm, low_hbm, velocity_hbm,
    force_ref, wzh_hbm, wzl_hbm, wy_ref, fx_ref, y0_ref, y1_ref,
    high_ref, low_ref, lower_ref, upper_ref, wzh_ref, wzl_ref, boxh_ref, boxl_ref, in_sem, edge_sem, out_sem,
):
    cells_x, cells_z = y0_ref.shape[1:]
    cells_y, slots = wy_ref.shape
    loads = []
    for c in range(3):
        pair = [
            pltpu.make_async_copy(high_hbm.at[c], high_ref.at[c], in_sem.at[0, c]),
            pltpu.make_async_copy(low_hbm.at[c], low_ref.at[c], in_sem.at[1, c]),
        ]
        for load in pair:
            load.start()
        loads.append(pair)
    edges = [
        pltpu.make_async_copy(velocity_hbm.at[:, :, pl.ds(0, 8), :], lower_ref, edge_sem.at[0]),
        pltpu.make_async_copy(velocity_hbm.at[:, :, pl.ds(cells_y - 8, 8), :], upper_ref, edge_sem.at[1]),
    ]
    for load in edges:
        load.start()
    kept = []
    for at, data in tiles_of(arrived_ref, tile, slots):
        corner = data[21:24, :].astype(i32)
        wy_ref[:, at] = window(data[9:15], corner[1:2], cells_y)
        high, low = halves(window(data[15:21], corner[2:3], cells_z))
        wzh_ref[:, at] = high
        wzl_ref[:, at] = low
        kept.append((at, data[0:3], window(data[3:9], corner[0:1], cells_x)))
    stores = [
        pltpu.make_async_copy(wzh_ref, wzh_hbm, out_sem.at[0]),
        pltpu.make_async_copy(wzl_ref, wzl_hbm, out_sem.at[1]),
    ]
    for store in stores:
        store.start()
    for c in range(3):
        for load in loads[c]:
            load.wait()
        for at, target, wx in kept:
            along = dot3(high_ref[c], low_ref[c], wzh_ref[:, at], wzl_ref[:, at])
            along = along.reshape(cells_x, cells_y, tile) * wy_ref[:, at][None]
            sampled = jnp.sum(jnp.sum(along, axis=1) * wx, axis=0, keepdims=True)
            force = target[c : c + 1] - sampled
            fx_ref[c, :, at] = force * wx
            for k in range(force_ref.shape[0]):
                force_ref[k, c : c + 1, at] = force
    pad = boxh_ref.shape[0] // 6
    base = 0
    for y in (0, cells_y - 1):
        for c in range(3):
            rows = fx_ref[c] * wy_ref[y : y + 1, :]
            rows = jnp.concatenate([rows, jnp.zeros((pad - cells_x, slots), f32)], axis=0)
            high, low = halves(rows)
            boxh_ref[base : base + pad] = high
            boxl_ref[base : base + pad] = low
            base += pad
    spread = dot3(boxh_ref[...], boxl_ref[...], wzh_ref[...], wzl_ref[...], NT)
    for load in edges:
        load.wait()
    base = 0
    for y, slab_ref, ref in ((0, lower_ref, y0_ref), (7, upper_ref, y1_ref)):
        for c in range(3):
            ref[c] = slab_ref[c, :, y, :] + spread[base : base + cells_x]
            base += pad
    for store in stores:
        store.wait()


def spread_kernel(
    velocity_hbm, wzh_ref, wzl_ref, wy_ref, fx_ref, rhs_hbm, boxh_ref, boxl_ref, cell_ref, in_sem, out_sem,
):
    _, cells_x, cells_y, cells_z = velocity_hbm.shape
    loads = [pltpu.make_async_copy(velocity_hbm.at[c], cell_ref.at[c], in_sem.at[c]) for c in range(3)]
    stores = [pltpu.make_async_copy(cell_ref.at[c], rhs_hbm.at[c], out_sem.at[c]) for c in range(3)]
    for load in loads:
        load.start()
    wy = wy_ref[...]
    for c in range(3):
        for x in range(cells_x):
            high, low = halves(fx_ref[c, x : x + 1, :] * wy)
            boxh_ref[x * cells_y : (x + 1) * cells_y] = high
            boxl_ref[x * cells_y : (x + 1) * cells_y] = low
        spread = dot3(boxh_ref[...], boxl_ref[...], wzh_ref[...], wzl_ref[...], NT)
        loads[c].wait()
        cell_ref[c] = cell_ref[c] + spread.reshape(cells_x, cells_y, cells_z)
        stores[c].start()
    for store in stores:
        store.wait()


def finish_kernel(
    tile, n_stream, n_wall, chunked,
    rhs_hbm, x0_ref, x1_ref, y0_ref, y1_ref, left_ref, right_ref, given_ref, held_ref, pos_ref,
    next_hbm, force_ref, rhs_ref, next_ref, face_ref, wzh_ref, wzl_ref, boxh_ref, boxl_ref, in_sem, out_sem,
):
    _, cells_x, cells_y, cells_z = rhs_hbm.shape
    slots = given_ref.shape[2]
    loads = [pltpu.make_async_copy(rhs_hbm.at[c], rhs_ref.at[c], in_sem.at[c]) for c in range(3)]
    stores = [pltpu.make_async_copy(next_ref.at[c], next_hbm.at[c], out_sem.at[c]) for c in range(3)]
    for load in loads:
        load.start()
    here = lax.axis_index("gx")
    wall = lax.axis_index("gy")
    sides = (
        (0, left_ref, x0_ref, cells_x - SPAN, SPAN - 1, lax.rem(here + n_stream - 1, n_stream)),
        (1, right_ref, x1_ref, 0, 0, lax.rem(here + 1, n_stream)),
    )
    for side, arrived_ref, plane_ref, touching, row, owner in sides:
        for at, data in tiles_of(arrived_ref, tile, slots):
            corner = data[21:24, :].astype(i32)
            wy = window(data[9:15], corner[1:2], cells_y)
            high, low = halves(window(data[15:21], corner[2:3], cells_z))
            wzh_ref[:, at] = high
            wzl_ref[:, at] = low
            wx = jnp.where(corner[0:1] == touching, data[3 + row : 4 + row], 0.0)
            force = given_ref[owner, :, at] * wx
            for c in range(3):
                high, low = halves(force[c : c + 1] * wy)
                boxh_ref[c * cells_y : (c + 1) * cells_y, at] = high
                boxl_ref[c * cells_y : (c + 1) * cells_y, at] = low
        spread = dot3(boxh_ref[...], boxl_ref[...], wzh_ref[...], wzl_ref[...], NT)
        face_ref[side] = plane_ref[...] + spread.reshape(3, cells_y, cells_z)
    y = lax.broadcasted_iota(i32, (cells_y, cells_z), 0)
    lower = jnp.where(wall == 0, 0.0, 1.0).astype(f32)
    upper = jnp.where(wall == n_wall - 1, 0.0, 1.0).astype(f32)
    scale = 1.0 / (1.0 + 6.0 * diffusion)
    for c in range(3):
        loads[c].wait()
        for x in range(cells_x):
            cell = rhs_ref[c, x]
            back = rhs_ref[c, x - 1] if x else face_ref[0, c]
            ahead = rhs_ref[c, x + 1] if x < cells_x - 1 else face_ref[1, c]
            below = jnp.where(y == 0, y0_ref[c, x : x + 1, :] * lower, pltpu.roll(cell, 1, 0))
            above = jnp.where(y == cells_y - 1, y1_ref[c, x : x + 1, :] * upper, pltpu.roll(cell, cells_y - 1, 0))
            side = pltpu.roll(cell, 1, 1) + pltpu.roll(cell, cells_z - 1, 1)
            near = (ahead + back) + (above + below) + side
            next_ref[c, x] = (cell + diffusion * near) * scale
        stores[c].start()
    if chunked:
        capacity = slots // n_stream
        mine = pl.ds(pl.multiple_of(here * capacity, capacity), capacity)
        held = jnp.concatenate([given_ref[k, :, mine] for k in range(n_stream)], axis=1)
    else:
        held = held_ref[...]
    held = jnp.concatenate([held, jnp.zeros((5, slots), f32)], axis=0)
    moved = dot(thirds(held), one_hot(pos_ref[...], slots))
    moved = moved[0:8] + moved[8:16] + moved[16:24]
    force_ref[...] = moved[0:3]
    for store in stores:
        store.wait()


def per_device(velocity, target, weights, corners, dest):
    n_stream = lax.axis_size("gx")
    n_wall = lax.axis_size("gy")
    owned = target.shape[1]
    capacity = max(SLOT_MIN, 2 * owned // n_stream)
    slots = n_stream * capacity
    _, cells_x, cells_y, cells_z = velocity.shape
    block = cells_x * cells_y
    chunked = capacity % 128 == 0
    tile = 256 if slots % 256 == 0 else 128
    shape = jax.ShapeDtypeStruct
    sems = pltpu.SemaphoreType.DMA

    outgoing, position = pl.pallas_call(
        functools.partial(pack_kernel, capacity, chunked, cells_y),
        out_shape=(
            shape((n_stream, ROWS, capacity) if chunked else (ROWS, slots), f32),
            shape((1, owned), i32),
        ),
        in_specs=[VMEM] * 4,
        out_specs=(VMEM, VMEM),
        scratch_shapes=[pltpu.VMEM((ROWS, owned), f32)],
        name="pack",
    )(dest.reshape(1, owned), target, weights, corners)
    if chunked:
        arrived = lax.all_to_all(outgoing, "gx", split_axis=0, concat_axis=0, tiled=True)
    else:
        outgoing = outgoing.reshape(ROWS, n_stream, capacity)
        arrived = lax.all_to_all(outgoing, "gx", split_axis=1, concat_axis=1, tiled=True)
        arrived = arrived.reshape(ROWS, slots)

    high, low, x0, x1 = pl.pallas_call(
        split_kernel,
        grid=(3,),
        out_shape=(
            shape((3, block, cells_z), bf16),
            shape((3, block, cells_z), bf16),
            shape((3, cells_y, cells_z), f32),
            shape((3, cells_y, cells_z), f32),
        ),
        in_specs=[pl.BlockSpec((1, cells_x, cells_y, cells_z), lambda c: (c, 0, 0, 0))],
        out_specs=(
            pl.BlockSpec((1, block, cells_z), lambda c: (c, 0, 0)),
            pl.BlockSpec((1, block, cells_z), lambda c: (c, 0, 0)),
            pl.BlockSpec((1, cells_y, cells_z), lambda c: (c, 0, 0)),
            pl.BlockSpec((1, cells_y, cells_z), lambda c: (c, 0, 0)),
        ),
        name="split",
    )(velocity)

    up_x = [(i, (i + 1) % n_stream) for i in range(n_stream)]
    down_x = [(j, i) for i, j in up_x]
    up_y = [(i, (i + 1) % n_wall) for i in range(n_wall)]
    down_y = [(j, i) for i, j in up_y]
    from_x0 = lax.ppermute(x1, "gx", up_x)
    from_x1 = lax.ppermute(x0, "gx", down_x)
    left = lax.ppermute(arrived, "gx", up_x)
    right = lax.ppermute(arrived, "gx", down_x)

    pad = -(-cells_x // 16) * 16
    force, wzh, wzl, wy, fx, y0, y1 = pl.pallas_call(
        functools.partial(sample_kernel, tile),
        out_shape=(
            shape((n_stream, 3, slots), f32),
            shape((cells_z, slots), bf16),
            shape((cells_z, slots), bf16),
            shape((cells_y, slots), f32),
            shape((3, cells_x, slots), f32),
            shape((3, cells_x, cells_z), f32),
            shape((3, cells_x, cells_z), f32),
        ),
        in_specs=[VMEM, HBM, HBM, HBM],
        out_specs=(VMEM, HBM, HBM, VMEM, VMEM, VMEM, VMEM),
        scratch_shapes=[
            pltpu.VMEM((3, block, cells_z), bf16),
            pltpu.VMEM((3, block, cells_z), bf16),
            pltpu.VMEM((3, cells_x, 8, cells_z), f32),
            pltpu.VMEM((3, cells_x, 8, cells_z), f32),
            pltpu.VMEM((cells_z, slots), bf16),
            pltpu.VMEM((cells_z, slots), bf16),
            pltpu.VMEM((6 * pad, slots), bf16),
            pltpu.VMEM((6 * pad, slots), bf16),
            sems((2, 3)),
            sems((2,)),
            sems((2,)),
        ],
        compiler_params=pltpu.CompilerParams(vmem_limit_bytes=63_280_000),
        name="sample",
    )(arrived, high, low, velocity)

    from_y0 = lax.ppermute(y1, "gy", up_y)
    from_y1 = lax.ppermute(y0, "gy", down_y)
    given = lax.all_to_all(force, "gx", split_axis=0, concat_axis=0, tiled=True)
    if chunked:
        held = jnp.zeros((8, 128), f32)
    else:
        held = lax.dynamic_slice_in_dim(given, lax.axis_index("gx") * capacity, capacity, axis=2)
        held = held.transpose(1, 0, 2).reshape(3, slots)

    rhs = pl.pallas_call(
        spread_kernel,
        out_shape=shape(velocity.shape, f32),
        in_specs=[HBM, VMEM, VMEM, VMEM, VMEM],
        out_specs=HBM,
        scratch_shapes=[
            pltpu.VMEM((block, slots), bf16),
            pltpu.VMEM((block, slots), bf16),
            pltpu.VMEM(velocity.shape, f32),
            sems((3,)),
            sems((3,)),
        ],
        cost_estimate=pl.CostEstimate(flops=18 * block * slots * cells_z, bytes_accessed=24 * block * cells_z, transcendentals=0),
        name="spread",
    )(velocity, wzh, wzl, wy, fx)

    return pl.pallas_call(
        functools.partial(finish_kernel, tile, n_stream, n_wall, chunked),
        out_shape=(shape(velocity.shape, f32), shape((3, owned), f32)),
        in_specs=[HBM] + [VMEM] * 9,
        out_specs=(HBM, VMEM),
        scratch_shapes=[
            pltpu.VMEM(velocity.shape, f32),
            pltpu.VMEM(velocity.shape, f32),
            pltpu.VMEM((2, 3, cells_y, cells_z), f32),
            pltpu.VMEM((cells_z, slots), bf16),
            pltpu.VMEM((cells_z, slots), bf16),
            pltpu.VMEM((3 * cells_y, slots), bf16),
            pltpu.VMEM((3 * cells_y, slots), bf16),
            sems((3,)),
            sems((3,)),
        ],
        compiler_params=pltpu.CompilerParams(vmem_limit_bytes=62_400_000),
        name="finish",
    )(rhs, from_x0, from_x1, from_y0, from_y1, left, right, given, held, position)


def solution(mesh):
    in_specs = (
        P(None, "gx", "gy", None),
        P(None, ("gx", "gy")),
        P(None, None, ("gx", "gy")),
        P(None, ("gx", "gy")),
        P(("gx", "gy"), None),
    )
    out_specs = (P(None, "gx", "gy", None), P(None, ("gx", "gy")))
    return jax.shard_map(
        per_device, mesh=mesh, in_specs=in_specs, out_specs=out_specs, check_vma=False
    )
```

time: 54.2 us -> 58.6 us (1.081)
  the two profiles are of different devices: /device:TPU:1 before, /device:TPU:0 now
where the time goes in v2:
time: 58.6 us; the launch traced here: 58.1 us
  Pallas kernels  30.8 us (53%)
  starting transfers between devices  22.4 us (38%)
  waiting for transfers between devices  2.52 us (4%)
  local copies, waits for them, and re-layouts  1.43 us (2%)
  between operations  0.95 us (2%)
    pallas_call x1, Pallas kernels, per_device(): pl.pallas_call(spread_kernel, out_shape=shape(velocity.shape, f32), in_sp...  9.3 us
    pallas_call x1, Pallas kernels, per_device(): pl.pallas_call(functools.partial(sample_kernel, tile), out_shape=(shape((...  8.39 us
    pallas_call x1, Pallas kernels, per_device(): pl.pallas_call(functools.partial(finish_kernel, tile, n_stream, n_wall, c...  6.75 us
    all_to_all x1, starting transfers between devices, per_device(): lax.all_to_all(outgoing, 'gx', split_axis=0, concat_axis=0, tiled=True)  4.88 us
    ppermute x1, starting transfers between devices, per_device(): from_x1 = lax.ppermute(x0, 'gx', down_x)  4.72 us
    ppermute x1, starting transfers between devices, per_device(): right = lax.ppermute(arrived, 'gx', down_x)  4.61 us
    pallas_call x1, Pallas kernels, per_device(): pl.pallas_call(split_kernel, grid=(3,), out_shape=(shape((3, block, cells...  3.99 us
    all_to_all x1, starting transfers between devices, per_device(): given = lax.all_to_all(force, 'gx', split_axis=0, concat_axis=0, tiled=True)  3.38 us
  transfers between devices with their start and end apart: 8, of which 1 were waited for; matrix products, arithmetic and copies ran while one was open for 0% of the time, Pallas kernels for 35%

profile of v2, /device:TPU:0, one launch (start us, length us, event | category | flops | bytes accessed | tf_op | source)
XLA Modules:
  0.0 58.1 jit_solution(17584867709556699302)
XLA Ops:
  0.6 4.0 %split.1 = (bf16[3,768,256]{2,1,0:T(8,128)(2,1)}, bf16[3,768,256]{2,1,0:T(8,128)(2,1)}, f32[3,64,256]{2,1,0:T(8,128)}, f32[3,64,256]{2,1,0:T(8,128)}) custom-call(f32[3,12,64,256]{3,2,1,0:T(8,128)} %velocity_hbm.3), custom_call_target="tpu_custom_call" | custom-call | tf_op jit(solution)/shard_map/split/pallas_call | solution.py:287
  4.6 3.0 %collective-permute-start = (f32[3,64,256]{2,1,0:T(8,128)}, f32[3,64,256]{2,1,0:T(8,128)S(1)}, u32[]{:S(2)}, u32[]{:S(2)}) collective-permute-start(f32[3,64,256]{2,1,0:T(8,128)} %get-tuple-element.22), channel_id=1, source_target_pairs={{0,4},{4,8},{8,12},{12,16},{16,20},{20,24},{24,28},{28,0},{1,5},{5... | collective-permute-start | bytes 589832 | tf_op jit(solution)/shard_map/ppermute | solution.py:310
  7.6 2.4 %pack.1 = (f32[8,24,128]{2,1,0:T(8,128)}, s32[1,512]{1,0:T(1,128)}) custom-call(s32[1,512]{1,0:T(1,128)} %bitcast.1, f32[3,512]{1,0:T(4,128)} %target_ref.1, f32[3,6,512]{2,1,0:T(8,128)} %weights_ref.1, s32[3,512]{1,0:T(4,128)} %corners_ref.1), custom_call_target="tpu_custom_call" | custom-call | tf_op jit(solution)/shard_map/pack/pallas_call | solution.py:269
  10.0 4.9 %all-to-all-start = ((f32[8,24,128]{2,1,0:T(8,128)}), f32[8,24,128]{2,1,0:T(8,128)S(1)}, u32[]{:S(2)}, u32[]{:S(2)}) async-start(f32[8,24,128]{2,1,0:T(8,128)} %get-tuple-element.15), calls=%async_computation | async-start | bytes 196608 | tf_op jit(solution)/shard_map/all_to_all | solution.py:281
  14.9 4.7 %collective-permute-start.1 = (f32[3,64,256]{2,1,0:T(8,128)}, f32[3,64,256]{2,1,0:T(8,128)S(1)}, u32[]{:S(2)}, u32[]{:S(2)}) collective-permute-start(f32[3,64,256]{2,1,0:T(8,128)} %get-tuple-element.23), channel_id=1, source_target_pairs={{4,0},{8,4},{12,8},{16,12},{20,16},{24,20},{28,24},{0,28},{5,1},{9... | collective-permute-start | bytes 589832 | tf_op jit(solution)/shard_map/ppermute | solution.py:311
  19.6 2.5 %all-to-all-done.arrived_ref = f32[8,24,128]{2,1,0:T(8,128)S(1)} async-done(((f32[8,24,128]{2,1,0:T(8,128)}), f32[8,24,128]{2,1,0:T(8,128)S(1)}, u32[]{:S(2)}, u32[]{:S(2)}) %all-to-all-start) | async-done | bytes 98336 | tf_op jit(solution)/shard_map/all_to_all | solution.py:281
  22.1 0.0 copy-start.1
  22.1 0.6 %copy-done.1 = f32[8,24,128]{2,1,0:T(8,128)} copy-done((f32[8,24,128]{2,1,0:T(8,128)}, f32[8,24,128]{2,1,0:T(8,128)S(1)}, u32[]{:S(2)}) %copy-start.1) | copy-done | bytes 98328
  22.8 8.4 %sample.1 = (f32[8,3,1024]{2,1,0:T(4,128)}, bf16[256,1024]{1,0:T(8,128)(2,1)}, bf16[256,1024]{1,0:T(8,128)(2,1)}, f32[64,1024]{1,0:T(8,128)}, f32[3,12,1024]{2,1...) custom-call(f32[8,24,128]{2,1,0:T(8,128)} %copy-done.1, bf16[3,768,256]{2,1,0:T(8,128)(2,1)} %get-tuple-element.16.high_hbm, ...), custom_call_target="tpu_custom_call" | custom-call | tf_op jit(solution)/shard_map/sample/pallas_call | solution.py:316
  31.2 3.4 %all-to-all-start.1 = ((f32[8,3,1024]{2,1,0:T(4,128)}), f32[8,3,1024]{2,1,0:T(4,128)S(1)}, u32[]{:S(2)}, u32[]{:S(2)}) async-start(f32[8,3,1024]{2,1,0:T(4,128)} %get-tuple-element.26), calls=%async_computation.1 | async-start | bytes 262144 | tf_op jit(solution)/shard_map/all_to_all | solution.py:348
  34.6 0.1 collective-permute-start.2
  34.6 1.7 %collective-permute-start.3 = (f32[3,12,256]{2,1,0:T(8,128)}, f32[3,12,256]{2,1,0:T(8,128)S(1)}, u32[]{:S(2)}, u32[]{:S(2)}) collective-permute-start(f32[3,12,256]{2,1,0:T(8,128)} %get-tuple-element.25), channel_id=1, source_target_pairs={{1,0},{2,1},{3,2},{0,3},{5,4},{6,5},{7,6},{4,7},{9,8},{10,9},{11,1... | collective-permute-start | bytes 110600 | tf_op jit(solution)/shard_map/ppermute | solution.py:347
  36.4 4.6 %collective-permute-start.5 = (f32[8,24,128]{2,1,0:T(8,128)}, f32[8,24,128]{2,1,0:T(8,128)S(1)}, u32[]{:S(2)}, u32[]{:S(2)}) collective-permute-start(f32[8,24,128]{2,1,0:T(8,128)} %copy-done.1), channel_id=1, source_target_pairs={{4,0},{8,4},{12,8},{16,12},{20,16},{24,20},{28,24},{0,28},{5,1},{9... | collective-permute-start | bytes 294920 | tf_op jit(solution)/shard_map/ppermute | solution.py:313
  41.0 0.0 collective-permute-done.x0_ref
  41.0 0.0 copy-start.2
  41.0 0.0 collective-permute-start.4
  41.0 9.3 %spread.1.rhs_hbm = f32[3,12,64,256]{3,2,1,0:T(8,128)} custom-call(f32[3,12,64,256]{3,2,1,0:T(8,128)} %velocity_hbm.3, bf16[256,1024]{1,0:T(8,128)(2,1)} %get-tuple-element.18.wzh_ref, bf16[256,1024]{1,0:T(8,128)(2,1)} %get-tuple-element.19.wzl_ref, f32[64,1024]{1,0:T(8,128)} %get-tuple-element.20.wy_ref, f32[3,12,1024]{2,1,0:T(8,128)} %get-tuple-element.21.fx_ref), custom_call_target="tpu_custom_call" | custom-call | flops 3623878656 | bytes 4718592 | tf_op jit(solution)/shard_map/spread/pallas_call | solution.py:355
  50.3 0.0 copy-done.2
  50.3 0.0 collective-permute-done.1.x1_ref
  50.3 0.0 copy-start.3
  50.3 0.0 collective-permute-done.2.y0_ref
  50.3 0.0 copy-start.6
  50.3 0.0 collective-permute-done.3.y1_ref
  50.3 0.0 copy-start.7
  50.4 0.0 collective-permute-done.5.right_ref
  50.4 0.0 copy-start.4
  50.4 0.0 collective-permute-done.4.left_ref
  50.4 0.0 copy-start.5
  50.4 0.0 all-to-all-done.1.given_ref
  50.4 0.0 copy-start
  50.4 0.7 %broadcast_in_dim.3.held_ref = f32[8,128]{1,0:T(8,128)} broadcast(f32[]{:T(128)} %constant.0.clone.1), dimensions={} | broadcast | bytes 4100 | tf_op jit(solution)/shard_map/broadcast_in_dim | solution.py:350
  51.1 0.0 copy-done.3
  51.1 0.0 copy-done.6
  51.1 0.0 copy-done.7
  51.1 0.0 copy-done.4
  51.1 0.0 copy-done.5
  51.1 0.1 copy-done
  51.2 6.7 %finish.1 = (f32[3,12,64,256]{3,2,1,0:T(8,128)}, f32[3,512]{1,0:T(4,128)}) custom-call(f32[3,12,64,256]{3,2,1,0:T(8,128)} %spread.1.rhs_hbm, f32[3,64,256]{2,1,0:T(8,128)} %copy-done.2, f32[3,64,256]{2,1,0:T(8,128)} %copy-done.3, f32[3,12,256]{2,1,0:T(8,128)} %copy-done.6, f32[3,12,256]{2,1,0:T(8,128)} %copy-done.7, f32[8,24,128]{2,1,0:T(8,128)} %copy-done.5, ...), custom_call_target="tpu_custom_call" | custom-call | tf_op jit(solution)/shard_map/finish/pallas_call | solution.py:371
Async XLA Ops:
  4.6 36.4 %collective-permute-start = (f32[3,64,256]{2,1,0:T(8,128)}, f32[3,64,256]{2,1,0:T(8,128)S(1)}, u32[]{:S(2)}, u32[]{:S(2)}) collective-permute-start(f32[3,64,256]{2,1,0:T(8,128)} %get-tuple-element.22), channel_id=1, source_target_pairs={{0,4},{4,8},{8,12},{12,16},{16,20},{20,24},{24,28},{28,0},{1,5},{5... | collective-permute-start | bytes 589832 | tf_op jit(solution)/shard_map/ppermute | solution.py:310
  10.0 12.1 %all-to-all-start = ((f32[8,24,128]{2,1,0:T(8,128)}), f32[8,24,128]{2,1,0:T(8,128)S(1)}, u32[]{:S(2)}, u32[]{:S(2)}) async-start(f32[8,24,128]{2,1,0:T(8,128)} %get-tuple-element.15), calls=%async_computation | async-start | bytes 196608 | tf_op jit(solution)/shard_map/all_to_all | solution.py:281
  14.9 35.4 %collective-permute-start.1 = (f32[3,64,256]{2,1,0:T(8,128)}, f32[3,64,256]{2,1,0:T(8,128)S(1)}, u32[]{:S(2)}, u32[]{:S(2)}) collective-permute-start(f32[3,64,256]{2,1,0:T(8,128)} %get-tuple-element.23), channel_id=1, source_target_pairs={{4,0},{8,4},{12,8},{16,12},{20,16},{24,20},{28,24},{0,28},{5,1},{9... | collective-permute-start | bytes 589832 | tf_op jit(solution)/shard_map/ppermute | solution.py:311
  22.1 0.7 %copy-start.1 = (f32[8,24,128]{2,1,0:T(8,128)}, f32[8,24,128]{2,1,0:T(8,128)S(1)}, u32[]{:S(2)}) copy-start(f32[8,24,128]{2,1,0:T(8,128)S(1)} %all-to-all-done.arrived_ref) | copy-start | bytes 294916
  31.2 19.2 %all-to-all-start.1 = ((f32[8,3,1024]{2,1,0:T(4,128)}), f32[8,3,1024]{2,1,0:T(4,128)S(1)}, u32[]{:S(2)}, u32[]{:S(2)}) async-start(f32[8,3,1024]{2,1,0:T(4,128)} %get-tuple-element.26), calls=%async_computation.1 | async-start | bytes 262144 | tf_op jit(solution)/shard_map/all_to_all | solution.py:348
  34.6 15.8 %collective-permute-start.2 = (f32[3,12,256]{2,1,0:T(8,128)}, f32[3,12,256]{2,1,0:T(8,128)S(1)}, u32[]{:S(2)}, u32[]{:S(2)}) collective-permute-start(f32[3,12,256]{2,1,0:T(8,128)} %get-tuple-element.24), channel_id=1, source_target_pairs={{0,1},{1,2},{2,3},{3,0},{4,5},{5,6},{6,7},{7,4},{8,9},{9,10},{10,1... | collective-permute-start | bytes 110600 | tf_op jit(solution)/shard_map/ppermute | solution.py:346
  34.6 15.7 %collective-permute-start.3 = (f32[3,12,256]{2,1,0:T(8,128)}, f32[3,12,256]{2,1,0:T(8,128)S(1)}, u32[]{:S(2)}, u32[]{:S(2)}) collective-permute-start(f32[3,12,256]{2,1,0:T(8,128)} %get-tuple-element.25), channel_id=1, source_target_pairs={{1,0},{2,1},{3,2},{0,3},{5,4},{6,5},{7,6},{4,7},{9,8},{10,9},{11,1... | collective-permute-start | bytes 110600 | tf_op jit(solution)/shard_map/ppermute | solution.py:347
  36.4 14.0 %collective-permute-start.5 = (f32[8,24,128]{2,1,0:T(8,128)}, f32[8,24,128]{2,1,0:T(8,128)S(1)}, u32[]{:S(2)}, u32[]{:S(2)}) collective-permute-start(f32[8,24,128]{2,1,0:T(8,128)} %copy-done.1), channel_id=1, source_target_pairs={{4,0},{8,4},{12,8},{16,12},{20,16},{24,20},{28,24},{0,28},{5,1},{9... | collective-permute-start | bytes 294920 | tf_op jit(solution)/shard_map/ppermute | solution.py:313
  41.0 9.3 %copy-start.2 = (f32[3,64,256]{2,1,0:T(8,128)}, f32[3,64,256]{2,1,0:T(8,128)S(1)}, u32[]{:S(2)}) copy-start(f32[3,64,256]{2,1,0:T(8,128)S(1)} %collective-permute-done.x0_ref) | copy-start | bytes 589828
  41.0 9.4 %collective-permute-start.4 = (f32[8,24,128]{2,1,0:T(8,128)}, f32[8,24,128]{2,1,0:T(8,128)S(1)}, u32[]{:S(2)}, u32[]{:S(2)}) collective-permute-start(f32[8,24,128]{2,1,0:T(8,128)} %copy-done.1), channel_id=1, source_target_pairs={{0,4},{4,8},{8,12},{12,16},{16,20},{20,24},{24,28},{28,0},{1,5},{5... | collective-permute-start | bytes 294920 | tf_op jit(solution)/shard_map/ppermute | solution.py:312
  50.3 0.8 %copy-start.3 = (f32[3,64,256]{2,1,0:T(8,128)}, f32[3,64,256]{2,1,0:T(8,128)S(1)}, u32[]{:S(2)}) copy-start(f32[3,64,256]{2,1,0:T(8,128)S(1)} %collective-permute-done.1.x1_ref) | copy-start | bytes 589828
  50.3 0.8 %copy-start.6 = (f32[3,12,256]{2,1,0:T(8,128)}, f32[3,12,256]{2,1,0:T(8,128)S(1)}, u32[]{:S(2)}) copy-start(f32[3,12,256]{2,1,0:T(8,128)S(1)} %collective-permute-done.2.y0_ref) | copy-start | bytes 110596
  50.3 0.8 %copy-start.7 = (f32[3,12,256]{2,1,0:T(8,128)}, f32[3,12,256]{2,1,0:T(8,128)S(1)}, u32[]{:S(2)}) copy-start(f32[3,12,256]{2,1,0:T(8,128)S(1)} %collective-permute-done.3.y1_ref) | copy-start | bytes 110596
  50.4 0.8 %copy-start.4 = (f32[8,24,128]{2,1,0:T(8,128)}, f32[8,24,128]{2,1,0:T(8,128)S(1)}, u32[]{:S(2)}) copy-start(f32[8,24,128]{2,1,0:T(8,128)S(1)} %collective-permute-done.5.right_ref) | copy-start | bytes 294916
  50.4 0.7 %copy-start.5 = (f32[8,24,128]{2,1,0:T(8,128)}, f32[8,24,128]{2,1,0:T(8,128)S(1)}, u32[]{:S(2)}) copy-start(f32[8,24,128]{2,1,0:T(8,128)S(1)} %collective-permute-done.4.left_ref) | copy-start | bytes 294916
  50.4 0.8 %copy-start = (f32[8,3,1024]{2,1,0:T(4,128)}, f32[8,3,1024]{2,1,0:T(4,128)S(1)}, u32[]{:S(2)}) copy-start(f32[8,3,1024]{2,1,0:T(4,128)S(1)} %all-to-all-done.1.given_ref) | copy-start | bytes 294916

commit v3 on v2

v3 whole, which is shorter than its diff:
```python
import functools

import jax
import jax.numpy as jnp
from jax import lax
from jax.experimental import pallas as pl
from jax.experimental.pallas import tpu as pltpu
from jax.sharding import PartitionSpec as P


SLOT_MIN = 12
SPAN = 6
ROWS = 24

diffusion = 0.4


f32 = jnp.float32
bf16 = jnp.bfloat16
i32 = jnp.int32
VMEM = pl.BlockSpec(memory_space=pltpu.VMEM)
HBM = pl.BlockSpec(memory_space=pltpu.HBM)
NN = (((1,), (0,)), ((), ()))
NT = (((1,), (1,)), ((), ()))


def dot(a, b, dims=NN):
    return lax.dot_general(a, b, dims, preferred_element_type=f32)


def halves(x):
    high = x.astype(bf16)
    return high, (x - high.astype(f32)).astype(bf16)


def dot3(ah, al, bh, bl, dims=NN):
    return dot(ah, bh, dims) + dot(ah, bl, dims) + dot(al, bh, dims)


def thirds(x):
    high = x.astype(bf16).astype(f32)
    rest = x - high
    mid = rest.astype(bf16).astype(f32)
    return jnp.concatenate([high, mid, rest - mid], axis=0).astype(bf16)


def one_hot(position, first, slots):
    rows = lax.broadcasted_iota(i32, (slots, position.shape[1]), 0) + first
    return jnp.where(rows == position, 1.0, 0.0).astype(bf16)


def span(index, size):
    return pl.ds(pl.multiple_of(index * size, size), size)


def loop(count, body):
    def step(index, _):
        body(index)

    lax.fori_loop(0, count, step, None)


def pack_kernel(
    capacity, tile, span_y, dest_ref, target_ref, weights_ref, corners_ref, out_ref, pos_ref, rows_ref, column_ref,
):
    owned = target_ref.shape[1]
    dest = dest_ref[...]
    lane = lax.broadcasted_iota(i32, (1, owned), 1)
    first = dest * (span_y * owned)
    key = first + corners_ref[1:2, :] * owned + lane
    column_ref[...] = jnp.transpose(jnp.broadcast_to(key, (8, owned)))

    def count(index, total):
        column = column_ref[span(index, 64), 0:1]
        ahead = jnp.where((column < key) & (column >= first), 1.0, 0.0)
        return total + jnp.sum(ahead, axis=0, keepdims=True)

    rank = lax.fori_loop(0, owned // 64, count, jnp.zeros((1, owned), f32))
    position = dest * capacity + rank.astype(i32)
    pos_ref[...] = position
    rows_ref[0:3, :] = target_ref[...]
    for dim in range(3):
        rows_ref[3 + 6 * dim : 9 + 6 * dim, :] = weights_ref[dim]
    rows_ref[21:24, :] = corners_ref[...].astype(f32)
    data = thirds(rows_ref[...])
    chunked = len(out_ref.shape) == 3

    def move(t):
        moved = dot(data, one_hot(position, t * tile, tile), NT)
        moved = moved[0:ROWS] + moved[ROWS : 2 * ROWS] + moved[2 * ROWS :]
        if chunked:
            per = tile // capacity
            for k in range(per):
                out_ref[t * per + k] = moved[:, k * capacity : (k + 1) * capacity]
        else:
            out_ref[:, span(t, tile)] = moved

    loop(out_ref.size // ROWS // tile, move)


def split_kernel(velocity_ref, high_ref, low_ref, x0_ref, x1_ref):
    _, cells_x, cells_y, cells_z = velocity_ref.shape
    high, low = halves(velocity_ref[0].reshape(cells_x * cells_y, cells_z))
    high_ref[0] = high
    low_ref[0] = low
    x0_ref[0] = velocity_ref[0, 0]
    x1_ref[0] = velocity_ref[0, cells_x - 1]


def window(weights, corner, length):
    offset = lax.broadcasted_iota(i32, (length, weights.shape[1]), 0) - corner
    out = jnp.zeros(offset.shape, f32)
    for k in range(SPAN):
        out = jnp.where(offset == k, weights[k : k + 1, :], out)
    return out


def markers(arrived_ref, t, tile):
    if len(arrived_ref.shape) == 3:
        per = tile // arrived_ref.shape[2]
        return jnp.concatenate([arrived_ref[t * per + k] for k in range(per)], axis=1)
    return arrived_ref[:, span(t, tile)]


def sample_kernel(
    tile, cells_x, arrived_ref, high_hbm, low_hbm, velocity_hbm,
    force_ref, wzh_hbm, wzl_hbm, wy_ref, fx_ref, y0_ref, y1_ref,
    high_ref, low_ref, lower_ref, upper_ref, wzh_ref, wzl_ref, wx_ref, goal_ref, face_ref, in_sem, edge_sem, out_sem,
):
    cells_z = y0_ref.shape[2]
    cells_y, slots = wy_ref.shape
    pad = wx_ref.shape[0]
    count = slots // tile
    loads = [
        pltpu.make_async_copy(high_hbm, high_ref, in_sem.at[0]),
        pltpu.make_async_copy(low_hbm, low_ref, in_sem.at[1]),
        pltpu.make_async_copy(velocity_hbm.at[:, :, pl.ds(0, 8), :], lower_ref, edge_sem.at[0]),
        pltpu.make_async_copy(velocity_hbm.at[:, :, pl.ds(cells_y - 8, 8), :], upper_ref, edge_sem.at[1]),
    ]
    for load in loads:
        load.start()

    def windows(t):
        at = span(t, tile)
        data = markers(arrived_ref, t, tile)
        corner = data[21:24, :].astype(i32)
        for c in range(3):
            goal_ref[c, 0:1, at] = data[c : c + 1]
        wx_ref[:, at] = window(data[3:9], corner[0:1], pad)
        wy_ref[:, at] = window(data[9:15], corner[1:2], cells_y)
        high, low = halves(window(data[15:21], corner[2:3], cells_z))
        wzh_ref[:, at] = high
        wzl_ref[:, at] = low

    loop(count, windows)
    stores = [
        pltpu.make_async_copy(wzh_ref, wzh_hbm, out_sem.at[0]),
        pltpu.make_async_copy(wzl_ref, wzl_hbm, out_sem.at[1]),
    ]
    for store in stores:
        store.start()
    for load in loads:
        load.wait()

    def sample(index):
        c, t = lax.div(index, count), lax.rem(index, count)
        at = span(t, tile)
        along = dot3(high_ref[c], low_ref[c], wzh_ref[:, at], wzl_ref[:, at])
        along = along.reshape(cells_x, cells_y, tile) * wy_ref[:, at][None]
        wx = wx_ref[:, at]
        sampled = jnp.sum(jnp.sum(along, axis=1) * wx[0:cells_x], axis=0, keepdims=True)
        force = goal_ref[c, 0:1, at] - sampled
        fx_ref[c, :, at] = force * wx
        goal_ref[c, 0:1, at] = force

    loop(3 * count, sample)

    def give(k):
        for c in range(3):
            force_ref[k, c : c + 1, :] = goal_ref[c, 0:1, :]

    loop(force_ref.shape[0], give)
    face_ref[...] = jnp.zeros_like(face_ref)

    def edges(t):
        at = span(t, tile)
        wy = wy_ref[:, at]
        rows = [fx_ref[c, :, at] * wy[y : y + 1] for y in (0, cells_y - 1) for c in range(3)]
        high, low = halves(jnp.concatenate(rows, axis=0))
        face_ref[...] += dot3(high, low, wzh_ref[:, at], wzl_ref[:, at], NT)

    loop(count, edges)
    base = 0
    for y, slab_ref, ref in ((0, lower_ref, y0_ref), (7, upper_ref, y1_ref)):
        for c in range(3):
            ref[c] = slab_ref[c, :, y, :] + face_ref[base : base + cells_x]
            base += pad
    for store in stores:
        store.wait()


def spread_kernel(
    tile, velocity_hbm, wzh_ref, wzl_ref, wy_ref, fx_ref, rhs_hbm, boxh_ref, boxl_ref, cell_ref, in_sem, out_sem,
):
    _, cells_x, cells_y, cells_z = velocity_hbm.shape
    count = wy_ref.shape[1] // tile
    load = pltpu.make_async_copy(velocity_hbm, cell_ref, in_sem)
    load.start()
    load.wait()

    def store(c):
        return pltpu.make_async_copy(cell_ref.at[c], rhs_hbm.at[c], out_sem.at[c])

    def spread(index):
        c, t = lax.div(index, count), lax.rem(index, count)
        at = span(t, tile)
        wy = wy_ref[:, at]
        for x in range(cells_x):
            high, low = halves(fx_ref[c, x : x + 1, at] * wy)
            boxh_ref[x * cells_y : (x + 1) * cells_y] = high
            boxl_ref[x * cells_y : (x + 1) * cells_y] = low
        added = dot3(boxh_ref[...], boxl_ref[...], wzh_ref[:, at], wzl_ref[:, at], NT)
        cell_ref[c] += added.reshape(cells_x, cells_y, cells_z)

        @pl.when(t == count - 1)
        def _():
            store(c).start()

    loop(3 * count, spread)
    for c in range(3):
        store(c).wait()


def finish_kernel(
    tile, n_stream, n_wall, chunked,
    rhs_hbm, x0_ref, x1_ref, y0_ref, y1_ref, left_ref, right_ref, given_ref, held_ref, pos_ref,
    next_hbm, force_ref, rhs_ref, next_ref, moved_ref, in_sem, out_sem,
):
    _, cells_x, cells_y, cells_z = rhs_hbm.shape
    slots = given_ref.shape[2]
    count = slots // tile
    loads = [
        pltpu.make_async_copy(rhs_hbm.at[c], rhs_ref.at[c, pl.ds(1, cells_x)], in_sem.at[c]) for c in range(3)
    ]
    for load in loads:
        load.start()
    here = lax.axis_index("gx")
    wall = lax.axis_index("gy")
    for c in range(3):
        rhs_ref[c, 0] = x0_ref[c]
        rhs_ref[c, cells_x + 1] = x1_ref[c]
    before = lax.rem(here + n_stream - 1, n_stream)
    after = lax.rem(here + 1, n_stream)

    def edges(index):
        side, t = lax.div(index, count), lax.rem(index, count)
        at = span(t, tile)
        first = side == 0
        data = jnp.where(first, markers(left_ref, t, tile), markers(right_ref, t, tile))
        corner = data[21:24, :].astype(i32)
        wy = window(data[9:15], corner[1:2], cells_y)
        wzh, wzl = halves(window(data[15:21], corner[2:3], cells_z))
        wx = jnp.where(first, data[8:9], data[3:4])
        wx = jnp.where(corner[0:1] == jnp.where(first, cells_x - SPAN, 0), wx, 0.0)
        force = given_ref[jnp.where(first, before, after), :, at] * wx
        high, low = halves(jnp.concatenate([force[c : c + 1] * wy for c in range(3)], axis=0))
        added = dot3(high, low, wzh, wzl, NT)
        plane = side * (cells_x + 1)
        for c in range(3):
            rhs_ref[c, plane] += added[c * cells_y : (c + 1) * cells_y]

    loop(2 * count, edges)
    y = lax.broadcasted_iota(i32, (cells_y, cells_z), 0)
    lower = jnp.where(wall == 0, 0.0, 1.0).astype(f32)
    upper = jnp.where(wall == n_wall - 1, 0.0, 1.0).astype(f32)
    scale = 1.0 / (1.0 + 6.0 * diffusion)
    for load in loads:
        load.wait()

    def store(c):
        return pltpu.make_async_copy(next_ref.at[c], next_hbm.at[c], out_sem.at[c])

    def stencil(index):
        c, x = lax.div(index, cells_x), lax.rem(index, cells_x)
        cell = rhs_ref[c, x + 1]
        below = jnp.where(y == 0, y0_ref[c, pl.ds(x, 1), :] * lower, pltpu.roll(cell, 1, 0))
        above = jnp.where(y == cells_y - 1, y1_ref[c, pl.ds(x, 1), :] * upper, pltpu.roll(cell, cells_y - 1, 0))
        side = pltpu.roll(cell, 1, 1) + pltpu.roll(cell, cells_z - 1, 1)
        near = (rhs_ref[c, x + 2] + rhs_ref[c, x]) + (above + below) + side
        next_ref[c, x] = (cell + diffusion * near) * scale

        @pl.when(x == cells_x - 1)
        def _():
            store(c).start()

    loop(3 * cells_x, stencil)
    moved_ref[...] = jnp.zeros_like(moved_ref)
    position = pos_ref[...]

    def unpack(t):
        if chunked:
            capacity = slots // n_stream
            per = tile // capacity
            mine = span(here, capacity)
            held = jnp.concatenate([given_ref[t * per + k, :, mine] for k in range(per)], axis=1)
        else:
            held = held_ref[:, span(t, tile)]
        held = jnp.concatenate([held, jnp.zeros((5, tile), f32)], axis=0)
        moved_ref[...] += dot(thirds(held), one_hot(position, t * tile, tile))

    loop(count, unpack)
    force_ref[...] = (moved_ref[0:8] + moved_ref[8:16] + moved_ref[16:24])[0:3]
    for c in range(3):
        store(c).wait()


def per_device(velocity, target, weights, corners, dest):
    n_stream = lax.axis_size("gx")
    n_wall = lax.axis_size("gy")
    owned = target.shape[1]
    capacity = max(SLOT_MIN, 2 * owned // n_stream)
    slots = n_stream * capacity
    _, cells_x, cells_y, cells_z = velocity.shape
    block = cells_x * cells_y
    chunked = capacity % 128 == 0
    tile = 256 if slots % 256 == 0 else 128
    shape = jax.ShapeDtypeStruct
    sems = pltpu.SemaphoreType.DMA

    outgoing, position = pl.pallas_call(
        functools.partial(pack_kernel, capacity, tile, cells_y),
        out_shape=(
            shape((n_stream, ROWS, capacity) if chunked else (ROWS, slots), f32),
            shape((1, owned), i32),
        ),
        in_specs=[VMEM] * 4,
        out_specs=(VMEM, VMEM),
        scratch_shapes=[pltpu.VMEM((ROWS, owned), f32), pltpu.VMEM((owned, 8), i32)],
        name="pack",
    )(dest.reshape(1, owned), target, weights, corners)
    if chunked:
        arrived = lax.all_to_all(outgoing, "gx", split_axis=0, concat_axis=0, tiled=True)
    else:
        outgoing = outgoing.reshape(ROWS, n_stream, capacity)
        arrived = lax.all_to_all(outgoing, "gx", split_axis=1, concat_axis=1, tiled=True)
        arrived = arrived.reshape(ROWS, slots)

    high, low, x0, x1 = pl.pallas_call(
        split_kernel,
        grid=(3,),
        out_shape=(
            shape((3, block, cells_z), bf16),
            shape((3, block, cells_z), bf16),
            shape((3, cells_y, cells_z), f32),
            shape((3, cells_y, cells_z), f32),
        ),
        in_specs=[pl.BlockSpec((1, cells_x, cells_y, cells_z), lambda c: (c, 0, 0, 0))],
        out_specs=(
            pl.BlockSpec((1, block, cells_z), lambda c: (c, 0, 0)),
            pl.BlockSpec((1, block, cells_z), lambda c: (c, 0, 0)),
            pl.BlockSpec((1, cells_y, cells_z), lambda c: (c, 0, 0)),
            pl.BlockSpec((1, cells_y, cells_z), lambda c: (c, 0, 0)),
        ),
        name="split",
    )(velocity)

    up_x = [(i, (i + 1) % n_stream) for i in range(n_stream)]
    down_x = [(j, i) for i, j in up_x]
    up_y = [(i, (i + 1) % n_wall) for i in range(n_wall)]
    down_y = [(j, i) for i, j in up_y]
    from_x0 = lax.ppermute(x1, "gx", up_x)
    from_x1 = lax.ppermute(x0, "gx", down_x)
    left = lax.ppermute(arrived, "gx", up_x)
    right = lax.ppermute(arrived, "gx", down_x)

    pad = -(-cells_x // 16) * 16
    force, wzh, wzl, wy, fx, y0, y1 = pl.pallas_call(
        functools.partial(sample_kernel, tile, cells_x),
        out_shape=(
            shape((n_stream, 3, slots), f32),
            shape((cells_z, slots), bf16),
            shape((cells_z, slots), bf16),
            shape((cells_y, slots), f32),
            shape((3, pad, slots), f32),
            shape((3, cells_x, cells_z), f32),
            shape((3, cells_x, cells_z), f32),
        ),
        in_specs=[VMEM, HBM, HBM, HBM],
        out_specs=(VMEM, HBM, HBM, VMEM, VMEM, VMEM, VMEM),
        scratch_shapes=[
            pltpu.VMEM((3, block, cells_z), bf16),
            pltpu.VMEM((3, block, cells_z), bf16),
            pltpu.VMEM((3, cells_x, 8, cells_z), f32),
            pltpu.VMEM((3, cells_x, 8, cells_z), f32),
            pltpu.VMEM((cells_z, slots), bf16),
            pltpu.VMEM((cells_z, slots), bf16),
            pltpu.VMEM((pad, slots), f32),
            pltpu.VMEM((3, 8, slots), f32),
            pltpu.VMEM((6 * pad, cells_z), f32),
            sems((2,)),
            sems((2,)),
            sems((2,)),
        ],
        compiler_params=pltpu.CompilerParams(vmem_limit_bytes=63_280_000),
        name="sample",
    )(arrived, high, low, velocity)

    from_y0 = lax.ppermute(y1, "gy", up_y)
    from_y1 = lax.ppermute(y0, "gy", down_y)
    given = lax.all_to_all(force, "gx", split_axis=0, concat_axis=0, tiled=True)
    if chunked:
        held = position
    else:
        held = lax.dynamic_slice_in_dim(given, lax.axis_index("gx") * capacity, capacity, axis=2)
        held = held.transpose(1, 0, 2).reshape(3, slots)

    rhs = pl.pallas_call(
        functools.partial(spread_kernel, tile),
        out_shape=shape(velocity.shape, f32),
        in_specs=[HBM, VMEM, VMEM, VMEM, VMEM],
        out_specs=HBM,
        scratch_shapes=[
            pltpu.VMEM((block, tile), bf16),
            pltpu.VMEM((block, tile), bf16),
            pltpu.VMEM(velocity.shape, f32),
            sems(()),
            sems((3,)),
        ],
        cost_estimate=pl.CostEstimate(flops=18 * block * slots * cells_z, bytes_accessed=24 * block * cells_z, transcendentals=0),
        name="spread",
    )(velocity, wzh, wzl, wy, fx)

    return pl.pallas_call(
        functools.partial(finish_kernel, tile, n_stream, n_wall, chunked),
        out_shape=(shape(velocity.shape, f32), shape((3, owned), f32)),
        in_specs=[HBM] + [VMEM] * 9,
        out_specs=(HBM, VMEM),
        scratch_shapes=[
            pltpu.VMEM((3, cells_x + 2, cells_y, cells_z), f32),
            pltpu.VMEM(velocity.shape, f32),
            pltpu.VMEM((24, owned), f32),
            sems((3,)),
            sems((3,)),
        ],
        compiler_params=pltpu.CompilerParams(vmem_limit_bytes=62_400_000),
        name="finish",
    )(rhs, from_x0, from_x1, from_y0, from_y1, left, right, given, held, position)


def solution(mesh):
    in_specs = (
        P(None, "gx", "gy", None),
        P(None, ("gx", "gy")),
        P(None, None, ("gx", "gy")),
        P(None, ("gx", "gy")),
        P(("gx", "gy"), None),
    )
    out_specs = (P(None, "gx", "gy", None), P(None, ("gx", "gy")))
    return jax.shard_map(
        per_device, mesh=mesh, in_specs=in_specs, out_specs=out_specs, check_vma=False
    )
```

time: 58.6 us -> 66.7 us (1.14)
  Pallas kernels: 30.8 us -> 39 us
    pallas_call x3, Pallas kernels: 20.1 us -> 24.7 us  [the longest x1 11.2 us: per_device(): pl.pallas_call(functools.partial(sample_kernel, tile, cells_x), out_shape...]
    pallas_call x1, Pallas kernels: 6.75 us -> 10.3 us  [per_device(): pl.pallas_call(functools.partial(finish_kernel, tile, n_stream, n_wall, c...]
    unnamed x16, local copies, waits for them, and re-layouts: 0.74 us -> 1.44 us
    broadcast_in_dim x1 -> x0, local copies, waits for them, and re-layouts: 0.7 us -> none  [per_device(): held = jnp.zeros((8, 128), f32)]
  transfers between devices with their start and end apart: 8 -> 8, of which waited for: 1 -> 1; matrix products, arithmetic and copies ran while one was open for 0% -> 0% of each run, Pallas kernels for 35% -> 37%
where the time goes in v3:
time: 66.7 us; the launch traced here: 66.1 us
  Pallas kernels  39 us (58%)
  starting transfers between devices  22.4 us (34%)
  waiting for transfers between devices  2.52 us (4%)
  local copies, waits for them, and re-layouts  1.44 us (2%)
  between operations  0.78 us (1%)
    pallas_call x1, Pallas kernels, per_device(): pl.pallas_call(functools.partial(sample_kernel, tile, cells_x), out_shape...  11.2 us
    pallas_call x1, Pallas kernels, per_device(): pl.pallas_call(functools.partial(finish_kernel, tile, n_stream, n_wall, c...  10.3 us
    pallas_call x1, Pallas kernels, per_device(): pl.pallas_call(functools.partial(spread_kernel, tile), out_shape=shape(ve...  10.2 us
    all_to_all x1, starting transfers between devices, per_device(): lax.all_to_all(outgoing, 'gx', split_axis=0, concat_axis=0, tiled=True)  4.88 us
    ppermute x1, starting transfers between devices, per_device(): from_x1 = lax.ppermute(x0, 'gx', down_x)  4.72 us
    ppermute x1, starting transfers between devices, per_device(): right = lax.ppermute(arrived, 'gx', down_x)  4.61 us
    pallas_call x1, Pallas kernels, per_device(): pl.pallas_call(split_kernel, grid=(3,), out_shape=(shape((3, block, cells...  3.99 us
    all_to_all x1, starting transfers between devices, per_device(): given = lax.all_to_all(force, 'gx', split_axis=0, concat_axis=0, tiled=True)  3.38 us
  transfers between devices with their start and end apart: 8, of which 1 were waited for; matrix products, arithmetic and copies ran while one was open for 0% of the time, Pallas kernels for 37%

profile of v3, /device:TPU:0, one launch (start us, length us, event | category | flops | bytes accessed | tf_op | source)
XLA Modules:
  0.0 66.1 jit_solution(15907567611694963843)
XLA Ops:
  0.6 4.0 %split.1 = (bf16[3,768,256]{2,1,0:T(8,128)(2,1)}, bf16[3,768,256]{2,1,0:T(8,128)(2,1)}, f32[3,64,256]{2,1,0:T(8,128)}, f32[3,64,256]{2,1,0:T(8,128)}) custom-call(f32[3,12,64,256]{3,2,1,0:T(8,128)} %velocity_hbm.3), custom_call_target="tpu_custom_call" | custom-call | tf_op jit(solution)/shard_map/split/pallas_call | solution.py:348
  4.6 3.0 %collective-permute-start = (f32[3,64,256]{2,1,0:T(8,128)}, f32[3,64,256]{2,1,0:T(8,128)S(1)}, u32[]{:S(2)}, u32[]{:S(2)}) collective-permute-start(f32[3,64,256]{2,1,0:T(8,128)} %get-tuple-element.22), channel_id=1, source_target_pairs={{0,4},{4,8},{8,12},{12,16},{16,20},{20,24},{24,28},{28,0},{1,5},{5... | collective-permute-start | bytes 589832 | tf_op jit(solution)/shard_map/ppermute | solution.py:371
  7.6 3.3 %pack.1 = (f32[8,24,128]{2,1,0:T(8,128)}, s32[1,512]{1,0:T(1,128)}) custom-call(s32[1,512]{1,0:T(1,128)} %bitcast.1, f32[3,512]{1,0:T(4,128)} %target_ref.1, f32[3,6,512]{2,1,0:T(8,128)} %weights_ref.1, s32[3,512]{1,0:T(4,128)} %corners_ref.1), custom_call_target="tpu_custom_call" | custom-call | tf_op jit(solution)/shard_map/pack/pallas_call | solution.py:330
  10.9 4.9 %all-to-all-start = ((f32[8,24,128]{2,1,0:T(8,128)}), f32[8,24,128]{2,1,0:T(8,128)S(1)}, u32[]{:S(2)}, u32[]{:S(2)}) async-start(f32[8,24,128]{2,1,0:T(8,128)} %get-tuple-element.15), calls=%async_computation | async-start | bytes 196608 | tf_op jit(solution)/shard_map/all_to_all | solution.py:342
  15.8 4.7 %collective-permute-start.1 = (f32[3,64,256]{2,1,0:T(8,128)}, f32[3,64,256]{2,1,0:T(8,128)S(1)}, u32[]{:S(2)}, u32[]{:S(2)}) collective-permute-start(f32[3,64,256]{2,1,0:T(8,128)} %get-tuple-element.23), channel_id=1, source_target_pairs={{4,0},{8,4},{12,8},{16,12},{20,16},{24,20},{28,24},{0,28},{5,1},{9... | collective-permute-start | bytes 589832 | tf_op jit(solution)/shard_map/ppermute | solution.py:372
  20.5 2.5 %all-to-all-done.arrived_ref = f32[8,24,128]{2,1,0:T(8,128)S(1)} async-done(((f32[8,24,128]{2,1,0:T(8,128)}), f32[8,24,128]{2,1,0:T(8,128)S(1)}, u32[]{:S(2)}, u32[]{:S(2)}) %all-to-all-start) | async-done | bytes 98336 | tf_op jit(solution)/shard_map/all_to_all | solution.py:342
  23.0 0.0 copy-start.1
  23.0 0.6 copy-done.1
  23.7 11.2 %sample.1 = (f32[8,3,1024]{2,1,0:T(4,128)}, bf16[256,1024]{1,0:T(8,128)(2,1)}, bf16[256,1024]{1,0:T(8,128)(2,1)}, f32[64,1024]{1,0:T(8,128)}, f32[3,16,1024]{2,1...) custom-call(f32[8,24,128]{2,1,0:T(8,128)} %copy-done.1, bf16[3,768,256]{2,1,0:T(8,128)(2,1)} %get-tuple-element.16.high_hbm, ...), custom_call_target="tpu_custom_call" | custom-call | tf_op jit(solution)/shard_map/sample/pallas_call | solution.py:377
  34.9 3.4 %all-to-all-start.1 = ((f32[8,3,1024]{2,1,0:T(4,128)}), f32[8,3,1024]{2,1,0:T(4,128)S(1)}, u32[]{:S(2)}, u32[]{:S(2)}) async-start(f32[8,3,1024]{2,1,0:T(4,128)} %get-tuple-element.26), calls=%async_computation.1 | async-start | bytes 262144 | tf_op jit(solution)/shard_map/all_to_all | solution.py:410
  38.3 0.1 collective-permute-start.2
  38.4 1.7 %collective-permute-start.3 = (f32[3,12,256]{2,1,0:T(8,128)}, f32[3,12,256]{2,1,0:T(8,128)S(1)}, u32[]{:S(2)}, u32[]{:S(2)}) collective-permute-start(f32[3,12,256]{2,1,0:T(8,128)} %get-tuple-element.25), channel_id=1, source_target_pairs={{1,0},{2,1},{3,2},{0,3},{5,4},{6,5},{7,6},{4,7},{9,8},{10,9},{11,1... | collective-permute-start | bytes 110600 | tf_op jit(solution)/shard_map/ppermute | solution.py:409
  40.1 4.6 %collective-permute-start.5 = (f32[8,24,128]{2,1,0:T(8,128)}, f32[8,24,128]{2,1,0:T(8,128)S(1)}, u32[]{:S(2)}, u32[]{:S(2)}) collective-permute-start(f32[8,24,128]{2,1,0:T(8,128)} %copy-done.1), channel_id=1, source_target_pairs={{4,0},{8,4},{12,8},{16,12},{20,16},{24,20},{28,24},{0,28},{5,1},{9... | collective-permute-start | bytes 294920 | tf_op jit(solution)/shard_map/ppermute | solution.py:374
  44.7 0.0 collective-permute-done.x0_ref
  44.7 0.0 copy-start.2
  44.7 0.0 collective-permute-start.4
  44.7 10.2 %spread.1.rhs_hbm = f32[3,12,64,256]{3,2,1,0:T(8,128)} custom-call(f32[3,12,64,256]{3,2,1,0:T(8,128)} %velocity_hbm.3, bf16[256,1024]{1,0:T(8,128)(2,1)} %get-tuple-element.18.wzh_ref, bf16[256,1024]{1,0:T(8,128)(2,1)} %get-tuple-element.19.wzl_ref, f32[64,1024]{1,0:T(8,128)} %get-tuple-element.20.wy_ref, f32[3,16,1024]{2,1,0:T(8,128)} %get-tuple-element.21.fx_ref), custom_call_target="tpu_custom_call" | custom-call | flops 3623878656 | bytes 4718592 | tf_op jit(solution)/shard_map/spread/pallas_call | solution.py:417
  54.9 0.0 copy-done.2
  54.9 0.0 collective-permute-done.1.x1_ref
  54.9 0.0 copy-start.3
  54.9 0.0 collective-permute-done.2.y0_ref
  54.9 0.0 copy-start.6
  55.0 0.0 collective-permute-done.3.y1_ref
  55.0 0.0 copy-start.7
  55.0 0.0 collective-permute-done.5.right_ref
  55.0 0.0 copy-start.4
  55.0 0.0 collective-permute-done.4.left_ref
  55.0 0.0 copy-start.5
  55.0 0.0 all-to-all-done.1.given_ref
  55.0 0.0 copy-start
  55.0 0.6 copy-done.3
  55.6 0.0 copy-done.6
  55.6 0.0 copy-done.7
  55.7 0.0 copy-done.4
  55.7 0.0 copy-done.5
  55.7 0.1 copy-done
  55.8 10.3 %finish.1 = (f32[3,12,64,256]{3,2,1,0:T(8,128)}, f32[3,512]{1,0:T(4,128)}) custom-call(f32[3,12,64,256]{3,2,1,0:T(8,128)} %spread.1.rhs_hbm, f32[3,64,256]{2,1,0:T(8,128)} %copy-done.2, f32[3,64,256]{2,1,0:T(8,128)} %copy-done.3, f32[3,12,256]{2,1,0:T(8,128)} %copy-done.6, f32[3,12,256]{2,1,0:T(8,128)} %copy-done.7, f32[8,24,128]{2,1,0:T(8,128)} %copy-done.5, ...), custom_call_target="tpu_custom_call" | custom-call | tf_op jit(solution)/shard_map/finish/pallas_call | solution.py:433
Async XLA Ops:
  4.6 40.1 %collective-permute-start = (f32[3,64,256]{2,1,0:T(8,128)}, f32[3,64,256]{2,1,0:T(8,128)S(1)}, u32[]{:S(2)}, u32[]{:S(2)}) collective-permute-start(f32[3,64,256]{2,1,0:T(8,128)} %get-tuple-element.22), channel_id=1, source_target_pairs={{0,4},{4,8},{8,12},{12,16},{16,20},{20,24},{24,28},{28,0},{1,5},{5... | collective-permute-start | bytes 589832 | tf_op jit(solution)/shard_map/ppermute | solution.py:371
  10.9 12.1 %all-to-all-start = ((f32[8,24,128]{2,1,0:T(8,128)}), f32[8,24,128]{2,1,0:T(8,128)S(1)}, u32[]{:S(2)}, u32[]{:S(2)}) async-start(f32[8,24,128]{2,1,0:T(8,128)} %get-tuple-element.15), calls=%async_computation | async-start | bytes 196608 | tf_op jit(solution)/shard_map/all_to_all | solution.py:342
  15.8 39.1 %collective-permute-start.1 = (f32[3,64,256]{2,1,0:T(8,128)}, f32[3,64,256]{2,1,0:T(8,128)S(1)}, u32[]{:S(2)}, u32[]{:S(2)}) collective-permute-start(f32[3,64,256]{2,1,0:T(8,128)} %get-tuple-element.23), channel_id=1, source_target_pairs={{4,0},{8,4},{12,8},{16,12},{20,16},{24,20},{28,24},{0,28},{5,1},{9... | collective-permute-start | bytes 589832 | tf_op jit(solution)/shard_map/ppermute | solution.py:372
  23.0 0.7 copy-start.1
  34.9 20.1 %all-to-all-start.1 = ((f32[8,3,1024]{2,1,0:T(4,128)}), f32[8,3,1024]{2,1,0:T(4,128)S(1)}, u32[]{:S(2)}, u32[]{:S(2)}) async-start(f32[8,3,1024]{2,1,0:T(4,128)} %get-tuple-element.26), calls=%async_computation.1 | async-start | bytes 262144 | tf_op jit(solution)/shard_map/all_to_all | solution.py:410
  38.3 16.6 %collective-permute-start.2 = (f32[3,12,256]{2,1,0:T(8,128)}, f32[3,12,256]{2,1,0:T(8,128)S(1)}, u32[]{:S(2)}, u32[]{:S(2)}) collective-permute-start(f32[3,12,256]{2,1,0:T(8,128)} %get-tuple-element.24), channel_id=1, source_target_pairs={{0,1},{1,2},{2,3},{3,0},{4,5},{5,6},{6,7},{7,4},{8,9},{9,10},{10,1... | collective-permute-start | bytes 110600 | tf_op jit(solution)/shard_map/ppermute | solution.py:408
  38.4 16.6 %collective-permute-start.3 = (f32[3,12,256]{2,1,0:T(8,128)}, f32[3,12,256]{2,1,0:T(8,128)S(1)}, u32[]{:S(2)}, u32[]{:S(2)}) collective-permute-start(f32[3,12,256]{2,1,0:T(8,128)} %get-tuple-element.25), channel_id=1, source_target_pairs={{1,0},{2,1},{3,2},{0,3},{5,4},{6,5},{7,6},{4,7},{9,8},{10,9},{11,1... | collective-permute-start | bytes 110600 | tf_op jit(solution)/shard_map/ppermute | solution.py:409
  40.1 14.9 %collective-permute-start.5 = (f32[8,24,128]{2,1,0:T(8,128)}, f32[8,24,128]{2,1,0:T(8,128)S(1)}, u32[]{:S(2)}, u32[]{:S(2)}) collective-permute-start(f32[8,24,128]{2,1,0:T(8,128)} %copy-done.1), channel_id=1, source_target_pairs={{4,0},{8,4},{12,8},{16,12},{20,16},{24,20},{28,24},{0,28},{5,1},{9... | collective-permute-start | bytes 294920 | tf_op jit(solution)/shard_map/ppermute | solution.py:374
  44.7 10.2 %copy-start.2 = (f32[3,64,256]{2,1,0:T(8,128)}, f32[3,64,256]{2,1,0:T(8,128)S(1)}, u32[]{:S(2)}) copy-start(f32[3,64,256]{2,1,0:T(8,128)S(1)} %collective-permute-done.x0_ref) | copy-start | bytes 589828
  44.7 10.3 %collective-permute-start.4 = (f32[8,24,128]{2,1,0:T(8,128)}, f32[8,24,128]{2,1,0:T(8,128)S(1)}, u32[]{:S(2)}, u32[]{:S(2)}) collective-permute-start(f32[8,24,128]{2,1,0:T(8,128)} %copy-done.1), channel_id=1, source_target_pairs={{0,4},{4,8},{8,12},{12,16},{16,20},{20,24},{24,28},{28,0},{1,5},{5... | collective-permute-start | bytes 294920 | tf_op jit(solution)/shard_map/ppermute | solution.py:373
  54.9 0.7 %copy-start.3 = (f32[3,64,256]{2,1,0:T(8,128)}, f32[3,64,256]{2,1,0:T(8,128)S(1)}, u32[]{:S(2)}) copy-start(f32[3,64,256]{2,1,0:T(8,128)S(1)} %collective-permute-done.1.x1_ref) | copy-start | bytes 589828
  54.9 0.7 %copy-start.6 = (f32[3,12,256]{2,1,0:T(8,128)}, f32[3,12,256]{2,1,0:T(8,128)S(1)}, u32[]{:S(2)}) copy-start(f32[3,12,256]{2,1,0:T(8,128)S(1)} %collective-permute-done.2.y0_ref) | copy-start | bytes 110596
  55.0 0.7 %copy-start.7 = (f32[3,12,256]{2,1,0:T(8,128)}, f32[3,12,256]{2,1,0:T(8,128)S(1)}, u32[]{:S(2)}) copy-start(f32[3,12,256]{2,1,0:T(8,128)S(1)} %collective-permute-done.3.y1_ref) | copy-start | bytes 110596
  55.0 0.7 %copy-start.4 = (f32[8,24,128]{2,1,0:T(8,128)}, f32[8,24,128]{2,1,0:T(8,128)S(1)}, u32[]{:S(2)}) copy-start(f32[8,24,128]{2,1,0:T(8,128)S(1)} %collective-permute-done.5.right_ref) | copy-start | bytes 294916
  55.0 0.7 %copy-start.5 = (f32[8,24,128]{2,1,0:T(8,128)}, f32[8,24,128]{2,1,0:T(8,128)S(1)}, u32[]{:S(2)}) copy-start(f32[8,24,128]{2,1,0:T(8,128)S(1)} %collective-permute-done.4.left_ref) | copy-start | bytes 294916
  55.0 0.8 %copy-start = (f32[8,3,1024]{2,1,0:T(4,128)}, f32[8,3,1024]{2,1,0:T(4,128)S(1)}, u32[]{:S(2)}) copy-start(f32[8,3,1024]{2,1,0:T(4,128)S(1)} %all-to-all-done.1.given_ref) | copy-start | bytes 294916

commit v4 on v2

--- a/solution.py
+++ b/solution.py
@@ -49,15 +49,33 @@
     return jnp.where(rows == position, 1.0, 0.0).astype(bf16)
 
 
-def pack_kernel(capacity, chunked, span_y, dest_ref, target_ref, weights_ref, corners_ref, out_ref, pos_ref, rows_ref):
+def span(index, size):
+    return pl.ds(pl.multiple_of(index * size, size), size)
+
+
+def pack_kernel(
+    capacity, chunked, dest_ref, target_ref, weights_ref, corners_ref, velocity_hbm,
+    out_ref, pos_ref, x0_hbm, x1_hbm, rows_ref, sem,
+):
     owned = target_ref.shape[1]
+    cells_x = velocity_hbm.shape[1]
+    faces = [
+        pltpu.make_async_copy(velocity_hbm.at[:, 0], x0_hbm, sem.at[0]),
+        pltpu.make_async_copy(velocity_hbm.at[:, cells_x - 1], x1_hbm, sem.at[1]),
+    ]
+    for face in faces:
+        face.start()
     dest = dest_ref[...]
+    corner = corners_ref[0:1, :]
     lane = lax.broadcasted_iota(i32, (1, owned), 1)
-    first = dest * (span_y * owned)
-    key = first + corners_ref[1:2, :] * owned + lane
+    last = corner == cells_x - SPAN
+    group = jnp.where(last, 2, jnp.where(corner == 0, 0, 1))
+    first = (dest * 4 + jnp.where(last, 2, 0)) * owned
+    key = (dest * 4 + group) * owned + lane
     column = jnp.transpose(jnp.broadcast_to(key, (8, owned)))[:, 0:1]
     ahead = jnp.where((column < key) & (column >= first), 1.0, 0.0)
-    position = dest * capacity + jnp.sum(ahead, axis=0, keepdims=True).astype(i32)
+    rank = jnp.sum(ahead, axis=0, keepdims=True).astype(i32)
+    position = dest * capacity + jnp.where(last, capacity - 1 - rank, rank)
     pos_ref[...] = position
     rows_ref[0:3, :] = target_ref[...]
     for dim in range(3):
@@ -71,15 +89,15 @@
             out_ref[chunk] = moved[:, chunk * capacity : (chunk + 1) * capacity]
     else:
         out_ref[...] = moved
-
-
-def split_kernel(velocity_ref, high_ref, low_ref, x0_ref, x1_ref):
+    for face in faces:
+        face.wait()
+
+
+def split_kernel(velocity_ref, high_ref, low_ref):
     _, cells_x, cells_y, cells_z = velocity_ref.shape
     high, low = halves(velocity_ref[0].reshape(cells_x * cells_y, cells_z))
     high_ref[0] = high
     low_ref[0] = low
-    x0_ref[0] = velocity_ref[0, 0]
-    x1_ref[0] = velocity_ref[0, cells_x - 1]
 
 
 def window(weights, corner, length):
@@ -191,10 +209,24 @@
         store.wait()
 
 
+def quarter(marks_ref, side, index, width):
+    lane = lax.broadcasted_iota(i32, marks_ref.shape[2:], 1)
+    capacity = marks_ref.shape[3]
+    per = capacity // width
+    out = []
+    for base in range(0, marks_ref.shape[1], per):
+        piece = jnp.zeros(marks_ref.shape[2:], f32)
+        for k in range(per):
+            moved = pltpu.roll(marks_ref[side, base + k], lax.rem(capacity + (k - index) * width, capacity), 1)
+            piece = jnp.where((lane >= k * width) & (lane < (k + 1) * width), moved, piece)
+        out.append(piece)
+    return jnp.concatenate(out, axis=1)
+
+
 def finish_kernel(
-    tile, n_stream, n_wall, chunked,
+    tile, n_stream, n_wall, chunked, quartered,
     rhs_hbm, x0_ref, x1_ref, y0_ref, y1_ref, left_ref, right_ref, given_ref, held_ref, pos_ref,
-    next_hbm, force_ref, rhs_ref, next_ref, face_ref, wzh_ref, wzl_ref, boxh_ref, boxl_ref, in_sem, out_sem,
+    next_hbm, force_ref, rhs_ref, next_ref, face_ref, marks_ref, in_sem, out_sem,
 ):
     _, cells_x, cells_y, cells_z = rhs_hbm.shape
     slots = given_ref.shape[2]
@@ -209,20 +241,38 @@
         (1, right_ref, x1_ref, 0, 0, lax.rem(here + 1, n_stream)),
     )
     for side, arrived_ref, plane_ref, touching, row, owner in sides:
-        for at, data in tiles_of(arrived_ref, tile, slots):
+        face_ref[side] = plane_ref[...]
+
+        def add(data, force):
             corner = data[21:24, :].astype(i32)
             wy = window(data[9:15], corner[1:2], cells_y)
-            high, low = halves(window(data[15:21], corner[2:3], cells_z))
-            wzh_ref[:, at] = high
-            wzl_ref[:, at] = low
+            wzh, wzl = halves(window(data[15:21], corner[2:3], cells_z))
             wx = jnp.where(corner[0:1] == touching, data[3 + row : 4 + row], 0.0)
-            force = given_ref[owner, :, at] * wx
-            for c in range(3):
-                high, low = halves(force[c : c + 1] * wy)
-                boxh_ref[c * cells_y : (c + 1) * cells_y, at] = high
-                boxl_ref[c * cells_y : (c + 1) * cells_y, at] = low
-        spread = dot3(boxh_ref[...], boxl_ref[...], wzh_ref[...], wzl_ref[...], NT)
-        face_ref[side] = plane_ref[...] + spread.reshape(3, cells_y, cells_z)
+            force = force * wx
+            high, low = halves(jnp.concatenate([force[c : c + 1] * wy for c in range(3)], axis=0))
+            face_ref[side] += dot3(high, low, wzh, wzl, NT).reshape(3, cells_y, cells_z)
+
+        if quartered:
+            capacity = slots // n_stream
+            width = tile // n_stream
+            for k in range(n_stream):
+                marks_ref[side, k] = arrived_ref[k]
+                marks_ref[side, k, 0:3] = given_ref[owner, :, k * capacity : (k + 1) * capacity]
+            held = marks_ref[side]
+            touches = (held[:, 21, :] == float(touching)) & (held[:, 3, :] != 0.0)
+            lane = lax.broadcasted_iota(i32, touches.shape, 1)
+            depth = lane + 1 if side else capacity - lane
+            reach = jnp.max(jnp.where(touches, depth.astype(f32), 0.0)).astype(i32)
+            per = capacity // width
+
+            def step(index, _):
+                data = quarter(marks_ref, side, index if side else per - 1 - index, width)
+                add(data, data[0:3])
+
+            lax.fori_loop(0, lax.div(reach + width - 1, width), step, None)
+        else:
+            for at, data in tiles_of(arrived_ref, tile, slots):
+                add(data, given_ref[owner, :, at])
     y = lax.broadcasted_iota(i32, (cells_y, cells_z), 0)
     lower = jnp.where(wall == 0, 0.0, 1.0).astype(f32)
     upper = jnp.where(wall == n_wall - 1, 0.0, 1.0).astype(f32)
@@ -241,7 +291,7 @@
         stores[c].start()
     if chunked:
         capacity = slots // n_stream
-        mine = pl.ds(pl.multiple_of(here * capacity, capacity), capacity)
+        mine = span(here, capacity)
         held = jnp.concatenate([given_ref[k, :, mine] for k in range(n_stream)], axis=1)
     else:
         held = held_ref[...]
@@ -263,20 +313,24 @@
     block = cells_x * cells_y
     chunked = capacity % 128 == 0
     tile = 256 if slots % 256 == 0 else 128
+    quartered = capacity == 128 and tile % n_stream == 0 and capacity % (tile // n_stream) == 0
     shape = jax.ShapeDtypeStruct
     sems = pltpu.SemaphoreType.DMA
 
-    outgoing, position = pl.pallas_call(
-        functools.partial(pack_kernel, capacity, chunked, cells_y),
+    face_x = shape((3, cells_y, cells_z), f32)
+    outgoing, position, x0, x1 = pl.pallas_call(
+        functools.partial(pack_kernel, capacity, chunked),
         out_shape=(
             shape((n_stream, ROWS, capacity) if chunked else (ROWS, slots), f32),
             shape((1, owned), i32),
+            face_x,
+            face_x,
         ),
-        in_specs=[VMEM] * 4,
-        out_specs=(VMEM, VMEM),
-        scratch_shapes=[pltpu.VMEM((ROWS, owned), f32)],
+        in_specs=[VMEM] * 4 + [HBM],
+        out_specs=(VMEM, VMEM, HBM, HBM),
+        scratch_shapes=[pltpu.VMEM((ROWS, owned), f32), sems((2,))],
         name="pack",
-    )(dest.reshape(1, owned), target, weights, corners)
+    )(dest.reshape(1, owned), target, weights, corners, velocity)
     if chunked:
         arrived = lax.all_to_all(outgoing, "gx", split_axis=0, concat_axis=0, tiled=True)
     else:
@@ -284,22 +338,12 @@
         arrived = lax.all_to_all(outgoing, "gx", split_axis=1, concat_axis=1, tiled=True)
         arrived = arrived.reshape(ROWS, slots)
 
-    high, low, x0, x1 = pl.pallas_call(
+    high, low = pl.pallas_call(
         split_kernel,
         grid=(3,),
-        out_shape=(
-            shape((3, block, cells_z), bf16),
-            shape((3, block, cells_z), bf16),
-            shape((3, cells_y, cells_z), f32),
-            shape((3, cells_y, cells_z), f32),
-        ),
+        out_shape=(shape((3, block, cells_z), bf16),) * 2,
         in_specs=[pl.BlockSpec((1, cells_x, cells_y, cells_z), lambda c: (c, 0, 0, 0))],
-        out_specs=(
-            pl.BlockSpec((1, block, cells_z), lambda c: (c, 0, 0)),
-            pl.BlockSpec((1, block, cells_z), lambda c: (c, 0, 0)),
-            pl.BlockSpec((1, cells_y, cells_z), lambda c: (c, 0, 0)),
-            pl.BlockSpec((1, cells_y, cells_z), lambda c: (c, 0, 0)),
-        ),
+        out_specs=(pl.BlockSpec((1, block, cells_z), lambda c: (c, 0, 0)),) * 2,
         name="split",
     )(velocity)
 
@@ -347,7 +391,7 @@
     from_y1 = lax.ppermute(y0, "gy", down_y)
     given = lax.all_to_all(force, "gx", split_axis=0, concat_axis=0, tiled=True)
     if chunked:
-        held = jnp.zeros((8, 128), f32)
+        held = position
     else:
         held = lax.dynamic_slice_in_dim(given, lax.axis_index("gx") * capacity, capacity, axis=2)
         held = held.transpose(1, 0, 2).reshape(3, slots)
@@ -369,7 +413,7 @@
     )(velocity, wzh, wzl, wy, fx)
 
     return pl.pallas_call(
-        functools.partial(finish_kernel, tile, n_stream, n_wall, chunked),
+        functools.partial(finish_kernel, tile, n_stream, n_wall, chunked, quartered),
         out_shape=(shape(velocity.shape, f32), shape((3, owned), f32)),
         in_specs=[HBM] + [VMEM] * 9,
         out_specs=(HBM, VMEM),
@@ -377,10 +421,7 @@
             pltpu.VMEM(velocity.shape, f32),
             pltpu.VMEM(velocity.shape, f32),
             pltpu.VMEM((2, 3, cells_y, cells_z), f32),
-            pltpu.VMEM((cells_z, slots), bf16),
-            pltpu.VMEM((cells_z, slots), bf16),
-            pltpu.VMEM((3 * cells_y, slots), bf16),
-            pltpu.VMEM((3 * cells_y, slots), bf16),
+            pltpu.VMEM((2, n_stream, ROWS, 128), f32),
             sems((3,)),
             sems((3,)),
         ],

time: 58.6 us -> 67 us (1.14)
  Pallas kernels: 30.8 us -> 41.8 us
  waiting for transfers between devices: 2.52 us -> 0.02 us
    pallas_call x1, Pallas kernels: 2.4 us -> 14.5 us  [per_device(): pl.pallas_call(functools.partial(pack_kernel, capacity, chunked), out_sha...]
    all_to_all x1, waiting for transfers between devices: 2.5 us -> 0.01 us  [per_device(): lax.all_to_all(outgoing, 'gx', split_axis=0, concat_axis=0, tiled=True)]
    pallas_call x1, Pallas kernels: 6.75 us -> 5.69 us  [per_device(): pl.pallas_call(functools.partial(finish_kernel, tile, n_stream, n_wall, c...]
    unnamed x16, local copies, waits for them, and re-layouts: 0.74 us -> 1.44 us
    broadcast_in_dim x1 -> x0, local copies, waits for them, and re-layouts: 0.7 us -> none  [per_device(): held = jnp.zeros((8, 128), f32)]
  transfers between devices with their start and end apart: 8 -> 8, of which waited for: 1 -> 0; matrix products, arithmetic and copies ran while one was open for 0% -> 0% of each run, Pallas kernels for 35% -> 33%
where the time goes in v4:
time: 67 us; the launch traced here: 66.5 us
  Pallas kernels  41.8 us (62%)
  starting transfers between devices  22.4 us (33%)
  local copies, waits for them, and re-layouts  1.44 us (2%)
  between operations  0.79 us (1%)
    pallas_call x1, Pallas kernels, per_device(): pl.pallas_call(functools.partial(pack_kernel, capacity, chunked), out_sha...  14.5 us
    pallas_call x1, Pallas kernels, per_device(): pl.pallas_call(spread_kernel, out_shape=shape(velocity.shape, f32), in_sp...  9.3 us
    pallas_call x1, Pallas kernels, per_device(): pl.pallas_call(functools.partial(sample_kernel, tile), out_shape=(shape((...  8.4 us
    pallas_call x1, Pallas kernels, per_device(): pl.pallas_call(functools.partial(finish_kernel, tile, n_stream, n_wall, c...  5.69 us
    all_to_all x1, starting transfers between devices, per_device(): lax.all_to_all(outgoing, 'gx', split_axis=0, concat_axis=0, tiled=True)  4.88 us
    ppermute x1, starting transfers between devices, per_device(): from_x1 = lax.ppermute(x0, 'gx', down_x)  4.72 us
    ppermute x1, starting transfers between devices, per_device(): right = lax.ppermute(arrived, 'gx', down_x)  4.61 us
    pallas_call x1, Pallas kernels, per_device(): pl.pallas_call(split_kernel, grid=(3,), out_shape=(shape((3, block, cells...  3.91 us
  transfers between devices with their start and end apart: 8, of which 0 were waited for; matrix products, arithmetic and copies ran while one was open for 0% of the time, Pallas kernels for 33%

profile of v4, /device:TPU:0, one launch (start us, length us, event | category | flops | bytes accessed | tf_op | source)
XLA Modules:
  0.0 66.5 jit_solution(18278712359886936451)
XLA Ops:
  0.6 14.5 %pack.1 = (f32[8,24,128]{2,1,0:T(8,128)}, s32[1,512]{1,0:T(1,128)}, f32[3,64,256]{2,1,0:T(8,128)}, f32[3,64,256]{2,1,0:T(8,128)}) custom-call(s32[1,512]{1,0:T(1,128)} %bitcast.1, f32[3,512]{1,0:T(4,128)} %target_ref.1, f32[3,6,512]{2,1,0:T(8,128)} %weights_ref.1, s32[3,512]{1,0:T(4,128)} %corners_ref.1, f32[3,12,64,256]{3,2,1,0:T(8,128)} %velocity_hbm.5), custom_call_target="tpu_custom_call" | custom-call | tf_op jit(solution)/shard_map/pack/pallas_call | solution.py:321
  15.2 3.0 %collective-permute-start = (f32[3,64,256]{2,1,0:T(8,128)}, f32[3,64,256]{2,1,0:T(8,128)S(1)}, u32[]{:S(2)}, u32[]{:S(2)}) collective-permute-start(f32[3,64,256]{2,1,0:T(8,128)} %get-tuple-element.22), channel_id=1, source_target_pairs={{0,4},{4,8},{8,12},{12,16},{16,20},{20,24},{24,28},{28,0},{1,5},{5... | collective-permute-start | bytes 589832 | tf_op jit(solution)/shard_map/ppermute | solution.py:354
  18.2 4.9 %all-to-all-start = ((f32[8,24,128]{2,1,0:T(8,128)}), f32[8,24,128]{2,1,0:T(8,128)S(1)}, u32[]{:S(2)}, u32[]{:S(2)}) async-start(f32[8,24,128]{2,1,0:T(8,128)} %get-tuple-element.15), calls=%async_computation | async-start | bytes 196608 | tf_op jit(solution)/shard_map/all_to_all | solution.py:335
  23.1 4.7 %collective-permute-start.1 = (f32[3,64,256]{2,1,0:T(8,128)}, f32[3,64,256]{2,1,0:T(8,128)S(1)}, u32[]{:S(2)}, u32[]{:S(2)}) collective-permute-start(f32[3,64,256]{2,1,0:T(8,128)} %get-tuple-element.23), channel_id=1, source_target_pairs={{4,0},{8,4},{12,8},{16,12},{20,16},{24,20},{28,24},{0,28},{5,1},{9... | collective-permute-start | bytes 589832 | tf_op jit(solution)/shard_map/ppermute | solution.py:355
  27.8 3.9 %split.1 = (bf16[3,768,256]{2,1,0:T(8,128)(2,1)}, bf16[3,768,256]{2,1,0:T(8,128)(2,1)}) custom-call(f32[3,12,64,256]{3,2,1,0:T(8,128)} %velocity_hbm.5), custom_call_target="tpu_custom_call" | custom-call | tf_op jit(solution)/shard_map/split/pallas_call | solution.py:341
  31.7 0.0 all-to-all-done.arrived_ref
  31.7 0.0 copy-start.1
  31.7 0.7 copy-done.1
  32.4 8.4 %sample.1 = (f32[8,3,1024]{2,1,0:T(4,128)}, bf16[256,1024]{1,0:T(8,128)(2,1)}, bf16[256,1024]{1,0:T(8,128)(2,1)}, f32[64,1024]{1,0:T(8,128)}, f32[3,12,1024]{2,1...) custom-call(f32[8,24,128]{2,1,0:T(8,128)} %copy-done.1, bf16[3,768,256]{2,1,0:T(8,128)(2,1)} %get-tuple-element.16.high_hbm, ...), custom_call_target="tpu_custom_call" | custom-call | tf_op jit(solution)/shard_map/sample/pallas_call | solution.py:360
  40.8 3.4 %all-to-all-start.1 = ((f32[8,3,1024]{2,1,0:T(4,128)}), f32[8,3,1024]{2,1,0:T(4,128)S(1)}, u32[]{:S(2)}, u32[]{:S(2)}) async-start(f32[8,3,1024]{2,1,0:T(4,128)} %get-tuple-element.26), calls=%async_computation.1 | async-start | bytes 262144 | tf_op jit(solution)/shard_map/all_to_all | solution.py:392
  44.2 0.1 collective-permute-start.2
  44.2 1.7 %collective-permute-start.3 = (f32[3,12,256]{2,1,0:T(8,128)}, f32[3,12,256]{2,1,0:T(8,128)S(1)}, u32[]{:S(2)}, u32[]{:S(2)}) collective-permute-start(f32[3,12,256]{2,1,0:T(8,128)} %get-tuple-element.25), channel_id=1, source_target_pairs={{1,0},{2,1},{3,2},{0,3},{5,4},{6,5},{7,6},{4,7},{9,8},{10,9},{11,1... | collective-permute-start | bytes 110600 | tf_op jit(solution)/shard_map/ppermute | solution.py:391
  46.0 4.6 %collective-permute-start.5 = (f32[8,24,128]{2,1,0:T(8,128)}, f32[8,24,128]{2,1,0:T(8,128)S(1)}, u32[]{:S(2)}, u32[]{:S(2)}) collective-permute-start(f32[8,24,128]{2,1,0:T(8,128)} %copy-done.1), channel_id=1, source_target_pairs={{4,0},{8,4},{12,8},{16,12},{20,16},{24,20},{28,24},{0,28},{5,1},{9... | collective-permute-start | bytes 294920 | tf_op jit(solution)/shard_map/ppermute | solution.py:357
  50.6 0.0 collective-permute-done.x0_ref
  50.6 0.0 copy-start.2
  50.6 0.0 collective-permute-start.4
  50.6 9.3 %spread.1.rhs_hbm = f32[3,12,64,256]{3,2,1,0:T(8,128)} custom-call(f32[3,12,64,256]{3,2,1,0:T(8,128)} %velocity_hbm.5, bf16[256,1024]{1,0:T(8,128)(2,1)} %get-tuple-element.18.wzh_ref, bf16[256,1024]{1,0:T(8,128)(2,1)} %get-tuple-element.19.wzl_ref, f32[64,1024]{1,0:T(8,128)} %get-tuple-element.20.wy_ref, f32[3,12,1024]{2,1,0:T(8,128)} %get-tuple-element.21.fx_ref), custom_call_target="tpu_custom_call" | custom-call | flops 3623878656 | bytes 4718592 | tf_op jit(solution)/shard_map/spread/pallas_call | solution.py:399
  59.9 0.0 copy-done.2
  59.9 0.0 collective-permute-done.1.x1_ref
  59.9 0.0 copy-start.3
  59.9 0.0 collective-permute-done.2.y0_ref
  59.9 0.0 copy-start.6
  59.9 0.0 collective-permute-done.3.y1_ref
  60.0 0.0 copy-start.7
  60.0 0.0 collective-permute-done.5.right_ref
  60.0 0.0 copy-start.4
  60.0 0.0 collective-permute-done.4.left_ref
  60.0 0.0 copy-start.5
  60.0 0.0 all-to-all-done.1.given_ref
  60.0 0.0 copy-start
  60.0 0.6 copy-done.3
  60.6 0.0 copy-done.6
  60.6 0.0 copy-done.7
  60.6 0.0 copy-done.4
  60.7 0.0 copy-done.5
  60.7 0.1 copy-done
  60.8 5.7 %finish.1 = (f32[3,12,64,256]{3,2,1,0:T(8,128)}, f32[3,512]{1,0:T(4,128)}) custom-call(f32[3,12,64,256]{3,2,1,0:T(8,128)} %spread.1.rhs_hbm, f32[3,64,256]{2,1,0:T(8,128)} %copy-done.2, f32[3,64,256]{2,1,0:T(8,128)} %copy-done.3, f32[3,12,256]{2,1,0:T(8,128)} %copy-done.6, f32[3,12,256]{2,1,0:T(8,128)} %copy-done.7, f32[8,24,128]{2,1,0:T(8,128)} %copy-done.5, ...), custom_call_target="tpu_custom_call" | custom-call | tf_op jit(solution)/shard_map/finish/pallas_call | solution.py:415
Async XLA Ops:
  15.2 35.4 %collective-permute-start = (f32[3,64,256]{2,1,0:T(8,128)}, f32[3,64,256]{2,1,0:T(8,128)S(1)}, u32[]{:S(2)}, u32[]{:S(2)}) collective-permute-start(f32[3,64,256]{2,1,0:T(8,128)} %get-tuple-element.22), channel_id=1, source_target_pairs={{0,4},{4,8},{8,12},{12,16},{16,20},{20,24},{24,28},{28,0},{1,5},{5... | collective-permute-start | bytes 589832 | tf_op jit(solution)/shard_map/ppermute | solution.py:354
  18.2 13.5 %all-to-all-start = ((f32[8,24,128]{2,1,0:T(8,128)}), f32[8,24,128]{2,1,0:T(8,128)S(1)}, u32[]{:S(2)}, u32[]{:S(2)}) async-start(f32[8,24,128]{2,1,0:T(8,128)} %get-tuple-element.15), calls=%async_computation | async-start | bytes 196608 | tf_op jit(solution)/shard_map/all_to_all | solution.py:335
  23.1 36.8 %collective-permute-start.1 = (f32[3,64,256]{2,1,0:T(8,128)}, f32[3,64,256]{2,1,0:T(8,128)S(1)}, u32[]{:S(2)}, u32[]{:S(2)}) collective-permute-start(f32[3,64,256]{2,1,0:T(8,128)} %get-tuple-element.23), channel_id=1, source_target_pairs={{4,0},{8,4},{12,8},{16,12},{20,16},{24,20},{28,24},{0,28},{5,1},{9... | collective-permute-start | bytes 589832 | tf_op jit(solution)/shard_map/ppermute | solution.py:355
  31.7 0.7 copy-start.1
  40.8 19.2 %all-to-all-start.1 = ((f32[8,3,1024]{2,1,0:T(4,128)}), f32[8,3,1024]{2,1,0:T(4,128)S(1)}, u32[]{:S(2)}, u32[]{:S(2)}) async-start(f32[8,3,1024]{2,1,0:T(4,128)} %get-tuple-element.26), calls=%async_computation.1 | async-start | bytes 262144 | tf_op jit(solution)/shard_map/all_to_all | solution.py:392
  44.2 15.8 %collective-permute-start.2 = (f32[3,12,256]{2,1,0:T(8,128)}, f32[3,12,256]{2,1,0:T(8,128)S(1)}, u32[]{:S(2)}, u32[]{:S(2)}) collective-permute-start(f32[3,12,256]{2,1,0:T(8,128)} %get-tuple-element.24), channel_id=1, source_target_pairs={{0,1},{1,2},{2,3},{3,0},{4,5},{5,6},{6,7},{7,4},{8,9},{9,10},{10,1... | collective-permute-start | bytes 110600 | tf_op jit(solution)/shard_map/ppermute | solution.py:390
  44.2 15.7 %collective-permute-start.3 = (f32[3,12,256]{2,1,0:T(8,128)}, f32[3,12,256]{2,1,0:T(8,128)S(1)}, u32[]{:S(2)}, u32[]{:S(2)}) collective-permute-start(f32[3,12,256]{2,1,0:T(8,128)} %get-tuple-element.25), channel_id=1, source_target_pairs={{1,0},{2,1},{3,2},{0,3},{5,4},{6,5},{7,6},{4,7},{9,8},{10,9},{11,1... | collective-permute-start | bytes 110600 | tf_op jit(solution)/shard_map/ppermute | solution.py:391
  46.0 14.0 %collective-permute-start.5 = (f32[8,24,128]{2,1,0:T(8,128)}, f32[8,24,128]{2,1,0:T(8,128)S(1)}, u32[]{:S(2)}, u32[]{:S(2)}) collective-permute-start(f32[8,24,128]{2,1,0:T(8,128)} %copy-done.1), channel_id=1, source_target_pairs={{4,0},{8,4},{12,8},{16,12},{20,16},{24,20},{28,24},{0,28},{5,1},{9... | collective-permute-start | bytes 294920 | tf_op jit(solution)/shard_map/ppermute | solution.py:357
  50.6 9.3 %copy-start.2 = (f32[3,64,256]{2,1,0:T(8,128)}, f32[3,64,256]{2,1,0:T(8,128)S(1)}, u32[]{:S(2)}) copy-start(f32[3,64,256]{2,1,0:T(8,128)S(1)} %collective-permute-done.x0_ref) | copy-start | bytes 589828
  50.6 9.4 %collective-permute-start.4 = (f32[8,24,128]{2,1,0:T(8,128)}, f32[8,24,128]{2,1,0:T(8,128)S(1)}, u32[]{:S(2)}, u32[]{:S(2)}) collective-permute-start(f32[8,24,128]{2,1,0:T(8,128)} %copy-done.1), channel_id=1, source_target_pairs={{0,4},{4,8},{8,12},{12,16},{16,20},{20,24},{24,28},{28,0},{1,5},{5... | collective-permute-start | bytes 294920 | tf_op jit(solution)/shard_map/ppermute | solution.py:356
  59.9 0.7 %copy-start.3 = (f32[3,64,256]{2,1,0:T(8,128)}, f32[3,64,256]{2,1,0:T(8,128)S(1)}, u32[]{:S(2)}) copy-start(f32[3,64,256]{2,1,0:T(8,128)S(1)} %collective-permute-done.1.x1_ref) | copy-start | bytes 589828
  59.9 0.7 %copy-start.6 = (f32[3,12,256]{2,1,0:T(8,128)}, f32[3,12,256]{2,1,0:T(8,128)S(1)}, u32[]{:S(2)}) copy-start(f32[3,12,256]{2,1,0:T(8,128)S(1)} %collective-permute-done.2.y0_ref) | copy-start | bytes 110596
  60.0 0.7 %copy-start.7 = (f32[3,12,256]{2,1,0:T(8,128)}, f32[3,12,256]{2,1,0:T(8,128)S(1)}, u32[]{:S(2)}) copy-start(f32[3,12,256]{2,1,0:T(8,128)S(1)} %collective-permute-done.3.y1_ref) | copy-start | bytes 110596
  60.0 0.7 %copy-start.4 = (f32[8,24,128]{2,1,0:T(8,128)}, f32[8,24,128]{2,1,0:T(8,128)S(1)}, u32[]{:S(2)}) copy-start(f32[8,24,128]{2,1,0:T(8,128)S(1)} %collective-permute-done.5.right_ref) | copy-start | bytes 294916
  60.0 0.7 %copy-start.5 = (f32[8,24,128]{2,1,0:T(8,128)}, f32[8,24,128]{2,1,0:T(8,128)S(1)}, u32[]{:S(2)}) copy-start(f32[8,24,128]{2,1,0:T(8,128)S(1)} %collective-permute-done.4.left_ref) | copy-start | bytes 294916
  60.0 0.8 %copy-start = (f32[8,3,1024]{2,1,0:T(4,128)}, f32[8,3,1024]{2,1,0:T(4,128)S(1)}, u32[]{:S(2)}) copy-start(f32[8,3,1024]{2,1,0:T(4,128)S(1)} %all-to-all-done.1.given_ref) | copy-start | bytes 294916

commit v5 on v4

--- a/solution.py
+++ b/solution.py
@@ -55,13 +55,13 @@
 
 def pack_kernel(
     capacity, chunked, dest_ref, target_ref, weights_ref, corners_ref, velocity_hbm,
-    out_ref, pos_ref, x0_hbm, x1_hbm, rows_ref, sem,
+    out_ref, pos_ref, x0_ref, x1_ref, rows_ref, sem,
 ):
     owned = target_ref.shape[1]
     cells_x = velocity_hbm.shape[1]
     faces = [
-        pltpu.make_async_copy(velocity_hbm.at[:, 0], x0_hbm, sem.at[0]),
-        pltpu.make_async_copy(velocity_hbm.at[:, cells_x - 1], x1_hbm, sem.at[1]),
+        pltpu.make_async_copy(velocity_hbm.at[:, 0], x0_ref, sem.at[0]),
+        pltpu.make_async_copy(velocity_hbm.at[:, cells_x - 1], x1_ref, sem.at[1]),
     ]
     for face in faces:
         face.start()
@@ -93,13 +93,6 @@
         face.wait()
 
 
-def split_kernel(velocity_ref, high_ref, low_ref):
-    _, cells_x, cells_y, cells_z = velocity_ref.shape
-    high, low = halves(velocity_ref[0].reshape(cells_x * cells_y, cells_z))
-    high_ref[0] = high
-    low_ref[0] = low
-
-
 def window(weights, corner, length):
     offset = lax.broadcasted_iota(i32, (length, weights.shape[1]), 0) - corner
     out = jnp.zeros(offset.shape, f32)
@@ -119,26 +112,14 @@
 
 
 def sample_kernel(
-    tile, arrived_ref, high_hbm, low_hbm, velocity_hbm,
+    tile, arrived_ref, velocity_hbm,
     force_ref, wzh_hbm, wzl_hbm, wy_ref, fx_ref, y0_ref, y1_ref,
-    high_ref, low_ref, lower_ref, upper_ref, wzh_ref, wzl_ref, boxh_ref, boxl_ref, in_sem, edge_sem, out_sem,
+    cell_ref, high_ref, low_ref, wzh_ref, wzl_ref, boxh_ref, boxl_ref, in_sem, out_sem,
 ):
     cells_x, cells_z = y0_ref.shape[1:]
     cells_y, slots = wy_ref.shape
-    loads = []
-    for c in range(3):
-        pair = [
-            pltpu.make_async_copy(high_hbm.at[c], high_ref.at[c], in_sem.at[0, c]),
-            pltpu.make_async_copy(low_hbm.at[c], low_ref.at[c], in_sem.at[1, c]),
-        ]
-        for load in pair:
-            load.start()
-        loads.append(pair)
-    edges = [
-        pltpu.make_async_copy(velocity_hbm.at[:, :, pl.ds(0, 8), :], lower_ref, edge_sem.at[0]),
-        pltpu.make_async_copy(velocity_hbm.at[:, :, pl.ds(cells_y - 8, 8), :], upper_ref, edge_sem.at[1]),
-    ]
-    for load in edges:
+    loads = [pltpu.make_async_copy(velocity_hbm.at[c], cell_ref.at[c], in_sem.at[c]) for c in range(3)]
+    for load in loads:
         load.start()
     kept = []
     for at, data in tiles_of(arrived_ref, tile, slots):
@@ -155,8 +136,10 @@
     for store in stores:
         store.start()
     for c in range(3):
-        for load in loads[c]:
-            load.wait()
+        loads[c].wait()
+        high, low = halves(cell_ref[c].reshape(cells_x * cells_y, cells_z))
+        high_ref[c] = high
+        low_ref[c] = low
         for at, target, wx in kept:
             along = dot3(high_ref[c], low_ref[c], wzh_ref[:, at], wzl_ref[:, at])
             along = along.reshape(cells_x, cells_y, tile) * wy_ref[:, at][None]
@@ -176,12 +159,10 @@
             boxl_ref[base : base + pad] = low
             base += pad
     spread = dot3(boxh_ref[...], boxl_ref[...], wzh_ref[...], wzl_ref[...], NT)
-    for load in edges:
-        load.wait()
     base = 0
-    for y, slab_ref, ref in ((0, lower_ref, y0_ref), (7, upper_ref, y1_ref)):
+    for y, ref in ((0, y0_ref), (cells_y - 1, y1_ref)):
         for c in range(3):
-            ref[c] = slab_ref[c, :, y, :] + spread[base : base + cells_x]
+            ref[c] = cell_ref[c, :, y, :] + spread[base : base + cells_x]
             base += pad
     for store in stores:
         store.wait()
@@ -327,7 +308,7 @@
             face_x,
         ),
         in_specs=[VMEM] * 4 + [HBM],
-        out_specs=(VMEM, VMEM, HBM, HBM),
+        out_specs=(VMEM,) * 4,
         scratch_shapes=[pltpu.VMEM((ROWS, owned), f32), sems((2,))],
         name="pack",
     )(dest.reshape(1, owned), target, weights, corners, velocity)
@@ -337,15 +318,6 @@
         outgoing = outgoing.reshape(ROWS, n_stream, capacity)
         arrived = lax.all_to_all(outgoing, "gx", split_axis=1, concat_axis=1, tiled=True)
         arrived = arrived.reshape(ROWS, slots)
-
-    high, low = pl.pallas_call(
-        split_kernel,
-        grid=(3,),
-        out_shape=(shape((3, block, cells_z), bf16),) * 2,
-        in_specs=[pl.BlockSpec((1, cells_x, cells_y, cells_z), lambda c: (c, 0, 0, 0))],
-        out_specs=(pl.BlockSpec((1, block, cells_z), lambda c: (c, 0, 0)),) * 2,
-        name="split",
-    )(velocity)
 
     up_x = [(i, (i + 1) % n_stream) for i in range(n_stream)]
     down_x = [(j, i) for i, j in up_x]
@@ -368,24 +340,22 @@
             shape((3, cells_x, cells_z), f32),
             shape((3, cells_x, cells_z), f32),
         ),
-        in_specs=[VMEM, HBM, HBM, HBM],
+        in_specs=[VMEM, HBM],
         out_specs=(VMEM, HBM, HBM, VMEM, VMEM, VMEM, VMEM),
         scratch_shapes=[
+            pltpu.VMEM(velocity.shape, f32),
             pltpu.VMEM((3, block, cells_z), bf16),
             pltpu.VMEM((3, block, cells_z), bf16),
-            pltpu.VMEM((3, cells_x, 8, cells_z), f32),
-            pltpu.VMEM((3, cells_x, 8, cells_z), f32),
             pltpu.VMEM((cells_z, slots), bf16),
             pltpu.VMEM((cells_z, slots), bf16),
             pltpu.VMEM((6 * pad, slots), bf16),
             pltpu.VMEM((6 * pad, slots), bf16),
-            sems((2, 3)),
-            sems((2,)),
+            sems((3,)),
             sems((2,)),
         ],
         compiler_params=pltpu.CompilerParams(vmem_limit_bytes=63_280_000),
         name="sample",
-    )(arrived, high, low, velocity)
+    )(arrived, velocity)
 
     from_y0 = lax.ppermute(y1, "gy", up_y)
     from_y1 = lax.ppermute(y0, "gy", down_y)

time: 67 us -> 53.6 us (0.80)
  Pallas kernels: 41.8 us -> 26 us
  waiting for transfers between devices: 0.02 us -> 2.52 us
    pallas_call x1, Pallas kernels: 14.5 us -> 2.65 us  [per_device(): pl.pallas_call(functools.partial(pack_kernel, capacity, chunked), out_sha...]
    pallas_call x1 -> x0, Pallas kernels: 3.91 us -> none  [per_device(): pl.pallas_call(split_kernel, grid=(3,), out_shape=(shape((3, block, cells...]
    all_to_all x1, waiting for transfers between devices: 0.01 us -> 2.5 us  [per_device(): lax.all_to_all(outgoing, 'gx', split_axis=0, concat_axis=0, tiled=True)]
  transfers between devices with their start and end apart: 8 -> 8, of which waited for: 0 -> 1; matrix products, arithmetic and copies ran while one was open for 0% -> 0% of each run, Pallas kernels for 33% -> 33%
where the time goes in v5:
time: 53.6 us; the launch traced here: 53.1 us
  Pallas kernels  26 us (49%)
  starting transfers between devices  22.4 us (42%)
  waiting for transfers between devices  2.52 us (5%)
  local copies, waits for them, and re-layouts  1.38 us (3%)
  between operations  0.78 us (1%)
    pallas_call x1, Pallas kernels, per_device(): pl.pallas_call(spread_kernel, out_shape=shape(velocity.shape, f32), in_sp...  9.3 us
    pallas_call x1, Pallas kernels, per_device(): pl.pallas_call(functools.partial(sample_kernel, tile), out_shape=(shape((...  8.32 us
    pallas_call x1, Pallas kernels, per_device(): pl.pallas_call(functools.partial(finish_kernel, tile, n_stream, n_wall, c...  5.69 us
    all_to_all x1, starting transfers between devices, per_device(): lax.all_to_all(outgoing, 'gx', split_axis=0, concat_axis=0, tiled=True)  4.88 us
    ppermute x1, starting transfers between devices, per_device(): from_x1 = lax.ppermute(x0, 'gx', down_x)  4.72 us
    ppermute x1, starting transfers between devices, per_device(): right = lax.ppermute(arrived, 'gx', down_x)  4.61 us
    all_to_all x1, starting transfers between devices, per_device(): given = lax.all_to_all(force, 'gx', split_axis=0, concat_axis=0, tiled=True)  3.38 us
    ppermute x1, starting transfers between devices, per_device(): from_x0 = lax.ppermute(x1, 'gx', up_x)  3.05 us
  transfers between devices with their start and end apart: 8, of which 1 were waited for; matrix products, arithmetic and copies ran while one was open for 0% of the time, Pallas kernels for 33%

profile of v5, /device:TPU:0, one launch (start us, length us, event | category | flops | bytes accessed | tf_op | source)
XLA Modules:
  0.0 53.1 jit_solution(16155917608856903220)
XLA Ops:
  0.6 2.6 %pack.1 = (f32[8,24,128]{2,1,0:T(8,128)}, s32[1,512]{1,0:T(1,128)}, f32[3,64,256]{2,1,0:T(8,128)}, f32[3,64,256]{2,1,0:T(8,128)}) custom-call(s32[1,512]{1,0:T(1,128)} %bitcast.1, f32[3,512]{1,0:T(4,128)} %target_ref.1, f32[3,6,512]{2,1,0:T(8,128)} %weights_ref.1, s32[3,512]{1,0:T(4,128)} %corners_ref.1, f32[3,12,64,256]{3,2,1,0:T(8,128)} %velocity_hbm.5), custom_call_target="tpu_custom_call" | custom-call | tf_op jit(solution)/shard_map/pack/pallas_call | solution.py:302
  3.3 3.0 %collective-permute-start = (f32[3,64,256]{2,1,0:T(8,128)}, f32[3,64,256]{2,1,0:T(8,128)S(1)}, u32[]{:S(2)}, u32[]{:S(2)}) collective-permute-start(f32[3,64,256]{2,1,0:T(8,128)} %get-tuple-element.18), channel_id=1, source_target_pairs={{0,4},{4,8},{8,12},{12,16},{16,20},{20,24},{24,28},{28,0},{1,5},{5... | collective-permute-start | bytes 589832 | tf_op jit(solution)/shard_map/ppermute | solution.py:326
  6.3 4.9 %all-to-all-start = ((f32[8,24,128]{2,1,0:T(8,128)}), f32[8,24,128]{2,1,0:T(8,128)S(1)}, u32[]{:S(2)}, u32[]{:S(2)}) async-start(f32[8,24,128]{2,1,0:T(8,128)} %get-tuple-element.13), calls=%async_computation | async-start | bytes 196608 | tf_op jit(solution)/shard_map/all_to_all | solution.py:316
  11.2 4.7 %collective-permute-start.1 = (f32[3,64,256]{2,1,0:T(8,128)}, f32[3,64,256]{2,1,0:T(8,128)S(1)}, u32[]{:S(2)}, u32[]{:S(2)}) collective-permute-start(f32[3,64,256]{2,1,0:T(8,128)} %get-tuple-element.19), channel_id=1, source_target_pairs={{4,0},{8,4},{12,8},{16,12},{20,16},{24,20},{28,24},{0,28},{5,1},{9... | collective-permute-start | bytes 589832 | tf_op jit(solution)/shard_map/ppermute | solution.py:327
  15.9 2.5 %all-to-all-done.arrived_ref = f32[8,24,128]{2,1,0:T(8,128)S(1)} async-done(((f32[8,24,128]{2,1,0:T(8,128)}), f32[8,24,128]{2,1,0:T(8,128)S(1)}, u32[]{:S(2)}, u32[]{:S(2)}) %all-to-all-start) | async-done | bytes 98336 | tf_op jit(solution)/shard_map/all_to_all | solution.py:316
  18.4 0.0 copy-start.1
  18.4 0.6 %copy-done.1 = f32[8,24,128]{2,1,0:T(8,128)} copy-done((f32[8,24,128]{2,1,0:T(8,128)}, f32[8,24,128]{2,1,0:T(8,128)S(1)}, u32[]{:S(2)}) %copy-start.1) | copy-done | bytes 98328
  19.1 8.3 %sample.1 = (f32[8,3,1024]{2,1,0:T(4,128)}, bf16[256,1024]{1,0:T(8,128)(2,1)}, bf16[256,1024]{1,0:T(8,128)(2,1)}, f32[64,1024]{1,0:T(8,128)}, f32[3,12,1024]{2,1...) custom-call(f32[8,24,128]{2,1,0:T(8,128)} %copy-done.1, f32[3,12,64,256]{3,2,1,0:T(8,128)} %velocity_hbm.5), custom_call_target="tpu_custom_call" | custom-call | tf_op jit(solution)/shard_map/sample/pallas_call | solution.py:332
  27.4 3.4 %all-to-all-start.1 = ((f32[8,3,1024]{2,1,0:T(4,128)}), f32[8,3,1024]{2,1,0:T(4,128)S(1)}, u32[]{:S(2)}, u32[]{:S(2)}) async-start(f32[8,3,1024]{2,1,0:T(4,128)} %get-tuple-element.22), calls=%async_computation.1 | async-start | bytes 262144 | tf_op jit(solution)/shard_map/all_to_all | solution.py:362
  30.8 0.1 collective-permute-start.2
  30.9 1.7 %collective-permute-start.3 = (f32[3,12,256]{2,1,0:T(8,128)}, f32[3,12,256]{2,1,0:T(8,128)S(1)}, u32[]{:S(2)}, u32[]{:S(2)}) collective-permute-start(f32[3,12,256]{2,1,0:T(8,128)} %get-tuple-element.21), channel_id=1, source_target_pairs={{1,0},{2,1},{3,2},{0,3},{5,4},{6,5},{7,6},{4,7},{9,8},{10,9},{11,1... | collective-permute-start | bytes 110600 | tf_op jit(solution)/shard_map/ppermute | solution.py:361
  32.6 4.6 %collective-permute-start.5 = (f32[8,24,128]{2,1,0:T(8,128)}, f32[8,24,128]{2,1,0:T(8,128)S(1)}, u32[]{:S(2)}, u32[]{:S(2)}) collective-permute-start(f32[8,24,128]{2,1,0:T(8,128)} %copy-done.1), channel_id=1, source_target_pairs={{4,0},{8,4},{12,8},{16,12},{20,16},{24,20},{28,24},{0,28},{5,1},{9... | collective-permute-start | bytes 294920 | tf_op jit(solution)/shard_map/ppermute | solution.py:329
  37.2 0.0 collective-permute-done.x0_ref
  37.2 0.0 copy-start.2
  37.2 0.0 collective-permute-start.4
  37.2 9.3 %spread.1.rhs_hbm = f32[3,12,64,256]{3,2,1,0:T(8,128)} custom-call(f32[3,12,64,256]{3,2,1,0:T(8,128)} %velocity_hbm.5, bf16[256,1024]{1,0:T(8,128)(2,1)} %get-tuple-element.14.wzh_ref, bf16[256,1024]{1,0:T(8,128)(2,1)} %get-tuple-element.15.wzl_ref, f32[64,1024]{1,0:T(8,128)} %get-tuple-element.16.wy_ref, f32[3,12,1024]{2,1,0:T(8,128)} %get-tuple-element.17.fx_ref), custom_call_target="tpu_custom_call" | custom-call | flops 3623878656 | bytes 4718592 | tf_op jit(solution)/shard_map/spread/pallas_call | solution.py:369
  46.5 0.0 copy-done.2
  46.5 0.0 collective-permute-done.1.x1_ref
  46.5 0.0 copy-start.3
  46.6 0.0 collective-permute-done.2.y0_ref
  46.6 0.0 copy-start.6
  46.6 0.0 collective-permute-done.3.y1_ref
  46.6 0.0 copy-start.7
  46.6 0.0 collective-permute-done.5.right_ref
  46.6 0.0 copy-start.4
  46.6 0.0 collective-permute-done.4.left_ref
  46.6 0.0 copy-start.5
  46.6 0.0 all-to-all-done.1.given_ref
  46.7 0.0 copy-start
  46.7 0.6 %copy-done.3 = f32[3,64,256]{2,1,0:T(8,128)} copy-done((f32[3,64,256]{2,1,0:T(8,128)}, f32[3,64,256]{2,1,0:T(8,128)S(1)}, u32[]{:S(2)}) %copy-start.3) | copy-done | bytes 196632
  47.2 0.0 copy-done.6
  47.3 0.0 copy-done.7
  47.3 0.0 copy-done.4
  47.3 0.0 copy-done.5
  47.3 0.0 copy-done
  47.4 5.7 %finish.1 = (f32[3,12,64,256]{3,2,1,0:T(8,128)}, f32[3,512]{1,0:T(4,128)}) custom-call(f32[3,12,64,256]{3,2,1,0:T(8,128)} %spread.1.rhs_hbm, f32[3,64,256]{2,1,0:T(8,128)} %copy-done.2, f32[3,64,256]{2,1,0:T(8,128)} %copy-done.3, f32[3,12,256]{2,1,0:T(8,128)} %copy-done.6, f32[3,12,256]{2,1,0:T(8,128)} %copy-done.7, f32[8,24,128]{2,1,0:T(8,128)} %copy-done.5, ...), custom_call_target="tpu_custom_call" | custom-call | tf_op jit(solution)/shard_map/finish/pallas_call | solution.py:385
Async XLA Ops:
  3.3 33.9 %collective-permute-start = (f32[3,64,256]{2,1,0:T(8,128)}, f32[3,64,256]{2,1,0:T(8,128)S(1)}, u32[]{:S(2)}, u32[]{:S(2)}) collective-permute-start(f32[3,64,256]{2,1,0:T(8,128)} %get-tuple-element.18), channel_id=1, source_target_pairs={{0,4},{4,8},{8,12},{12,16},{16,20},{20,24},{24,28},{28,0},{1,5},{5... | collective-permute-start | bytes 589832 | tf_op jit(solution)/shard_map/ppermute | solution.py:326
  6.3 12.1 %all-to-all-start = ((f32[8,24,128]{2,1,0:T(8,128)}), f32[8,24,128]{2,1,0:T(8,128)S(1)}, u32[]{:S(2)}, u32[]{:S(2)}) async-start(f32[8,24,128]{2,1,0:T(8,128)} %get-tuple-element.13), calls=%async_computation | async-start | bytes 196608 | tf_op jit(solution)/shard_map/all_to_all | solution.py:316
  11.2 35.3 %collective-permute-start.1 = (f32[3,64,256]{2,1,0:T(8,128)}, f32[3,64,256]{2,1,0:T(8,128)S(1)}, u32[]{:S(2)}, u32[]{:S(2)}) collective-permute-start(f32[3,64,256]{2,1,0:T(8,128)} %get-tuple-element.19), channel_id=1, source_target_pairs={{4,0},{8,4},{12,8},{16,12},{20,16},{24,20},{28,24},{0,28},{5,1},{9... | collective-permute-start | bytes 589832 | tf_op jit(solution)/shard_map/ppermute | solution.py:327
  18.4 0.6 %copy-start.1 = (f32[8,24,128]{2,1,0:T(8,128)}, f32[8,24,128]{2,1,0:T(8,128)S(1)}, u32[]{:S(2)}) copy-start(f32[8,24,128]{2,1,0:T(8,128)S(1)} %all-to-all-done.arrived_ref) | copy-start | bytes 294916
  27.4 19.2 %all-to-all-start.1 = ((f32[8,3,1024]{2,1,0:T(4,128)}), f32[8,3,1024]{2,1,0:T(4,128)S(1)}, u32[]{:S(2)}, u32[]{:S(2)}) async-start(f32[8,3,1024]{2,1,0:T(4,128)} %get-tuple-element.22), calls=%async_computation.1 | async-start | bytes 262144 | tf_op jit(solution)/shard_map/all_to_all | solution.py:362
  30.8 15.8 %collective-permute-start.2 = (f32[3,12,256]{2,1,0:T(8,128)}, f32[3,12,256]{2,1,0:T(8,128)S(1)}, u32[]{:S(2)}, u32[]{:S(2)}) collective-permute-start(f32[3,12,256]{2,1,0:T(8,128)} %get-tuple-element.20), channel_id=1, source_target_pairs={{0,1},{1,2},{2,3},{3,0},{4,5},{5,6},{6,7},{7,4},{8,9},{9,10},{10,1... | collective-permute-start | bytes 110600 | tf_op jit(solution)/shard_map/ppermute | solution.py:360
  30.9 15.7 %collective-permute-start.3 = (f32[3,12,256]{2,1,0:T(8,128)}, f32[3,12,256]{2,1,0:T(8,128)S(1)}, u32[]{:S(2)}, u32[]{:S(2)}) collective-permute-start(f32[3,12,256]{2,1,0:T(8,128)} %get-tuple-element.21), channel_id=1, source_target_pairs={{1,0},{2,1},{3,2},{0,3},{5,4},{6,5},{7,6},{4,7},{9,8},{10,9},{11,1... | collective-permute-start | bytes 110600 | tf_op jit(solution)/shard_map/ppermute | solution.py:361
  32.6 14.0 %collective-permute-start.5 = (f32[8,24,128]{2,1,0:T(8,128)}, f32[8,24,128]{2,1,0:T(8,128)S(1)}, u32[]{:S(2)}, u32[]{:S(2)}) collective-permute-start(f32[8,24,128]{2,1,0:T(8,128)} %copy-done.1), channel_id=1, source_target_pairs={{4,0},{8,4},{12,8},{16,12},{20,16},{24,20},{28,24},{0,28},{5,1},{9... | collective-permute-start | bytes 294920 | tf_op jit(solution)/shard_map/ppermute | solution.py:329
  37.2 9.3 %copy-start.2 = (f32[3,64,256]{2,1,0:T(8,128)}, f32[3,64,256]{2,1,0:T(8,128)S(1)}, u32[]{:S(2)}) copy-start(f32[3,64,256]{2,1,0:T(8,128)S(1)} %collective-permute-done.x0_ref) | copy-start | bytes 589828
  37.2 9.4 %collective-permute-start.4 = (f32[8,24,128]{2,1,0:T(8,128)}, f32[8,24,128]{2,1,0:T(8,128)S(1)}, u32[]{:S(2)}, u32[]{:S(2)}) collective-permute-start(f32[8,24,128]{2,1,0:T(8,128)} %copy-done.1), channel_id=1, source_target_pairs={{0,4},{4,8},{8,12},{12,16},{16,20},{20,24},{24,28},{28,0},{1,5},{5... | collective-permute-start | bytes 294920 | tf_op jit(solution)/shard_map/ppermute | solution.py:328
  46.5 0.7 %copy-start.3 = (f32[3,64,256]{2,1,0:T(8,128)}, f32[3,64,256]{2,1,0:T(8,128)S(1)}, u32[]{:S(2)}) copy-start(f32[3,64,256]{2,1,0:T(8,128)S(1)} %collective-permute-done.1.x1_ref) | copy-start | bytes 589828
  46.6 0.7 %copy-start.6 = (f32[3,12,256]{2,1,0:T(8,128)}, f32[3,12,256]{2,1,0:T(8,128)S(1)}, u32[]{:S(2)}) copy-start(f32[3,12,256]{2,1,0:T(8,128)S(1)} %collective-permute-done.2.y0_ref) | copy-start | bytes 110596
  46.6 0.7 %copy-start.7 = (f32[3,12,256]{2,1,0:T(8,128)}, f32[3,12,256]{2,1,0:T(8,128)S(1)}, u32[]{:S(2)}) copy-start(f32[3,12,256]{2,1,0:T(8,128)S(1)} %collective-permute-done.3.y1_ref) | copy-start | bytes 110596
  46.6 0.7 %copy-start.4 = (f32[8,24,128]{2,1,0:T(8,128)}, f32[8,24,128]{2,1,0:T(8,128)S(1)}, u32[]{:S(2)}) copy-start(f32[8,24,128]{2,1,0:T(8,128)S(1)} %collective-permute-done.5.right_ref) | copy-start | bytes 294916
  46.6 0.7 %copy-start.5 = (f32[8,24,128]{2,1,0:T(8,128)}, f32[8,24,128]{2,1,0:T(8,128)S(1)}, u32[]{:S(2)}) copy-start(f32[8,24,128]{2,1,0:T(8,128)S(1)} %collective-permute-done.4.left_ref) | copy-start | bytes 294916
  46.7 0.7 %copy-start = (f32[8,3,1024]{2,1,0:T(4,128)}, f32[8,3,1024]{2,1,0:T(4,128)S(1)}, u32[]{:S(2)}) copy-start(f32[8,3,1024]{2,1,0:T(4,128)S(1)} %all-to-all-done.1.given_ref) | copy-start | bytes 294916

commit v6 on v5

--- a/solution.py
+++ b/solution.py
@@ -19,6 +19,7 @@
 bf16 = jnp.bfloat16
 i32 = jnp.int32
 VMEM = pl.BlockSpec(memory_space=pltpu.VMEM)
+SMEM = pl.BlockSpec(memory_space=pltpu.SMEM)
 HBM = pl.BlockSpec(memory_space=pltpu.HBM)
 NN = (((1,), (0,)), ((), ()))
 NT = (((1,), (1,)), ((), ()))
@@ -68,10 +69,10 @@
     dest = dest_ref[...]
     corner = corners_ref[0:1, :]
     lane = lax.broadcasted_iota(i32, (1, owned), 1)
-    last = corner == cells_x - SPAN
-    group = jnp.where(last, 2, jnp.where(corner == 0, 0, 1))
-    first = (dest * 4 + jnp.where(last, 2, 0)) * owned
-    key = (dest * 4 + group) * owned + lane
+    top = cells_x - SPAN
+    last = corner > top // 2
+    first = (dest * 2 + jnp.where(last, 1, 0)) * (cells_x * owned)
+    key = first + jnp.where(last, top - corner, corner) * owned + lane
     column = jnp.transpose(jnp.broadcast_to(key, (8, owned)))[:, 0:1]
     ahead = jnp.where((column < key) & (column >= first), 1.0, 0.0)
     rank = jnp.sum(ahead, axis=0, keepdims=True).astype(i32)
@@ -111,97 +112,178 @@
             yield at, arrived_ref[:, at]
 
 
+def quarter(chunk, chunks, capacity, index, width):
+    lane = lax.broadcasted_iota(i32, (ROWS, capacity), 1)
+    per = capacity // width
+    out = []
+    for base in range(0, chunks, per):
+        piece = jnp.zeros((ROWS, capacity), f32)
+        for k in range(per):
+            moved = pltpu.roll(chunk(base + k), lax.rem(capacity + (k - index) * width, capacity), 1)
+            piece = jnp.where((lane >= k * width) & (lane < (k + 1) * width), moved, piece)
+        out.append(piece)
+    return jnp.concatenate(out, axis=1)
+
+
 def sample_kernel(
-    tile, arrived_ref, velocity_hbm,
-    force_ref, wzh_hbm, wzl_hbm, wy_ref, fx_ref, y0_ref, y1_ref,
-    cell_ref, high_ref, low_ref, wzh_ref, wzl_ref, boxh_ref, boxl_ref, in_sem, out_sem,
+    tile, n_stream, quartered, band, arrived_ref, velocity_hbm,
+    force_ref, wzh_hbm, wzl_hbm, wy_ref, fx_ref, y0_ref, y1_ref, start_ref,
+    cell_ref, high_ref, low_ref, wzh_ref, wzl_ref, wx_ref, rel_ref, goal_ref, face_ref, in_sem, out_sem,
 ):
     cells_x, cells_z = y0_ref.shape[1:]
     cells_y, slots = wy_ref.shape
+    pad = wx_ref.shape[0]
+    count = slots // tile
+    capacity = slots // n_stream
+    width = tile // n_stream
     loads = [pltpu.make_async_copy(velocity_hbm.at[c], cell_ref.at[c], in_sem.at[c]) for c in range(3)]
     for load in loads:
         load.start()
+
+    def tile_data(t):
+        if quartered:
+            return quarter(lambda k: arrived_ref[k], n_stream, capacity, t, width)
+        if len(arrived_ref.shape) == 3:
+            per = tile // capacity
+            return jnp.concatenate([arrived_ref[t * per + k] for k in range(per)], axis=1)
+        return arrived_ref[:, t * tile : (t + 1) * tile]
+
     kept = []
-    for at, data in tiles_of(arrived_ref, tile, slots):
+    fits = None
+    for t in range(count):
+        at = slice(t * tile, (t + 1) * tile)
+        data = tile_data(t)
         corner = data[21:24, :].astype(i32)
+        if quartered:
+            used = data[3:4] != 0.0
+            low = jnp.min(jnp.where(used, data[21:22], float(cells_x))).astype(i32)
+            high = jnp.max(jnp.where(used, data[21:22], -1.0)).astype(i32)
+            start = jnp.minimum(low, cells_x - band)
+            inside = high + SPAN <= start + band
+            fits = inside if fits is None else fits & inside
+        else:
+            start = 0
+        kept.append((at, data, corner, start))
         wy_ref[:, at] = window(data[9:15], corner[1:2], cells_y)
         high, low = halves(window(data[15:21], corner[2:3], cells_z))
         wzh_ref[:, at] = high
         wzl_ref[:, at] = low
-        kept.append((at, data[0:3], window(data[3:9], corner[0:1], cells_x)))
+        for c in range(3):
+            goal_ref[c, 0:1, at] = data[c : c + 1]
     stores = [
         pltpu.make_async_copy(wzh_ref, wzh_hbm, out_sem.at[0]),
         pltpu.make_async_copy(wzl_ref, wzl_hbm, out_sem.at[1]),
     ]
     for store in stores:
         store.start()
+    if not quartered:
+        fits = jnp.bool_(False)
+    for t, (at, data, corner, start) in enumerate(kept):
+        start = jnp.where(fits, start, 0)
+        start_ref[t] = start
+        wx_ref[:, at] = window(data[3:9], corner[0:1], pad)
+        rel_ref[:, at] = window(data[3:9], corner[0:1] - start, pad)
+    start_ref[count] = jnp.where(fits, 1, 0)
     for c in range(3):
         loads[c].wait()
         high, low = halves(cell_ref[c].reshape(cells_x * cells_y, cells_z))
         high_ref[c] = high
         low_ref[c] = low
-        for at, target, wx in kept:
-            along = dot3(high_ref[c], low_ref[c], wzh_ref[:, at], wzl_ref[:, at])
-            along = along.reshape(cells_x, cells_y, tile) * wy_ref[:, at][None]
-            sampled = jnp.sum(jnp.sum(along, axis=1) * wx, axis=0, keepdims=True)
-            force = target[c : c + 1] - sampled
-            fx_ref[c, :, at] = force * wx
-            for k in range(force_ref.shape[0]):
-                force_ref[k, c : c + 1, at] = force
-    pad = boxh_ref.shape[0] // 6
-    base = 0
-    for y in (0, cells_y - 1):
-        for c in range(3):
-            rows = fx_ref[c] * wy_ref[y : y + 1, :]
-            rows = jnp.concatenate([rows, jnp.zeros((pad - cells_x, slots), f32)], axis=0)
-            high, low = halves(rows)
-            boxh_ref[base : base + pad] = high
-            boxl_ref[base : base + pad] = low
-            base += pad
-    spread = dot3(boxh_ref[...], boxl_ref[...], wzh_ref[...], wzl_ref[...], NT)
+
+    def sample(planes):
+        def step(t, _):
+            at = span(t, tile)
+            rows = pl.ds(pl.multiple_of(start_ref[t] * cells_y, cells_y), planes * cells_y)
+            wx = rel_ref[:, at]
+            wy = wy_ref[:, at]
+            for c in range(3):
+                along = dot3(high_ref[c, rows, :], low_ref[c, rows, :], wzh_ref[:, at], wzl_ref[:, at])
+                along = along.reshape(planes, cells_y, tile) * wy[None]
+                sampled = jnp.sum(jnp.sum(along, axis=1) * wx[0:planes], axis=0, keepdims=True)
+                force = goal_ref[c, 0:1, at] - sampled
+                fx_ref[c, :, at] = force * wx
+                goal_ref[c, 0:1, at] = force
+
+        lax.fori_loop(0, count, step, None)
+
+    if quartered:
+        pl.when(fits)(lambda: sample(band))
+        pl.when(jnp.logical_not(fits))(lambda: sample(cells_x))
+    else:
+        sample(cells_x)
+    forces = [goal_ref[c, 0:1, :] for c in range(3)]
+    if quartered:
+        lane = lax.broadcasted_iota(i32, (8, capacity), 1)
+        mixed = jnp.concatenate(forces + [jnp.zeros((5, slots), f32)], axis=0)
+        per = capacity // width
+        own = []
+        for k in range(n_stream):
+            piece = jnp.zeros((8, capacity), f32)
+            for t in range(count):
+                base = t * tile + k // per * capacity
+                moved = pltpu.roll(mixed[:, base : base + capacity], (t - k % per) * width % capacity, 1)
+                piece = jnp.where((lane >= t * width) & (lane < (t + 1) * width), moved, piece)
+            own.append(piece)
+        natural = jnp.concatenate(own, axis=1)[0:3]
+    else:
+        natural = jnp.concatenate(forces, axis=0)
+    for k in range(force_ref.shape[0]):
+        force_ref[k] = natural
+    face_ref[...] = jnp.zeros_like(face_ref)
+
+    def edges(t, _):
+        at = span(t, tile)
+        wx = wx_ref[:, at]
+        wy = wy_ref[:, at]
+        rows = [goal_ref[c, 0:1, at] * wx * wy[y : y + 1] for y in (0, cells_y - 1) for c in range(3)]
+        high, low = halves(jnp.concatenate(rows, axis=0))
+        face_ref[...] += dot3(high, low, wzh_ref[:, at], wzl_ref[:, at], NT)
+
+    lax.fori_loop(0, count, edges, None)
     base = 0
     for y, ref in ((0, y0_ref), (cells_y - 1, y1_ref)):
         for c in range(3):
-            ref[c] = cell_ref[c, :, y, :] + spread[base : base + cells_x]
+            ref[c] = cell_ref[c, :, y, :] + face_ref[base : base + cells_x]
             base += pad
     for store in stores:
         store.wait()
 
 
 def spread_kernel(
-    velocity_hbm, wzh_ref, wzl_ref, wy_ref, fx_ref, rhs_hbm, boxh_ref, boxl_ref, cell_ref, in_sem, out_sem,
+    tile, quartered, band, velocity_hbm, wzh_ref, wzl_ref, wy_ref, fx_ref, start_ref, rhs_hbm, cell_ref, in_sem, out_sem,
 ):
     _, cells_x, cells_y, cells_z = velocity_hbm.shape
+    count = wy_ref.shape[1] // tile
     loads = [pltpu.make_async_copy(velocity_hbm.at[c], cell_ref.at[c], in_sem.at[c]) for c in range(3)]
     stores = [pltpu.make_async_copy(cell_ref.at[c], rhs_hbm.at[c], out_sem.at[c]) for c in range(3)]
     for load in loads:
         load.start()
-    wy = wy_ref[...]
-    for c in range(3):
-        for x in range(cells_x):
-            high, low = halves(fx_ref[c, x : x + 1, :] * wy)
-            boxh_ref[x * cells_y : (x + 1) * cells_y] = high
-            boxl_ref[x * cells_y : (x + 1) * cells_y] = low
-        spread = dot3(boxh_ref[...], boxl_ref[...], wzh_ref[...], wzl_ref[...], NT)
-        loads[c].wait()
-        cell_ref[c] = cell_ref[c] + spread.reshape(cells_x, cells_y, cells_z)
-        stores[c].start()
+    for load in loads:
+        load.wait()
+
+    def spread(planes):
+        def step(t, _):
+            at = span(t, tile)
+            rows = pl.ds(start_ref[t], planes)
+            wy = wy_ref[:, at]
+            for c in range(3):
+                boxes = jnp.concatenate([fx_ref[c, x : x + 1, at] * wy for x in range(planes)], axis=0)
+                high, low = halves(boxes)
+                added = dot3(high, low, wzh_ref[:, at], wzl_ref[:, at], NT)
+                cell_ref[c, rows] += added.reshape(planes, cells_y, cells_z)
+
+        lax.fori_loop(0, count, step, None)
+
+    if quartered:
+        fits = start_ref[count] == 1
+        pl.when(fits)(lambda: spread(band))
+        pl.when(jnp.logical_not(fits))(lambda: spread(cells_x))
+    else:
+        spread(cells_x)
+    for store in stores:
+        store.start()
     for store in stores:
         store.wait()
-
-
-def quarter(marks_ref, side, index, width):
-    lane = lax.broadcasted_iota(i32, marks_ref.shape[2:], 1)
-    capacity = marks_ref.shape[3]
-    per = capacity // width
-    out = []
-    for base in range(0, marks_ref.shape[1], per):
-        piece = jnp.zeros(marks_ref.shape[2:], f32)
-        for k in range(per):
-            moved = pltpu.roll(marks_ref[side, base + k], lax.rem(capacity + (k - index) * width, capacity), 1)
-            piece = jnp.where((lane >= k * width) & (lane < (k + 1) * width), moved, piece)
-        out.append(piece)
-    return jnp.concatenate(out, axis=1)
 
 
 def finish_kernel(
@@ -247,7 +329,8 @@
             per = capacity // width
 
             def step(index, _):
-                data = quarter(marks_ref, side, index if side else per - 1 - index, width)
+                at = index if side else per - 1 - index
+                data = quarter(lambda k: marks_ref[side, k], n_stream, capacity, at, width)
                 add(data, data[0:3])
 
             lax.fori_loop(0, lax.div(reach + width - 1, width), step, None)
@@ -295,6 +378,7 @@
     chunked = capacity % 128 == 0
     tile = 256 if slots % 256 == 0 else 128
     quartered = capacity == 128 and tile % n_stream == 0 and capacity % (tile // n_stream) == 0
+    band = min(cells_x, SPAN + (cells_x - SPAN + 1) // 2)
     shape = jax.ShapeDtypeStruct
     sems = pltpu.SemaphoreType.DMA
 
@@ -329,27 +413,30 @@
     right = lax.ppermute(arrived, "gx", down_x)
 
     pad = -(-cells_x // 16) * 16
-    force, wzh, wzl, wy, fx, y0, y1 = pl.pallas_call(
-        functools.partial(sample_kernel, tile),
+    force, wzh, wzl, wy, fx, y0, y1, starts = pl.pallas_call(
+        functools.partial(sample_kernel, tile, n_stream, quartered, band),
         out_shape=(
             shape((n_stream, 3, slots), f32),
             shape((cells_z, slots), bf16),
             shape((cells_z, slots), bf16),
             shape((cells_y, slots), f32),
-            shape((3, cells_x, slots), f32),
+            shape((3, pad, slots), f32),
             shape((3, cells_x, cells_z), f32),
             shape((3, cells_x, cells_z), f32),
+            shape((slots // tile + 1,), i32),
         ),
         in_specs=[VMEM, HBM],
-        out_specs=(VMEM, HBM, HBM, VMEM, VMEM, VMEM, VMEM),
+        out_specs=(VMEM, HBM, HBM, VMEM, VMEM, VMEM, VMEM, SMEM),
         scratch_shapes=[
             pltpu.VMEM(velocity.shape, f32),
             pltpu.VMEM((3, block, cells_z), bf16),
             pltpu.VMEM((3, block, cells_z), bf16),
             pltpu.VMEM((cells_z, slots), bf16),
             pltpu.VMEM((cells_z, slots), bf16),
-            pltpu.VMEM((6 * pad, slots), bf16),
-            pltpu.VMEM((6 * pad, slots), bf16),
+            pltpu.VMEM((pad, slots), f32),
+            pltpu.VMEM((pad, slots), f32),
+            pltpu.VMEM((3, 8, slots), f32),
+            pltpu.VMEM((6 * pad, cells_z), f32),
             sems((3,)),
             sems((2,)),
         ],
@@ -367,20 +454,18 @@
         held = held.transpose(1, 0, 2).reshape(3, slots)
 
     rhs = pl.pallas_call(
-        spread_kernel,
+        functools.partial(spread_kernel, tile, quartered, band),
         out_shape=shape(velocity.shape, f32),
-        in_specs=[HBM, VMEM, VMEM, VMEM, VMEM],
+        in_specs=[HBM, VMEM, VMEM, VMEM, VMEM, SMEM],
         out_specs=HBM,
         scratch_shapes=[
-            pltpu.VMEM((block, slots), bf16),
-            pltpu.VMEM((block, slots), bf16),
             pltpu.VMEM(velocity.shape, f32),
             sems((3,)),
             sems((3,)),
         ],
         cost_estimate=pl.CostEstimate(flops=18 * block * slots * cells_z, bytes_accessed=24 * block * cells_z, transcendentals=0),
         name="spread",
-    )(velocity, wzh, wzl, wy, fx)
+    )(velocity, wzh, wzl, wy, fx, starts)
 
     return pl.pallas_call(
         functools.partial(finish_kernel, tile, n_stream, n_wall, chunked, quartered),

time: 53.6 us -> 52.7 us (0.983)
  Pallas kernels: 26 us -> 25 us
    pallas_call x2, Pallas kernels: 17.6 us -> 16.7 us  [the longest x1 8.6 us: per_device(): pl.pallas_call(functools.partial(sample_kernel, tile, n_stream, quartered...]
  transfers between devices with their start and end apart: 8 -> 8, of which waited for: 1 -> 1; matrix products, arithmetic and copies ran while one was open for 0% -> 0% of each run, Pallas kernels for 33% -> 32%
where the time goes in v6:
time: 52.7 us; the launch traced here: 52.1 us
  Pallas kernels  25 us (47%)
  starting transfers between devices  22.4 us (43%)
  waiting for transfers between devices  2.52 us (5%)
  local copies, waits for them, and re-layouts  1.38 us (3%)
  between operations  0.78 us (1%)
    pallas_call x1, Pallas kernels, per_device(): pl.pallas_call(functools.partial(sample_kernel, tile, n_stream, quartered...  8.6 us
    pallas_call x1, Pallas kernels, per_device(): pl.pallas_call(functools.partial(spread_kernel, tile, quartered, band), o...  8.09 us
    pallas_call x1, Pallas kernels, per_device(): pl.pallas_call(functools.partial(finish_kernel, tile, n_stream, n_wall, c...  5.7 us
    all_to_all x1, starting transfers between devices, per_device(): lax.all_to_all(outgoing, 'gx', split_axis=0, concat_axis=0, tiled=True)  4.88 us
    ppermute x1, starting transfers between devices, per_device(): from_x1 = lax.ppermute(x0, 'gx', down_x)  4.72 us
    ppermute x1, starting transfers between devices, per_device(): right = lax.ppermute(arrived, 'gx', down_x)  4.61 us
    all_to_all x1, starting transfers between devices, per_device(): given = lax.all_to_all(force, 'gx', split_axis=0, concat_axis=0, tiled=True)  3.38 us
    ppermute x1, starting transfers between devices, per_device(): from_x0 = lax.ppermute(x1, 'gx', up_x)  3.05 us
  transfers between devices with their start and end apart: 8, of which 1 were waited for; matrix products, arithmetic and copies ran while one was open for 0% of the time, Pallas kernels for 32%

profile of v6, /device:TPU:0, one launch (start us, length us, event | category | flops | bytes accessed | tf_op | source)
XLA Modules:
  0.0 52.1 jit_solution(2167167891327934802)
XLA Ops:
  0.6 2.6 %pack.1 = (f32[8,24,128]{2,1,0:T(8,128)}, s32[1,512]{1,0:T(1,128)}, f32[3,64,256]{2,1,0:T(8,128)}, f32[3,64,256]{2,1,0:T(8,128)}) custom-call(s32[1,512]{1,0:T(1,128)} %bitcast.1, f32[3,512]{1,0:T(4,128)} %target_ref.1, f32[3,6,512]{2,1,0:T(8,128)} %weights_ref.1, s32[3,512]{1,0:T(4,128)} %corners_ref.1, f32[3,12,64,256]{3,2,1,0:T(8,128)} %velocity_hbm.5), custom_call_target="tpu_custom_call" | custom-call | tf_op jit(solution)/shard_map/pack/pallas_call | solution.py:386
  3.3 3.0 %collective-permute-start = (f32[3,64,256]{2,1,0:T(8,128)}, f32[3,64,256]{2,1,0:T(8,128)S(1)}, u32[]{:S(2)}, u32[]{:S(2)}) collective-permute-start(f32[3,64,256]{2,1,0:T(8,128)} %get-tuple-element.20), channel_id=1, source_target_pairs={{0,4},{4,8},{8,12},{12,16},{16,20},{20,24},{24,28},{28,0},{1,5},{5... | collective-permute-start | bytes 589832 | tf_op jit(solution)/shard_map/ppermute | solution.py:410
  6.3 4.9 %all-to-all-start = ((f32[8,24,128]{2,1,0:T(8,128)}), f32[8,24,128]{2,1,0:T(8,128)S(1)}, u32[]{:S(2)}, u32[]{:S(2)}) async-start(f32[8,24,128]{2,1,0:T(8,128)} %get-tuple-element.14), calls=%async_computation | async-start | bytes 196608 | tf_op jit(solution)/shard_map/all_to_all | solution.py:400
  11.2 4.7 %collective-permute-start.1 = (f32[3,64,256]{2,1,0:T(8,128)}, f32[3,64,256]{2,1,0:T(8,128)S(1)}, u32[]{:S(2)}, u32[]{:S(2)}) collective-permute-start(f32[3,64,256]{2,1,0:T(8,128)} %get-tuple-element.21), channel_id=1, source_target_pairs={{4,0},{8,4},{12,8},{16,12},{20,16},{24,20},{28,24},{0,28},{5,1},{9... | collective-permute-start | bytes 589832 | tf_op jit(solution)/shard_map/ppermute | solution.py:411
  15.9 2.5 %all-to-all-done.arrived_ref = f32[8,24,128]{2,1,0:T(8,128)S(1)} async-done(((f32[8,24,128]{2,1,0:T(8,128)}), f32[8,24,128]{2,1,0:T(8,128)S(1)}, u32[]{:S(2)}, u32[]{:S(2)}) %all-to-all-start) | async-done | bytes 98336 | tf_op jit(solution)/shard_map/all_to_all | solution.py:400
  18.4 0.0 copy-start.1
  18.4 0.6 %copy-done.1 = f32[8,24,128]{2,1,0:T(8,128)} copy-done((f32[8,24,128]{2,1,0:T(8,128)}, f32[8,24,128]{2,1,0:T(8,128)S(1)}, u32[]{:S(2)}) %copy-start.1) | copy-done | bytes 98328
  19.1 8.6 %sample.1 = (f32[8,3,1024]{2,1,0:T(4,128)}, bf16[256,1024]{1,0:T(8,128)(2,1)}, bf16[256,1024]{1,0:T(8,128)(2,1)}, f32[64,1024]{1,0:T(8,128)}, f32[3,16,1024]{2,1...) custom-call(f32[8,24,128]{2,1,0:T(8,128)} %copy-done.1, f32[3,12,64,256]{3,2,1,0:T(8,128)} %velocity_hbm.5), custom_call_target="tpu_custom_call" | custom-call | tf_op jit(solution)/shard_map/sample/pallas_call | solution.py:416
  27.7 3.4 %all-to-all-start.1 = ((f32[8,3,1024]{2,1,0:T(4,128)}), f32[8,3,1024]{2,1,0:T(4,128)S(1)}, u32[]{:S(2)}, u32[]{:S(2)}) async-start(f32[8,3,1024]{2,1,0:T(4,128)} %get-tuple-element.24), calls=%async_computation.1 | async-start | bytes 262144 | tf_op jit(solution)/shard_map/all_to_all | solution.py:449
  31.1 0.1 collective-permute-start.2
  31.1 1.7 %collective-permute-start.3 = (f32[3,12,256]{2,1,0:T(8,128)}, f32[3,12,256]{2,1,0:T(8,128)S(1)}, u32[]{:S(2)}, u32[]{:S(2)}) collective-permute-start(f32[3,12,256]{2,1,0:T(8,128)} %get-tuple-element.23), channel_id=1, source_target_pairs={{1,0},{2,1},{3,2},{0,3},{5,4},{6,5},{7,6},{4,7},{9,8},{10,9},{11,1... | collective-permute-start | bytes 110600 | tf_op jit(solution)/shard_map/ppermute | solution.py:448
  32.9 4.6 %collective-permute-start.5 = (f32[8,24,128]{2,1,0:T(8,128)}, f32[8,24,128]{2,1,0:T(8,128)S(1)}, u32[]{:S(2)}, u32[]{:S(2)}) collective-permute-start(f32[8,24,128]{2,1,0:T(8,128)} %copy-done.1), channel_id=1, source_target_pairs={{4,0},{8,4},{12,8},{16,12},{20,16},{24,20},{28,24},{0,28},{5,1},{9... | collective-permute-start | bytes 294920 | tf_op jit(solution)/shard_map/ppermute | solution.py:413
  37.5 0.0 collective-permute-done.x0_ref
  37.5 0.0 copy-start.2
  37.5 0.0 collective-permute-start.4
  37.5 8.1 %spread.1.rhs_hbm = f32[3,12,64,256]{3,2,1,0:T(8,128)} custom-call(f32[3,12,64,256]{3,2,1,0:T(8,128)} %velocity_hbm.5, bf16[256,1024]{1,0:T(8,128)(2,1)} %get-tuple-element.15.wzh_ref, bf16[256,1024]{1,0:T(8,128)(2,1)} %get-tuple-element.16.wzl_ref, f32[64,1024]{1,0:T(8,128)} %get-tuple-element.17.wy_ref, f32[3,16,1024]{2,1,0:T(8,128)} %get-tuple-element.18.fx_ref, ...), custom_call_target="tpu_custom_call" | custom-call | flops 3623878656 | bytes 4718592 | tf_op jit(solution)/shard_map/spread/pallas_call | solution.py:456
  45.6 0.0 copy-done.2
  45.6 0.0 collective-permute-done.1.x1_ref
  45.6 0.0 copy-start.3
  45.6 0.0 collective-permute-done.2.y0_ref
  45.6 0.0 copy-start.6
  45.6 0.0 collective-permute-done.3.y1_ref
  45.6 0.0 copy-start.7
  45.7 0.0 collective-permute-done.5.right_ref
  45.7 0.0 copy-start.4
  45.7 0.0 collective-permute-done.4.left_ref
  45.7 0.0 copy-start.5
  45.7 0.0 all-to-all-done.1.given_ref
  45.7 0.0 copy-start
  45.7 0.6 %copy-done.3 = f32[3,64,256]{2,1,0:T(8,128)} copy-done((f32[3,64,256]{2,1,0:T(8,128)}, f32[3,64,256]{2,1,0:T(8,128)S(1)}, u32[]{:S(2)}) %copy-start.3) | copy-done | bytes 196632
  46.3 0.0 copy-done.6
  46.3 0.0 copy-done.7
  46.3 0.0 copy-done.4
  46.4 0.0 copy-done.5
  46.4 0.0 copy-done
  46.4 5.7 %finish.1 = (f32[3,12,64,256]{3,2,1,0:T(8,128)}, f32[3,512]{1,0:T(4,128)}) custom-call(f32[3,12,64,256]{3,2,1,0:T(8,128)} %spread.1.rhs_hbm, f32[3,64,256]{2,1,0:T(8,128)} %copy-done.2, f32[3,64,256]{2,1,0:T(8,128)} %copy-done.3, f32[3,12,256]{2,1,0:T(8,128)} %copy-done.6, f32[3,12,256]{2,1,0:T(8,128)} %copy-done.7, f32[8,24,128]{2,1,0:T(8,128)} %copy-done.5, ...), custom_call_target="tpu_custom_call" | custom-call | tf_op jit(solution)/shard_map/finish/pallas_call | solution.py:470
Async XLA Ops:
  3.3 34.2 %collective-permute-start = (f32[3,64,256]{2,1,0:T(8,128)}, f32[3,64,256]{2,1,0:T(8,128)S(1)}, u32[]{:S(2)}, u32[]{:S(2)}) collective-permute-start(f32[3,64,256]{2,1,0:T(8,128)} %get-tuple-element.20), channel_id=1, source_target_pairs={{0,4},{4,8},{8,12},{12,16},{16,20},{20,24},{24,28},{28,0},{1,5},{5... | collective-permute-start | bytes 589832 | tf_op jit(solution)/shard_map/ppermute | solution.py:410
  6.3 12.1 %all-to-all-start = ((f32[8,24,128]{2,1,0:T(8,128)}), f32[8,24,128]{2,1,0:T(8,128)S(1)}, u32[]{:S(2)}, u32[]{:S(2)}) async-start(f32[8,24,128]{2,1,0:T(8,128)} %get-tuple-element.14), calls=%async_computation | async-start | bytes 196608 | tf_op jit(solution)/shard_map/all_to_all | solution.py:400
  11.2 34.4 %collective-permute-start.1 = (f32[3,64,256]{2,1,0:T(8,128)}, f32[3,64,256]{2,1,0:T(8,128)S(1)}, u32[]{:S(2)}, u32[]{:S(2)}) collective-permute-start(f32[3,64,256]{2,1,0:T(8,128)} %get-tuple-element.21), channel_id=1, source_target_pairs={{4,0},{8,4},{12,8},{16,12},{20,16},{24,20},{28,24},{0,28},{5,1},{9... | collective-permute-start | bytes 589832 | tf_op jit(solution)/shard_map/ppermute | solution.py:411
  18.4 0.6 %copy-start.1 = (f32[8,24,128]{2,1,0:T(8,128)}, f32[8,24,128]{2,1,0:T(8,128)S(1)}, u32[]{:S(2)}) copy-start(f32[8,24,128]{2,1,0:T(8,128)S(1)} %all-to-all-done.arrived_ref) | copy-start | bytes 294916
  27.7 18.0 %all-to-all-start.1 = ((f32[8,3,1024]{2,1,0:T(4,128)}), f32[8,3,1024]{2,1,0:T(4,128)S(1)}, u32[]{:S(2)}, u32[]{:S(2)}) async-start(f32[8,3,1024]{2,1,0:T(4,128)} %get-tuple-element.24), calls=%async_computation.1 | async-start | bytes 262144 | tf_op jit(solution)/shard_map/all_to_all | solution.py:449
  31.1 14.5 %collective-permute-start.2 = (f32[3,12,256]{2,1,0:T(8,128)}, f32[3,12,256]{2,1,0:T(8,128)S(1)}, u32[]{:S(2)}, u32[]{:S(2)}) collective-permute-start(f32[3,12,256]{2,1,0:T(8,128)} %get-tuple-element.22), channel_id=1, source_target_pairs={{0,1},{1,2},{2,3},{3,0},{4,5},{5,6},{6,7},{7,4},{8,9},{9,10},{10,1... | collective-permute-start | bytes 110600 | tf_op jit(solution)/shard_map/ppermute | solution.py:447
  31.1 14.5 %collective-permute-start.3 = (f32[3,12,256]{2,1,0:T(8,128)}, f32[3,12,256]{2,1,0:T(8,128)S(1)}, u32[]{:S(2)}, u32[]{:S(2)}) collective-permute-start(f32[3,12,256]{2,1,0:T(8,128)} %get-tuple-element.23), channel_id=1, source_target_pairs={{1,0},{2,1},{3,2},{0,3},{5,4},{6,5},{7,6},{4,7},{9,8},{10,9},{11,1... | collective-permute-start | bytes 110600 | tf_op jit(solution)/shard_map/ppermute | solution.py:448
  32.9 12.8 %collective-permute-start.5 = (f32[8,24,128]{2,1,0:T(8,128)}, f32[8,24,128]{2,1,0:T(8,128)S(1)}, u32[]{:S(2)}, u32[]{:S(2)}) collective-permute-start(f32[8,24,128]{2,1,0:T(8,128)} %copy-done.1), channel_id=1, source_target_pairs={{4,0},{8,4},{12,8},{16,12},{20,16},{24,20},{28,24},{0,28},{5,1},{9... | collective-permute-start | bytes 294920 | tf_op jit(solution)/shard_map/ppermute | solution.py:413
  37.5 8.1 %copy-start.2 = (f32[3,64,256]{2,1,0:T(8,128)}, f32[3,64,256]{2,1,0:T(8,128)S(1)}, u32[]{:S(2)}) copy-start(f32[3,64,256]{2,1,0:T(8,128)S(1)} %collective-permute-done.x0_ref) | copy-start | bytes 589828
  37.5 8.2 %collective-permute-start.4 = (f32[8,24,128]{2,1,0:T(8,128)}, f32[8,24,128]{2,1,0:T(8,128)S(1)}, u32[]{:S(2)}, u32[]{:S(2)}) collective-permute-start(f32[8,24,128]{2,1,0:T(8,128)} %copy-done.1), channel_id=1, source_target_pairs={{0,4},{4,8},{8,12},{12,16},{16,20},{20,24},{24,28},{28,0},{1,5},{5... | collective-permute-start | bytes 294920 | tf_op jit(solution)/shard_map/ppermute | solution.py:412
  45.6 0.7 %copy-start.3 = (f32[3,64,256]{2,1,0:T(8,128)}, f32[3,64,256]{2,1,0:T(8,128)S(1)}, u32[]{:S(2)}) copy-start(f32[3,64,256]{2,1,0:T(8,128)S(1)} %collective-permute-done.1.x1_ref) | copy-start | bytes 589828
  45.6 0.7 %copy-start.6 = (f32[3,12,256]{2,1,0:T(8,128)}, f32[3,12,256]{2,1,0:T(8,128)S(1)}, u32[]{:S(2)}) copy-start(f32[3,12,256]{2,1,0:T(8,128)S(1)} %collective-permute-done.2.y0_ref) | copy-start | bytes 110596
  45.6 0.7 %copy-start.7 = (f32[3,12,256]{2,1,0:T(8,128)}, f32[3,12,256]{2,1,0:T(8,128)S(1)}, u32[]{:S(2)}) copy-start(f32[3,12,256]{2,1,0:T(8,128)S(1)} %collective-permute-done.3.y1_ref) | copy-start | bytes 110596
  45.7 0.7 %copy-start.4 = (f32[8,24,128]{2,1,0:T(8,128)}, f32[8,24,128]{2,1,0:T(8,128)S(1)}, u32[]{:S(2)}) copy-start(f32[8,24,128]{2,1,0:T(8,128)S(1)} %collective-permute-done.5.right_ref) | copy-start | bytes 294916
  45.7 0.7 %copy-start.5 = (f32[8,24,128]{2,1,0:T(8,128)}, f32[8,24,128]{2,1,0:T(8,128)S(1)}, u32[]{:S(2)}) copy-start(f32[8,24,128]{2,1,0:T(8,128)S(1)} %collective-permute-done.4.left_ref) | copy-start | bytes 294916
  45.7 0.7 %copy-start = (f32[8,3,1024]{2,1,0:T(4,128)}, f32[8,3,1024]{2,1,0:T(4,128)S(1)}, u32[]{:S(2)}) copy-start(f32[8,3,1024]{2,1,0:T(4,128)S(1)} %all-to-all-done.1.given_ref) | copy-start | bytes 294916

commit v7 on v6

--- a/solution.py
+++ b/solution.py
@@ -250,7 +250,7 @@
 
 
 def spread_kernel(
-    tile, quartered, band, velocity_hbm, wzh_ref, wzl_ref, wy_ref, fx_ref, start_ref, rhs_hbm, cell_ref, in_sem, out_sem,
+    tile, quartered, band, velocity_hbm, wzh_ref, wzl_ref, wy_ref, fx_ref, start_ref, rhs_hbm, cell_ref, sum_ref, in_sem, out_sem,
 ):
     _, cells_x, cells_y, cells_z = velocity_hbm.shape
     count = wy_ref.shape[1] // tile
@@ -258,8 +258,7 @@
     stores = [pltpu.make_async_copy(cell_ref.at[c], rhs_hbm.at[c], out_sem.at[c]) for c in range(3)]
     for load in loads:
         load.start()
-    for load in loads:
-        load.wait()
+    sum_ref[...] = jnp.zeros_like(sum_ref)
 
     def spread(planes):
         def step(t, _):
@@ -270,7 +269,7 @@
                 boxes = jnp.concatenate([fx_ref[c, x : x + 1, at] * wy for x in range(planes)], axis=0)
                 high, low = halves(boxes)
                 added = dot3(high, low, wzh_ref[:, at], wzl_ref[:, at], NT)
-                cell_ref[c, rows] += added.reshape(planes, cells_y, cells_z)
+                sum_ref[c, rows] += added.reshape(planes, cells_y, cells_z)
 
         lax.fori_loop(0, count, step, None)
 
@@ -280,8 +279,10 @@
         pl.when(jnp.logical_not(fits))(lambda: spread(cells_x))
     else:
         spread(cells_x)
-    for store in stores:
-        store.start()
+    for c in range(3):
+        loads[c].wait()
+        cell_ref[c] += sum_ref[c]
+        stores[c].start()
     for store in stores:
         store.wait()
 
@@ -460,6 +461,7 @@
         out_specs=HBM,
         scratch_shapes=[
             pltpu.VMEM(velocity.shape, f32),
+            pltpu.VMEM(velocity.shape, f32),
             sems((3,)),
             sems((3,)),
         ],

time: 52.7 us -> 51.9 us (0.985)
  Pallas kernels: 25 us -> 23.7 us
  waiting for transfers between devices: 2.52 us -> 3.22 us
    pallas_call x1, Pallas kernels: 8.09 us -> 6.72 us  [per_device(): pl.pallas_call(functools.partial(spread_kernel, tile, quartered, band), o...]
    ppermute x1, waiting for transfers between devices: 0.01 us -> 0.7 us  [per_device(): left = lax.ppermute(arrived, 'gx', up_x)]
  transfers between devices with their start and end apart: 8 -> 8, of which waited for: 1 -> 2; matrix products, arithmetic and copies ran while one was open for 0% -> 0% of each run, Pallas kernels for 32% -> 30%
where the time goes in v7:
time: 51.9 us; the launch traced here: 51.4 us
  Pallas kernels  23.7 us (46%)
  starting transfers between devices  22.4 us (43%)
  waiting for transfers between devices  3.22 us (6%)
  local copies, waits for them, and re-layouts  1.33 us (3%)
  between operations  0.78 us (2%)
    pallas_call x1, Pallas kernels, per_device(): pl.pallas_call(functools.partial(sample_kernel, tile, n_stream, quartered...  8.6 us
    pallas_call x1, Pallas kernels, per_device(): pl.pallas_call(functools.partial(spread_kernel, tile, quartered, band), o...  6.72 us
    pallas_call x1, Pallas kernels, per_device(): pl.pallas_call(functools.partial(finish_kernel, tile, n_stream, n_wall, c...  5.69 us
    all_to_all x1, starting transfers between devices, per_device(): lax.all_to_all(outgoing, 'gx', split_axis=0, concat_axis=0, tiled=True)  4.88 us
    ppermute x1, starting transfers between devices, per_device(): from_x1 = lax.ppermute(x0, 'gx', down_x)  4.72 us
    ppermute x1, starting transfers between devices, per_device(): right = lax.ppermute(arrived, 'gx', down_x)  4.61 us
    all_to_all x1, starting transfers between devices, per_device(): given = lax.all_to_all(force, 'gx', split_axis=0, concat_axis=0, tiled=True)  3.38 us
    ppermute x1, starting transfers between devices, per_device(): from_x0 = lax.ppermute(x1, 'gx', up_x)  3.05 us
  transfers between devices with their start and end apart: 8, of which 2 were waited for; matrix products, arithmetic and copies ran while one was open for 0% of the time, Pallas kernels for 30%

profile of v7, /device:TPU:0, one launch (start us, length us, event | category | flops | bytes accessed | tf_op | source)
XLA Modules:
  0.0 51.4 jit_solution(12878694155883865546)
XLA Ops:
  0.6 2.6 %pack.1 = (f32[8,24,128]{2,1,0:T(8,128)}, s32[1,512]{1,0:T(1,128)}, f32[3,64,256]{2,1,0:T(8,128)}, f32[3,64,256]{2,1,0:T(8,128)}) custom-call(s32[1,512]{1,0:T(1,128)} %bitcast.1, f32[3,512]{1,0:T(4,128)} %target_ref.1, f32[3,6,512]{2,1,0:T(8,128)} %weights_ref.1, s32[3,512]{1,0:T(4,128)} %corners_ref.1, f32[3,12,64,256]{3,2,1,0:T(8,128)} %velocity_hbm.5), custom_call_target="tpu_custom_call" | custom-call | tf_op jit(solution)/shard_map/pack/pallas_call | solution.py:387
  3.3 3.0 %collective-permute-start = (f32[3,64,256]{2,1,0:T(8,128)}, f32[3,64,256]{2,1,0:T(8,128)S(1)}, u32[]{:S(2)}, u32[]{:S(2)}) collective-permute-start(f32[3,64,256]{2,1,0:T(8,128)} %get-tuple-element.20), channel_id=1, source_target_pairs={{0,4},{4,8},{8,12},{12,16},{16,20},{20,24},{24,28},{28,0},{1,5},{5... | collective-permute-start | bytes 589832 | tf_op jit(solution)/shard_map/ppermute | solution.py:411
  6.3 4.9 %all-to-all-start = ((f32[8,24,128]{2,1,0:T(8,128)}), f32[8,24,128]{2,1,0:T(8,128)S(1)}, u32[]{:S(2)}, u32[]{:S(2)}) async-start(f32[8,24,128]{2,1,0:T(8,128)} %get-tuple-element.14), calls=%async_computation | async-start | bytes 196608 | tf_op jit(solution)/shard_map/all_to_all | solution.py:401
  11.2 4.7 %collective-permute-start.1 = (f32[3,64,256]{2,1,0:T(8,128)}, f32[3,64,256]{2,1,0:T(8,128)S(1)}, u32[]{:S(2)}, u32[]{:S(2)}) collective-permute-start(f32[3,64,256]{2,1,0:T(8,128)} %get-tuple-element.21), channel_id=1, source_target_pairs={{4,0},{8,4},{12,8},{16,12},{20,16},{24,20},{28,24},{0,28},{5,1},{9... | collective-permute-start | bytes 589832 | tf_op jit(solution)/shard_map/ppermute | solution.py:412
  15.9 2.5 %all-to-all-done.arrived_ref = f32[8,24,128]{2,1,0:T(8,128)S(1)} async-done(((f32[8,24,128]{2,1,0:T(8,128)}), f32[8,24,128]{2,1,0:T(8,128)S(1)}, u32[]{:S(2)}, u32[]{:S(2)}) %all-to-all-start) | async-done | bytes 98336 | tf_op jit(solution)/shard_map/all_to_all | solution.py:401
  18.4 0.0 copy-start.1
  18.4 0.6 %copy-done.1 = f32[8,24,128]{2,1,0:T(8,128)} copy-done((f32[8,24,128]{2,1,0:T(8,128)}, f32[8,24,128]{2,1,0:T(8,128)S(1)}, u32[]{:S(2)}) %copy-start.1) | copy-done | bytes 98328
  19.1 8.6 %sample.1 = (f32[8,3,1024]{2,1,0:T(4,128)}, bf16[256,1024]{1,0:T(8,128)(2,1)}, bf16[256,1024]{1,0:T(8,128)(2,1)}, f32[64,1024]{1,0:T(8,128)}, f32[3,16,1024]{2,1...) custom-call(f32[8,24,128]{2,1,0:T(8,128)} %copy-done.1, f32[3,12,64,256]{3,2,1,0:T(8,128)} %velocity_hbm.5), custom_call_target="tpu_custom_call" | custom-call | tf_op jit(solution)/shard_map/sample/pallas_call | solution.py:417
  27.7 3.4 %all-to-all-start.1 = ((f32[8,3,1024]{2,1,0:T(4,128)}), f32[8,3,1024]{2,1,0:T(4,128)S(1)}, u32[]{:S(2)}, u32[]{:S(2)}) async-start(f32[8,3,1024]{2,1,0:T(4,128)} %get-tuple-element.24), calls=%async_computation.1 | async-start | bytes 262144 | tf_op jit(solution)/shard_map/all_to_all | solution.py:450
  31.1 0.1 collective-permute-start.2
  31.1 1.7 %collective-permute-start.3 = (f32[3,12,256]{2,1,0:T(8,128)}, f32[3,12,256]{2,1,0:T(8,128)S(1)}, u32[]{:S(2)}, u32[]{:S(2)}) collective-permute-start(f32[3,12,256]{2,1,0:T(8,128)} %get-tuple-element.23), channel_id=1, source_target_pairs={{1,0},{2,1},{3,2},{0,3},{5,4},{6,5},{7,6},{4,7},{9,8},{10,9},{11,1... | collective-permute-start | bytes 110600 | tf_op jit(solution)/shard_map/ppermute | solution.py:449
  32.9 4.6 %collective-permute-start.5 = (f32[8,24,128]{2,1,0:T(8,128)}, f32[8,24,128]{2,1,0:T(8,128)S(1)}, u32[]{:S(2)}, u32[]{:S(2)}) collective-permute-start(f32[8,24,128]{2,1,0:T(8,128)} %copy-done.1), channel_id=1, source_target_pairs={{4,0},{8,4},{12,8},{16,12},{20,16},{24,20},{28,24},{0,28},{5,1},{9... | collective-permute-start | bytes 294920 | tf_op jit(solution)/shard_map/ppermute | solution.py:414
  37.5 0.0 collective-permute-done.x0_ref
  37.5 0.0 copy-start.2
  37.5 0.0 collective-permute-start.4
  37.5 6.7 %spread.1.rhs_hbm = f32[3,12,64,256]{3,2,1,0:T(8,128)} custom-call(f32[3,12,64,256]{3,2,1,0:T(8,128)} %velocity_hbm.5, bf16[256,1024]{1,0:T(8,128)(2,1)} %get-tuple-element.15.wzh_ref, bf16[256,1024]{1,0:T(8,128)(2,1)} %get-tuple-element.16.wzl_ref, f32[64,1024]{1,0:T(8,128)} %get-tuple-element.17.wy_ref, f32[3,16,1024]{2,1,0:T(8,128)} %get-tuple-element.18.fx_ref, ...), custom_call_target="tpu_custom_call" | custom-call | flops 3623878656 | bytes 4718592 | tf_op jit(solution)/shard_map/spread/pallas_call | solution.py:457
  44.2 0.0 copy-done.2
  44.2 0.0 collective-permute-done.1.x1_ref
  44.2 0.0 copy-start.3
  44.2 0.0 collective-permute-done.2.y0_ref
  44.3 0.0 copy-start.6
  44.3 0.0 collective-permute-done.3.y1_ref
  44.3 0.0 copy-start.7
  44.3 0.0 collective-permute-done.5.right_ref
  44.3 0.0 copy-start.4
  44.3 0.7 %collective-permute-done.4.left_ref = f32[8,24,128]{2,1,0:T(8,128)S(1)} collective-permute-done((f32[8,24,128]{2,1,0:T(8,128)}, f32[8,24,128]{2,1,0:T(8,128)S(1)}, u32[]{:S(2)}, u32[]{:S(2)}) %collective-permute-start.4) | collective-permute-done | bytes 98336 | tf_op jit(solution)/shard_map/ppermute | solution.py:413
  45.0 0.0 copy-start.5
  45.0 0.0 all-to-all-done.1.given_ref
  45.0 0.0 copy-start
  45.0 0.0 copy-done.3
  45.0 0.0 copy-done.6
  45.0 0.0 copy-done.7
  45.0 0.0 copy-done.4
  45.1 0.6 %copy-done.5 = f32[8,24,128]{2,1,0:T(8,128)} copy-done((f32[8,24,128]{2,1,0:T(8,128)}, f32[8,24,128]{2,1,0:T(8,128)S(1)}, u32[]{:S(2)}) %copy-start.5) | copy-done | bytes 98328
  45.7 0.1 copy-done
  45.7 5.7 %finish.1 = (f32[3,12,64,256]{3,2,1,0:T(8,128)}, f32[3,512]{1,0:T(4,128)}) custom-call(f32[3,12,64,256]{3,2,1,0:T(8,128)} %spread.1.rhs_hbm, f32[3,64,256]{2,1,0:T(8,128)} %copy-done.2, f32[3,64,256]{2,1,0:T(8,128)} %copy-done.3, f32[3,12,256]{2,1,0:T(8,128)} %copy-done.6, f32[3,12,256]{2,1,0:T(8,128)} %copy-done.7, f32[8,24,128]{2,1,0:T(8,128)} %copy-done.5, ...), custom_call_target="tpu_custom_call" | custom-call | tf_op jit(solution)/shard_map/finish/pallas_call | solution.py:472
Async XLA Ops:
  3.3 34.2 %collective-permute-start = (f32[3,64,256]{2,1,0:T(8,128)}, f32[3,64,256]{2,1,0:T(8,128)S(1)}, u32[]{:S(2)}, u32[]{:S(2)}) collective-permute-start(f32[3,64,256]{2,1,0:T(8,128)} %get-tuple-element.20), channel_id=1, source_target_pairs={{0,4},{4,8},{8,12},{12,16},{16,20},{20,24},{24,28},{28,0},{1,5},{5... | collective-permute-start | bytes 589832 | tf_op jit(solution)/shard_map/ppermute | solution.py:411
  6.3 12.1 %all-to-all-start = ((f32[8,24,128]{2,1,0:T(8,128)}), f32[8,24,128]{2,1,0:T(8,128)S(1)}, u32[]{:S(2)}, u32[]{:S(2)}) async-start(f32[8,24,128]{2,1,0:T(8,128)} %get-tuple-element.14), calls=%async_computation | async-start | bytes 196608 | tf_op jit(solution)/shard_map/all_to_all | solution.py:401
  11.2 33.0 %collective-permute-start.1 = (f32[3,64,256]{2,1,0:T(8,128)}, f32[3,64,256]{2,1,0:T(8,128)S(1)}, u32[]{:S(2)}, u32[]{:S(2)}) collective-permute-start(f32[3,64,256]{2,1,0:T(8,128)} %get-tuple-element.21), channel_id=1, source_target_pairs={{4,0},{8,4},{12,8},{16,12},{20,16},{24,20},{28,24},{0,28},{5,1},{9... | collective-permute-start | bytes 589832 | tf_op jit(solution)/shard_map/ppermute | solution.py:412
  18.4 0.6 %copy-start.1 = (f32[8,24,128]{2,1,0:T(8,128)}, f32[8,24,128]{2,1,0:T(8,128)S(1)}, u32[]{:S(2)}) copy-start(f32[8,24,128]{2,1,0:T(8,128)S(1)} %all-to-all-done.arrived_ref) | copy-start | bytes 294916
  27.7 17.3 %all-to-all-start.1 = ((f32[8,3,1024]{2,1,0:T(4,128)}), f32[8,3,1024]{2,1,0:T(4,128)S(1)}, u32[]{:S(2)}, u32[]{:S(2)}) async-start(f32[8,3,1024]{2,1,0:T(4,128)} %get-tuple-element.24), calls=%async_computation.1 | async-start | bytes 262144 | tf_op jit(solution)/shard_map/all_to_all | solution.py:450
  31.1 13.2 %collective-permute-start.2 = (f32[3,12,256]{2,1,0:T(8,128)}, f32[3,12,256]{2,1,0:T(8,128)S(1)}, u32[]{:S(2)}, u32[]{:S(2)}) collective-permute-start(f32[3,12,256]{2,1,0:T(8,128)} %get-tuple-element.22), channel_id=1, source_target_pairs={{0,1},{1,2},{2,3},{3,0},{4,5},{5,6},{6,7},{7,4},{8,9},{9,10},{10,1... | collective-permute-start | bytes 110600 | tf_op jit(solution)/shard_map/ppermute | solution.py:448
  31.1 13.1 %collective-permute-start.3 = (f32[3,12,256]{2,1,0:T(8,128)}, f32[3,12,256]{2,1,0:T(8,128)S(1)}, u32[]{:S(2)}, u32[]{:S(2)}) collective-permute-start(f32[3,12,256]{2,1,0:T(8,128)} %get-tuple-element.23), channel_id=1, source_target_pairs={{1,0},{2,1},{3,2},{0,3},{5,4},{6,5},{7,6},{4,7},{9,8},{10,9},{11,1... | collective-permute-start | bytes 110600 | tf_op jit(solution)/shard_map/ppermute | solution.py:449
  32.9 11.4 %collective-permute-start.5 = (f32[8,24,128]{2,1,0:T(8,128)}, f32[8,24,128]{2,1,0:T(8,128)S(1)}, u32[]{:S(2)}, u32[]{:S(2)}) collective-permute-start(f32[8,24,128]{2,1,0:T(8,128)} %copy-done.1), channel_id=1, source_target_pairs={{4,0},{8,4},{12,8},{16,12},{20,16},{24,20},{28,24},{0,28},{5,1},{9... | collective-permute-start | bytes 294920 | tf_op jit(solution)/shard_map/ppermute | solution.py:414
  37.5 6.7 %copy-start.2 = (f32[3,64,256]{2,1,0:T(8,128)}, f32[3,64,256]{2,1,0:T(8,128)S(1)}, u32[]{:S(2)}) copy-start(f32[3,64,256]{2,1,0:T(8,128)S(1)} %collective-permute-done.x0_ref) | copy-start | bytes 589828
  37.5 7.5 %collective-permute-start.4 = (f32[8,24,128]{2,1,0:T(8,128)}, f32[8,24,128]{2,1,0:T(8,128)S(1)}, u32[]{:S(2)}, u32[]{:S(2)}) collective-permute-start(f32[8,24,128]{2,1,0:T(8,128)} %copy-done.1), channel_id=1, source_target_pairs={{0,4},{4,8},{8,12},{12,16},{16,20},{20,24},{24,28},{28,0},{1,5},{5... | collective-permute-start | bytes 294920 | tf_op jit(solution)/shard_map/ppermute | solution.py:413
  44.2 0.8 %copy-start.3 = (f32[3,64,256]{2,1,0:T(8,128)}, f32[3,64,256]{2,1,0:T(8,128)S(1)}, u32[]{:S(2)}) copy-start(f32[3,64,256]{2,1,0:T(8,128)S(1)} %collective-permute-done.1.x1_ref) | copy-start | bytes 589828
  44.3 0.8 %copy-start.6 = (f32[3,12,256]{2,1,0:T(8,128)}, f32[3,12,256]{2,1,0:T(8,128)S(1)}, u32[]{:S(2)}) copy-start(f32[3,12,256]{2,1,0:T(8,128)S(1)} %collective-permute-done.2.y0_ref) | copy-start | bytes 110596
  44.3 0.8 %copy-start.7 = (f32[3,12,256]{2,1,0:T(8,128)}, f32[3,12,256]{2,1,0:T(8,128)S(1)}, u32[]{:S(2)}) copy-start(f32[3,12,256]{2,1,0:T(8,128)S(1)} %collective-permute-done.3.y1_ref) | copy-start | bytes 110596
  44.3 0.7 %copy-start.4 = (f32[8,24,128]{2,1,0:T(8,128)}, f32[8,24,128]{2,1,0:T(8,128)S(1)}, u32[]{:S(2)}) copy-start(f32[8,24,128]{2,1,0:T(8,128)S(1)} %collective-permute-done.5.right_ref) | copy-start | bytes 294916
  45.0 0.7 %copy-start.5 = (f32[8,24,128]{2,1,0:T(8,128)}, f32[8,24,128]{2,1,0:T(8,128)S(1)}, u32[]{:S(2)}) copy-start(f32[8,24,128]{2,1,0:T(8,128)S(1)} %collective-permute-done.4.left_ref) | copy-start | bytes 294916
  45.0 0.7 %copy-start = (f32[8,3,1024]{2,1,0:T(4,128)}, f32[8,3,1024]{2,1,0:T(4,128)S(1)}, u32[]{:S(2)}) copy-start(f32[8,3,1024]{2,1,0:T(4,128)S(1)} %all-to-all-done.1.given_ref) | copy-start | bytes 294916
